TPU v7x, 32 devices: a whole 2x2x4 slice. The times are simulated.
32 devices in a mesh: lat: 16 (over z, x, core), freq: 2 (over y).
Axes of the slice: x: 2, y: 2, z: 4, core: 2. Of those that a mesh axis runs over, the one named last changes fastest.
Arguments:
- wavefield: float32 [4, 2, 8, 32768], P(None, 'freq', None, 'lat'), may hold values from -6 to 6
- propagator_table: bfloat16 [2, 4, 2112, 128], P('freq'), may hold values from -0.125 to 0.125
- table_index: int32 [3, 256], P(None, 'lat'), may hold values from 0 to 3
- slowness: float32 [3, 32768], P(None, 'lat'), may hold values from -1 to 1
- frequency_scale: float32 [2], P('freq'), may hold values from 1 to 8
Outputs:
- image: float32 [3, 8, 32768], P(None, 'freq', 'lat')
All inputs are finite; a program needn't handle non-finite values.
Results may differ from a plain program's by a relative error of at most 0.024.
Values may be sent and summed in bfloat16 or wider, within the bound.
No kernel may reach another device: no remote copies, remote signals or barrier semaphores. Data moves between devices by JAX's collectives and lax.ppermute only.
A program may use at most 64 MiB of HBM per device.

v0:
```python
import math

import jax
import jax.numpy as jnp
from jax import lax
from jax.sharding import PartitionSpec as P

WINDOW = 128
COEFS = 64
REACH = 16
MARGIN = 64
STEPS = 3


def extended_2(cells, sides, width):
    for axis, dim in sides:
        count = lax.axis_size(axis)
        ends = count - 1
        head = lax.slice_in_dim(cells, 0, width, axis=dim)
        tail = lax.slice_in_dim(cells, cells.shape[dim] - width, cells.shape[dim], axis=dim)
        cells = jnp.concatenate(
            [
                lax.ppermute(tail, axis, [(i, (i + 1) % count) for i in range(ends)]),
                cells,
                lax.ppermute(head, axis, [((i + 1) % count, i) for i in range(ends)]),
            ],
            axis=dim,
        )
    return cells


def shifted(array, axis, by):
    size = lax.axis_size(axis)
    pairs = [(i, i + by) for i in range(size) if 0 <= i + by < size]
    return lax.ppermute(array, axis, pairs)


def basis_table():
    points = jnp.arange(2 * WINDOW, dtype=jnp.float32)[:, None]
    orders = jnp.arange(COEFS, dtype=jnp.float32)[None, :]
    bell_taper = jnp.sin(math.pi * (points + 0.5) / (2 * WINDOW))
    cosine = jnp.cos(math.pi * (orders + 0.5) * (points - MARGIN + 0.5) / WINDOW)
    return (bell_taper * math.sqrt(2.0 / WINDOW) * cosine).astype(jnp.bfloat16)


def on_device(wavefield, propagator_table, table_index, slowness, frequency_scale):
    basis = basis_table()
    freq_dev = wavefield.shape[1]
    sources = wavefield.shape[2]
    points = wavefield.shape[3]
    windows = points // WINDOW
    hops = -(-REACH // windows)
    band = 2 * REACH + 1
    tables = propagator_table.shape[1]
    all_tables = jnp.moveaxis(propagator_table, 1, 2).reshape(
        freq_dev, band * COEFS, tables * 2 * COEFS
    )
    table_ids = jnp.arange(tables, dtype=jnp.int32)
    field = wavefield
    partials = []
    for step in range(STEPS):
        samples = field.astype(jnp.bfloat16)
        padded = extended_2(samples, (("lat", 3),), MARGIN)
        blocks = padded.reshape(4, freq_dev, sources, windows + 1, WINDOW)
        coefs = jnp.einsum(
            "afsbl,lk->fbask",
            blocks[:, :, :, :windows],
            basis[:WINDOW],
            preferred_element_type=jnp.float32,
        )
        coefs = coefs + jnp.einsum(
            "afsbl,lk->fbask",
            blocks[:, :, :, 1:],
            basis[WINDOW:],
            preferred_element_type=jnp.float32,
        )
        coefs = coefs.reshape(freq_dev, windows, 4 * sources, COEFS).astype(jnp.bfloat16)
        offsets = list(range(-hops, 0)) + list(range(1, hops + 1))
        nearby = {distance: shifted(coefs, "lat", distance) for distance in offsets}
        left_pieces = nearby[1]
        right_pieces = nearby[-1]
        extended = jnp.concatenate([left_pieces, coefs, right_pieces], axis=1)
        unfolded = jnp.stack(
            [extended[:, offset : offset + windows] for offset in range(band)], axis=3
        )
        unfolded = unfolded.reshape(freq_dev, windows, 4 * sources, band * COEFS)
        every_table = jnp.einsum(
            "fwrk,fkc->fwrc", unfolded, all_tables, preferred_element_type=jnp.float32
        )
        every_table = every_table.reshape(freq_dev, windows, 4 * sources, tables, 2 * COEFS)
        selector = (table_index[step][:, None] == table_ids[None, :]).astype(jnp.float32)
        products = jnp.sum(every_table * selector[None, :, None, :, None], axis=3)
        products = products.reshape(freq_dev, windows, 4, sources, 2 * COEFS)
        real_part = products[..., :COEFS]
        imag_part = products[..., COEFS:]
        propagated = jnp.stack(
            [
                real_part[:, :, 0] - imag_part[:, :, 1],
                real_part[:, :, 1] + imag_part[:, :, 0],
                real_part[:, :, 2] + imag_part[:, :, 3],
                real_part[:, :, 3] - imag_part[:, :, 2],
            ],
            axis=2,
        )
        propagated = propagated.astype(jnp.bfloat16)
        segments = jnp.einsum(
            "fwask,tk->afswt", propagated, basis, preferred_element_type=jnp.float32
        )
        zero_block = jnp.zeros((4, freq_dev, sources, 1, WINDOW), jnp.float32)
        summed = jnp.concatenate([segments[..., :WINDOW], zero_block], 3) + jnp.concatenate(
            [zero_block, segments[..., WINDOW:]], 3
        )
        flat = summed.reshape(4, freq_dev, sources, (windows + 1) * WINDOW)
        tails = jnp.concatenate([flat[..., :MARGIN], flat[..., -MARGIN:]], axis=3)
        rims = extended_2(tails, (("lat", 3),), MARGIN)
        back = flat[..., MARGIN : MARGIN + points]
        back = back.at[..., :MARGIN].add(rims[..., :MARGIN])
        back = back.at[..., points - MARGIN :].add(rims[..., 3 * MARGIN :])
        phase = frequency_scale[:, None, None] * slowness[step][None, None, :]
        cosines = jnp.cos(phase)
        sines = jnp.sin(phase)
        field = jnp.stack(
            [
                back[0] * cosines - back[1] * sines,
                back[0] * sines + back[1] * cosines,
                back[2] * cosines + back[3] * sines,
                back[3] * cosines - back[2] * sines,
            ]
        )
        partial_image = jnp.sum(field[0] * field[2] + field[1] * field[3], axis=0)
        partials.append(partial_image)
    return lax.psum_scatter(
        jnp.stack(partials).astype(jnp.bfloat16), "freq", scatter_dimension=1, tiled=True
    ).astype(jnp.float32)


def solution(mesh):
    placed = (
        P(None, "freq", None, "lat"),
        P("freq", None, None, None),
        P(None, "lat"),
        P(None, "lat"),
        P("freq"),
    )
    return jax.shard_map(
        on_device, mesh=mesh, in_specs=placed, out_specs=P(None, "freq", "lat"), check_vma=False
    )
```

profile of v0, /device:TPU:10, one launch (start us, length us, event | category | flops | bytes accessed | tf_op | source)
XLA Modules:
  0.0 178.0 jit_solution(5613676368379103097)
XLA Ops:
  9.7 2.4 %collective-permute-start = (bf16[4,1,8,64]{3,2,0,1:T(8,128)(2,1)S(1)}, bf16[4,1,8,64]{3,2,0,1:T(8,128)(2,1)S(1)}, u32[]{:S(2)}, u32[]{:S(2)}) collective-permute-start(bf16[4,1,8,64]{3,2,0,1:T(8,128)(2,1)S(1)} %get-tuple-element.126), channel_id=1, source_target_pairs={{0,2},{2,4},{4,6},{6,8},{8,10},{10,12},{12,14},{14,16},{16,18},{18... | collective-permute-start | bytes 12296 | tf_op jit(solution)/shard_map/ppermute | solution.py:23
  15.2 2.5 %collective-permute-start.2 = (bf16[1,16,32,64]{3,2,1,0:T(8,128)(2,1)S(1)}, bf16[1,16,32,64]{3,2,1,0:T(8,128)(2,1)S(1)}, u32[]{:S(2)}, u32[]{:S(2)}) collective-permute-start(bf16[1,16,32,64]{3,2,1,0:T(8,128)(2,1)S(1)} %copy.185), channel_id=1, source_target_pairs={{0,2},{2,4},{4,6},{6,8},{8,10},{10,12},{12,14},{14,16},{16,18},{18... | collective-permute-start | bytes 196616 | tf_op jit(solution)/shard_map/ppermute | solution.py:35
  18.5 3.1 %collective-permute-start.3 = (bf16[1,16,32,64]{3,2,1,0:T(8,128)(2,1)S(1)}, bf16[1,16,32,64]{3,2,1,0:T(8,128)(2,1)S(1)}, u32[]{:S(2)}, u32[]{:S(2)}) collective-permute-start(bf16[1,16,32,64]{3,2,1,0:T(8,128)(2,1)S(1)} %copy.185), channel_id=1, source_target_pairs={{2,0},{4,2},{6,4},{8,6},{10,8},{12,10},{14,12},{16,14},{18,16},{20... | collective-permute-start | bytes 196616 | tf_op jit(solution)/shard_map/ppermute | solution.py:35
  22.1 1.9 %collective-permute-done.3 = bf16[1,16,32,64]{3,2,1,0:T(8,128)(2,1)S(1)} collective-permute-done((bf16[1,16,32,64]{3,2,1,0:T(8,128)(2,1)S(1)}, bf16[1,16,32,64]{3,2,1,0:T(8,128)(2,1)S(1)}, u32[]{:S(2)}, u32[]{:S(2)}) %collective-permute-start.3) | collective-permute-done | bytes 65568 | tf_op jit(solution)/shard_map/ppermute | solution.py:35
  24.5 5.3 %copy.190 = bf16[1,16,32,33,64]{4,3,2,1,0:T(8,128)(2,1)} copy(bf16[1,16,32,33,64]{4,2,1,3,0:T(8,128)(2,1)S(1)} %constant_dynamic-update-slice_fusion.4) | data formatting | bytes 4325376 | tf_op jit(solution)/shard_map/stack | solution.py:83
  29.8 7.4 %reshape.2081 = bf16[16,32,2112,1]{2,1,0,3:T(8,128)(2,1)} reshape(bf16[1,16,32,33,64]{4,3,2,1,0:T(8,128)(2,1)} %copy.190) | data formatting | bytes 4325376 | tf_op jit(solution)/shard_map/reshape.209
  37.2 3.0 %fusion.34 = f32[16,32,128]{2,1,0:T(8,128)S(1)} fusion(bf16[1,4,2112,128]{3,2,1,0:T(8,128)(2,1)S(1)} %copy-done, bf16[16,32,2112,1]{2,1,0,3:T(8,128)(2,1)} %reshape.2081, f32[16,4]{1,0:T(8,128)S(1)} %get-tuple-element.138), kind=kOutput, calls=%fused_computation.14 | convolution fusion | flops 1107755008 | bytes 4587776 | tf_op jit(solution)/shard_map/fwrk,fkc->fwrc/dot_general | solution.py:87
  41.3 6.3 %collective-permute-start.4 = (f32[4,1,8,64]{3,2,0,1:T(8,128)S(1)}, f32[4,1,8,64]{3,2,0,1:T(8,128)S(1)}, u32[]{:S(2)}, u32[]{:S(2)}) collective-permute-start(f32[4,1,8,64]{3,2,0,1:T(8,128)S(1)} %get-tuple-element.96), channel_id=1, source_target_pairs={{0,2},{2,4},{4,6},{6,8},{8,10},{10,12},{12,14},{14,16},{16,18},{18... | collective-permute-start | bytes 24584 | tf_op jit(solution)/shard_map/ppermute | solution.py:23
  48.5 1.9 %collective-permute-start.5 = (f32[4,1,8,64]{3,2,0,1:T(8,128)S(1)}, f32[4,1,8,64]{3,2,0,1:T(8,128)S(1)}, u32[]{:S(2)}, u32[]{:S(2)}) collective-permute-start(f32[4,1,8,64]{3,2,0,1:T(8,128)S(1)} %get-tuple-element.95), channel_id=1, source_target_pairs={{2,0},{4,2},{6,4},{8,6},{10,8},{12,10},{14,12},{16,14},{18,16},{20... | collective-permute-start | bytes 24584 | tf_op jit(solution)/shard_map/ppermute | solution.py:25
  52.7 3.6 %collective-permute-start.7 = (bf16[4,1,8,64]{3,2,0,1:T(8,128)(2,1)S(1)}, bf16[4,1,8,64]{3,2,0,1:T(8,128)(2,1)S(1)}, u32[]{:S(2)}, u32[]{:S(2)}) collective-permute-start(bf16[4,1,8,64]{3,2,0,1:T(8,128)(2,1)S(1)} %get-tuple-element.121), channel_id=1, source_target_pairs={{2,0},{4,2},{6,4},{8,6},{10,8},{12,10},{14,12},{16,14},{18,16},{20... | collective-permute-start | bytes 12296 | tf_op jit(solution)/shard_map/ppermute | solution.py:25
  56.3 2.8 %collective-permute-start.6 = (bf16[4,1,8,64]{3,2,0,1:T(8,128)(2,1)S(1)}, bf16[4,1,8,64]{3,2,0,1:T(8,128)(2,1)S(1)}, u32[]{:S(2)}, u32[]{:S(2)}) collective-permute-start(bf16[4,1,8,64]{3,2,0,1:T(8,128)(2,1)S(1)} %get-tuple-element.122), channel_id=1, source_target_pairs={{0,2},{2,4},{4,6},{6,8},{8,10},{10,12},{12,14},{14,16},{16,18},{18... | collective-permute-start | bytes 12296 | tf_op jit(solution)/shard_map/ppermute | solution.py:23
  59.1 2.1 %collective-permute-done.6 = bf16[4,1,8,64]{3,2,0,1:T(8,128)(2,1)S(1)} collective-permute-done((bf16[4,1,8,64]{3,2,0,1:T(8,128)(2,1)S(1)}, bf16[4,1,8,64]{3,2,0,1:T(8,128)(2,1)S(1)}, u32[]{:S(2)}, u32[]{:S(2)}) %collective-permute-start.6) | collective-permute-done | bytes 4128 | tf_op jit(solution)/shard_map/ppermute | solution.py:23
  61.9 3.2 %collective-permute-start.8 = (bf16[1,16,32,64]{3,2,1,0:T(8,128)(2,1)S(1)}, bf16[1,16,32,64]{3,2,1,0:T(8,128)(2,1)S(1)}, u32[]{:S(2)}, u32[]{:S(2)}) collective-permute-start(bf16[1,16,32,64]{3,2,1,0:T(8,128)(2,1)S(1)} %copy.196), channel_id=1, source_target_pairs={{0,2},{2,4},{4,6},{6,8},{8,10},{10,12},{12,14},{14,16},{16,18},{18... | collective-permute-start | bytes 196616 | tf_op jit(solution)/shard_map/ppermute | solution.py:35
  65.1 2.6 %collective-permute-start.9 = (bf16[1,16,32,64]{3,2,1,0:T(8,128)(2,1)S(1)}, bf16[1,16,32,64]{3,2,1,0:T(8,128)(2,1)S(1)}, u32[]{:S(2)}, u32[]{:S(2)}) collective-permute-start(bf16[1,16,32,64]{3,2,1,0:T(8,128)(2,1)S(1)} %copy.196), channel_id=1, source_target_pairs={{2,0},{4,2},{6,4},{8,6},{10,8},{12,10},{14,12},{16,14},{18,16},{20... | collective-permute-start | bytes 196616 | tf_op jit(solution)/shard_map/ppermute | solution.py:35
  68.7 2.6 %collective-permute-done.9 = bf16[1,16,32,64]{3,2,1,0:T(8,128)(2,1)S(1)} collective-permute-done((bf16[1,16,32,64]{3,2,1,0:T(8,128)(2,1)S(1)}, bf16[1,16,32,64]{3,2,1,0:T(8,128)(2,1)S(1)}, u32[]{:S(2)}, u32[]{:S(2)}) %collective-permute-start.9) | collective-permute-done | bytes 65568 | tf_op jit(solution)/shard_map/ppermute | solution.py:35
  71.8 5.3 %copy.201 = bf16[1,16,32,33,64]{4,3,2,1,0:T(8,128)(2,1)} copy(bf16[1,16,32,33,64]{4,2,1,3,0:T(8,128)(2,1)S(1)} %constant_dynamic-update-slice_fusion.41) | data formatting | bytes 4325376 | tf_op jit(solution)/shard_map/stack | solution.py:83
  77.1 7.4 %reshape.2084 = bf16[16,32,2112,1]{2,1,0,3:T(8,128)(2,1)} reshape(bf16[1,16,32,33,64]{4,3,2,1,0:T(8,128)(2,1)} %copy.201) | data formatting | bytes 4325376 | tf_op jit(solution)/shard_map/reshape.235
  84.5 3.0 %fusion.29 = f32[16,32,128]{2,1,0:T(8,128)S(1)} fusion(bf16[1,4,2112,128]{3,2,1,0:T(8,128)(2,1)S(1)} %copy-done, bf16[16,32,2112,1]{2,1,0,3:T(8,128)(2,1)} %reshape.2084, f32[16,4]{1,0:T(8,128)S(1)} %get-tuple-element.139), kind=kOutput, calls=%fused_computation.13 | convolution fusion | flops 1107755008 | bytes 4587776 | tf_op jit(solution)/shard_map/fwrk,fkc->fwrc/dot_general | solution.py:87
  88.6 6.0 %collective-permute-start.10 = (f32[4,1,8,64]{3,2,1,0:T(8,128)S(1)}, f32[4,1,8,64]{3,2,1,0:T(8,128)S(1)}, u32[]{:S(2)}, u32[]{:S(2)}) collective-permute-start(f32[4,1,8,64]{3,2,1,0:T(8,128)S(1)} %get-tuple-element.90), channel_id=1, source_target_pairs={{0,2},{2,4},{4,6},{6,8},{8,10},{10,12},{12,14},{14,16},{16,18},{18... | collective-permute-start | bytes 24584 | tf_op jit(solution)/shard_map/ppermute | solution.py:23
  94.7 1.9 %collective-permute-start.11 = (f32[4,1,8,64]{3,2,1,0:T(8,128)S(1)}, f32[4,1,8,64]{3,2,1,0:T(8,128)S(1)}, u32[]{:S(2)}, u32[]{:S(2)}) collective-permute-start(f32[4,1,8,64]{3,2,1,0:T(8,128)S(1)} %get-tuple-element.89), channel_id=1, source_target_pairs={{2,0},{4,2},{6,4},{8,6},{10,8},{12,10},{14,12},{16,14},{18,16},{20... | collective-permute-start | bytes 24584 | tf_op jit(solution)/shard_map/ppermute | solution.py:25
  98.9 3.6 %collective-permute-start.13 = (bf16[4,1,8,64]{3,2,1,0:T(8,128)(2,1)S(1)}, bf16[4,1,8,64]{3,2,1,0:T(8,128)(2,1)S(1)}, u32[]{:S(2)}, u32[]{:S(2)}) collective-permute-start(bf16[4,1,8,64]{3,2,1,0:T(8,128)(2,1)S(1)} %get-tuple-element.117), channel_id=1, source_target_pairs={{2,0},{4,2},{6,4},{8,6},{10,8},{12,10},{14,12},{16,14},{18,16},{20... | collective-permute-start | bytes 12296 | tf_op jit(solution)/shard_map/ppermute | solution.py:25
  102.6 2.8 %collective-permute-start.12 = (bf16[4,1,8,64]{3,2,1,0:T(8,128)(2,1)S(1)}, bf16[4,1,8,64]{3,2,1,0:T(8,128)(2,1)S(1)}, u32[]{:S(2)}, u32[]{:S(2)}) collective-permute-start(bf16[4,1,8,64]{3,2,1,0:T(8,128)(2,1)S(1)} %get-tuple-element.118), channel_id=1, source_target_pairs={{0,2},{2,4},{4,6},{6,8},{8,10},{10,12},{12,14},{14,16},{16,18},{18... | collective-permute-start | bytes 12296 | tf_op jit(solution)/shard_map/ppermute | solution.py:23
  105.5 2.1 %collective-permute-done.12 = bf16[4,1,8,64]{3,2,1,0:T(8,128)(2,1)S(1)} collective-permute-done((bf16[4,1,8,64]{3,2,1,0:T(8,128)(2,1)S(1)}, bf16[4,1,8,64]{3,2,1,0:T(8,128)(2,1)S(1)}, u32[]{:S(2)}, u32[]{:S(2)}) %collective-permute-start.12) | collective-permute-done | bytes 4128 | tf_op jit(solution)/shard_map/ppermute | solution.py:23
  108.2 3.2 %collective-permute-start.14 = (bf16[1,16,32,64]{3,2,1,0:T(8,128)(2,1)S(1)}, bf16[1,16,32,64]{3,2,1,0:T(8,128)(2,1)S(1)}, u32[]{:S(2)}, u32[]{:S(2)}) collective-permute-start(bf16[1,16,32,64]{3,2,1,0:T(8,128)(2,1)S(1)} %copy.210), channel_id=1, source_target_pairs={{0,2},{2,4},{4,6},{6,8},{8,10},{10,12},{12,14},{14,16},{16,18},{18... | collective-permute-start | bytes 196616 | tf_op jit(solution)/shard_map/ppermute | solution.py:35
  111.4 2.6 %collective-permute-start.15 = (bf16[1,16,32,64]{3,2,1,0:T(8,128)(2,1)S(1)}, bf16[1,16,32,64]{3,2,1,0:T(8,128)(2,1)S(1)}, u32[]{:S(2)}, u32[]{:S(2)}) collective-permute-start(bf16[1,16,32,64]{3,2,1,0:T(8,128)(2,1)S(1)} %copy.210), channel_id=1, source_target_pairs={{2,0},{4,2},{6,4},{8,6},{10,8},{12,10},{14,12},{16,14},{18,16},{20... | collective-permute-start | bytes 196616 | tf_op jit(solution)/shard_map/ppermute | solution.py:35
  115.0 2.6 %collective-permute-done.15 = bf16[1,16,32,64]{3,2,1,0:T(8,128)(2,1)S(1)} collective-permute-done((bf16[1,16,32,64]{3,2,1,0:T(8,128)(2,1)S(1)}, bf16[1,16,32,64]{3,2,1,0:T(8,128)(2,1)S(1)}, u32[]{:S(2)}, u32[]{:S(2)}) %collective-permute-start.15) | collective-permute-done | bytes 65568 | tf_op jit(solution)/shard_map/ppermute | solution.py:35
  118.0 5.3 %copy.215 = bf16[1,16,32,33,64]{4,3,2,1,0:T(8,128)(2,1)} copy(bf16[1,16,32,33,64]{4,2,1,3,0:T(8,128)(2,1)S(1)} %constant_dynamic-update-slice_fusion.78) | data formatting | bytes 4325376 | tf_op jit(solution)/shard_map/stack | solution.py:83
  123.3 7.4 %reshape.2086 = bf16[16,32,2112,1]{2,1,0,3:T(8,128)(2,1)} reshape(bf16[1,16,32,33,64]{4,3,2,1,0:T(8,128)(2,1)} %copy.215) | data formatting | bytes 4325376 | tf_op jit(solution)/shard_map/reshape.257
  130.8 3.0 %fusion.24 = f32[16,32,128]{2,1,0:T(8,128)S(1)} fusion(bf16[1,4,2112,128]{3,2,1,0:T(8,128)(2,1)S(1)} %copy-done, bf16[16,32,2112,1]{2,1,0,3:T(8,128)(2,1)} %reshape.2086, f32[16,4]{1,0:T(8,128)S(1)} %fusion.111), kind=kOutput, calls=%fused_computation.12 | convolution fusion | flops 1107755008 | bytes 4587776 | tf_op jit(solution)/shard_map/fwrk,fkc->fwrc/dot_general | solution.py:87
  134.8 6.1 %collective-permute-start.16 = (f32[4,1,8,64]{3,2,1,0:T(8,128)S(1)}, f32[4,1,8,64]{3,2,1,0:T(8,128)S(1)}, u32[]{:S(2)}, u32[]{:S(2)}) collective-permute-start(f32[4,1,8,64]{3,2,1,0:T(8,128)S(1)} %get-tuple-element.84), channel_id=1, source_target_pairs={{0,2},{2,4},{4,6},{6,8},{8,10},{10,12},{12,14},{14,16},{16,18},{18... | collective-permute-start | bytes 24584 | tf_op jit(solution)/shard_map/ppermute | solution.py:23
  141.1 1.9 %collective-permute-start.17 = (f32[4,1,8,64]{3,2,1,0:T(8,128)S(1)}, f32[4,1,8,64]{3,2,1,0:T(8,128)S(1)}, u32[]{:S(2)}, u32[]{:S(2)}) collective-permute-start(f32[4,1,8,64]{3,2,1,0:T(8,128)S(1)} %get-tuple-element.83), channel_id=1, source_target_pairs={{2,0},{4,2},{6,4},{8,6},{10,8},{12,10},{14,12},{16,14},{18,16},{20... | collective-permute-start | bytes 24584 | tf_op jit(solution)/shard_map/ppermute | solution.py:25
  147.1 22.5 %all-reduce.9.cloned.1.call-done = bf16[3,8,2048]{2,1,0:T(8,128)(2,1)} async-done(((bf16[3,8,2048]{2,1,0:T(8,128)(2,1)}), bf16[3,8,2048]{2,1,0:T(8,128)(2,1)}) %all-reduce.9.cloned.1.call-update) | async-done | bytes 98320
  (202 shorter events, 24.4 us)
Async XLA Ops:
  6.5 30.7 %copy-start = (bf16[1,4,2112,128]{3,2,1,0:T(8,128)(2,1)S(1)}, bf16[1,4,2112,128]{3,2,1,0:T(8,128)(2,1)}, u32[]{:S(2)}) copy-start(bf16[1,4,2112,128]{3,2,1,0:T(8,128)(2,1)} %param.18) | copy-start | bytes 6488068
  6.5 163.1 %all-reduce.9.cloned.1.call-start = ((), (), s32[]{:S(2)}) async-start(), calls=%async_computation | async-start | bytes 196608
  7.7 5.5 %collective-permute-start.1 = (bf16[4,1,8,64]{3,2,0,1:T(8,128)(2,1)S(1)}, bf16[4,1,8,64]{3,2,0,1:T(8,128)(2,1)S(1)}, u32[]{:S(2)}, u32[]{:S(2)}) collective-permute-start(bf16[4,1,8,64]{3,2,0,1:T(8,128)(2,1)S(1)} %get-tuple-element.125), channel_id=1, source_target_pairs={{2,0},{4,2},{6,4},{8,6},{10,8},{12,10},{14,12},{16,14},{18,16},{20... | collective-permute-start | bytes 12296 | tf_op jit(solution)/shard_map/ppermute | solution.py:25
  9.7 5.0 %collective-permute-start = (bf16[4,1,8,64]{3,2,0,1:T(8,128)(2,1)S(1)}, bf16[4,1,8,64]{3,2,0,1:T(8,128)(2,1)S(1)}, u32[]{:S(2)}, u32[]{:S(2)}) collective-permute-start(bf16[4,1,8,64]{3,2,0,1:T(8,128)(2,1)S(1)} %get-tuple-element.126), channel_id=1, source_target_pairs={{0,2},{2,4},{4,6},{6,8},{8,10},{10,12},{12,14},{14,16},{16,18},{18... | collective-permute-start | bytes 12296 | tf_op jit(solution)/shard_map/ppermute | solution.py:23
  15.2 6.3 %collective-permute-start.2 = (bf16[1,16,32,64]{3,2,1,0:T(8,128)(2,1)S(1)}, bf16[1,16,32,64]{3,2,1,0:T(8,128)(2,1)S(1)}, u32[]{:S(2)}, u32[]{:S(2)}) collective-permute-start(bf16[1,16,32,64]{3,2,1,0:T(8,128)(2,1)S(1)} %copy.185), channel_id=1, source_target_pairs={{0,2},{2,4},{4,6},{6,8},{8,10},{10,12},{12,14},{14,16},{16,18},{18... | collective-permute-start | bytes 196616 | tf_op jit(solution)/shard_map/ppermute | solution.py:35
  18.5 5.6 %collective-permute-start.3 = (bf16[1,16,32,64]{3,2,1,0:T(8,128)(2,1)S(1)}, bf16[1,16,32,64]{3,2,1,0:T(8,128)(2,1)S(1)}, u32[]{:S(2)}, u32[]{:S(2)}) collective-permute-start(bf16[1,16,32,64]{3,2,1,0:T(8,128)(2,1)S(1)} %copy.185), channel_id=1, source_target_pairs={{2,0},{4,2},{6,4},{8,6},{10,8},{12,10},{14,12},{16,14},{18,16},{20... | collective-permute-start | bytes 196616 | tf_op jit(solution)/shard_map/ppermute | solution.py:35
  40.3 7.3 %copy-start.1 = (f32[3,2048]{1,0:T(4,128)S(1)}, f32[3,2048]{1,0:T(4,128)}, u32[]{:S(2)}) copy-start(f32[3,2048]{1,0:T(4,128)} %param.20) | copy-start | bytes 73732
  41.3 9.1 %collective-permute-start.4 = (f32[4,1,8,64]{3,2,0,1:T(8,128)S(1)}, f32[4,1,8,64]{3,2,0,1:T(8,128)S(1)}, u32[]{:S(2)}, u32[]{:S(2)}) collective-permute-start(f32[4,1,8,64]{3,2,0,1:T(8,128)S(1)} %get-tuple-element.96), channel_id=1, source_target_pairs={{0,2},{2,4},{4,6},{6,8},{8,10},{10,12},{12,14},{14,16},{16,18},{18... | collective-permute-start | bytes 24584 | tf_op jit(solution)/shard_map/ppermute | solution.py:23
  48.5 3.4 %collective-permute-start.5 = (f32[4,1,8,64]{3,2,0,1:T(8,128)S(1)}, f32[4,1,8,64]{3,2,0,1:T(8,128)S(1)}, u32[]{:S(2)}, u32[]{:S(2)}) collective-permute-start(f32[4,1,8,64]{3,2,0,1:T(8,128)S(1)} %get-tuple-element.95), channel_id=1, source_target_pairs={{2,0},{4,2},{6,4},{8,6},{10,8},{12,10},{14,12},{16,14},{18,16},{20... | collective-permute-start | bytes 24584 | tf_op jit(solution)/shard_map/ppermute | solution.py:25
  52.7 6.5 %collective-permute-start.7 = (bf16[4,1,8,64]{3,2,0,1:T(8,128)(2,1)S(1)}, bf16[4,1,8,64]{3,2,0,1:T(8,128)(2,1)S(1)}, u32[]{:S(2)}, u32[]{:S(2)}) collective-permute-start(bf16[4,1,8,64]{3,2,0,1:T(8,128)(2,1)S(1)} %get-tuple-element.121), channel_id=1, source_target_pairs={{2,0},{4,2},{6,4},{8,6},{10,8},{12,10},{14,12},{16,14},{18,16},{20... | collective-permute-start | bytes 12296 | tf_op jit(solution)/shard_map/ppermute | solution.py:25
  56.3 5.0 %collective-permute-start.6 = (bf16[4,1,8,64]{3,2,0,1:T(8,128)(2,1)S(1)}, bf16[4,1,8,64]{3,2,0,1:T(8,128)(2,1)S(1)}, u32[]{:S(2)}, u32[]{:S(2)}) collective-permute-start(bf16[4,1,8,64]{3,2,0,1:T(8,128)(2,1)S(1)} %get-tuple-element.122), channel_id=1, source_target_pairs={{0,2},{2,4},{4,6},{6,8},{8,10},{10,12},{12,14},{14,16},{16,18},{18... | collective-permute-start | bytes 12296 | tf_op jit(solution)/shard_map/ppermute | solution.py:23
  61.9 6.3 %collective-permute-start.8 = (bf16[1,16,32,64]{3,2,1,0:T(8,128)(2,1)S(1)}, bf16[1,16,32,64]{3,2,1,0:T(8,128)(2,1)S(1)}, u32[]{:S(2)}, u32[]{:S(2)}) collective-permute-start(bf16[1,16,32,64]{3,2,1,0:T(8,128)(2,1)S(1)} %copy.196), channel_id=1, source_target_pairs={{0,2},{2,4},{4,6},{6,8},{8,10},{10,12},{12,14},{14,16},{16,18},{18... | collective-permute-start | bytes 196616 | tf_op jit(solution)/shard_map/ppermute | solution.py:35
  65.1 6.2 %collective-permute-start.9 = (bf16[1,16,32,64]{3,2,1,0:T(8,128)(2,1)S(1)}, bf16[1,16,32,64]{3,2,1,0:T(8,128)(2,1)S(1)}, u32[]{:S(2)}, u32[]{:S(2)}) collective-permute-start(bf16[1,16,32,64]{3,2,1,0:T(8,128)(2,1)S(1)} %copy.196), channel_id=1, source_target_pairs={{2,0},{4,2},{6,4},{8,6},{10,8},{12,10},{14,12},{16,14},{18,16},{20... | collective-permute-start | bytes 196616 | tf_op jit(solution)/shard_map/ppermute | solution.py:35
  88.6 8.1 %collective-permute-start.10 = (f32[4,1,8,64]{3,2,1,0:T(8,128)S(1)}, f32[4,1,8,64]{3,2,1,0:T(8,128)S(1)}, u32[]{:S(2)}, u32[]{:S(2)}) collective-permute-start(f32[4,1,8,64]{3,2,1,0:T(8,128)S(1)} %get-tuple-element.90), channel_id=1, source_target_pairs={{0,2},{2,4},{4,6},{6,8},{8,10},{10,12},{12,14},{14,16},{16,18},{18... | collective-permute-start | bytes 24584 | tf_op jit(solution)/shard_map/ppermute | solution.py:23
  94.7 3.4 %collective-permute-start.11 = (f32[4,1,8,64]{3,2,1,0:T(8,128)S(1)}, f32[4,1,8,64]{3,2,1,0:T(8,128)S(1)}, u32[]{:S(2)}, u32[]{:S(2)}) collective-permute-start(f32[4,1,8,64]{3,2,1,0:T(8,128)S(1)} %get-tuple-element.89), channel_id=1, source_target_pairs={{2,0},{4,2},{6,4},{8,6},{10,8},{12,10},{14,12},{16,14},{18,16},{20... | collective-permute-start | bytes 24584 | tf_op jit(solution)/shard_map/ppermute | solution.py:25
  98.9 6.5 %collective-permute-start.13 = (bf16[4,1,8,64]{3,2,1,0:T(8,128)(2,1)S(1)}, bf16[4,1,8,64]{3,2,1,0:T(8,128)(2,1)S(1)}, u32[]{:S(2)}, u32[]{:S(2)}) collective-permute-start(bf16[4,1,8,64]{3,2,1,0:T(8,128)(2,1)S(1)} %get-tuple-element.117), channel_id=1, source_target_pairs={{2,0},{4,2},{6,4},{8,6},{10,8},{12,10},{14,12},{16,14},{18,16},{20... | collective-permute-start | bytes 12296 | tf_op jit(solution)/shard_map/ppermute | solution.py:25
  102.6 5.0 %collective-permute-start.12 = (bf16[4,1,8,64]{3,2,1,0:T(8,128)(2,1)S(1)}, bf16[4,1,8,64]{3,2,1,0:T(8,128)(2,1)S(1)}, u32[]{:S(2)}, u32[]{:S(2)}) collective-permute-start(bf16[4,1,8,64]{3,2,1,0:T(8,128)(2,1)S(1)} %get-tuple-element.118), channel_id=1, source_target_pairs={{0,2},{2,4},{4,6},{6,8},{8,10},{10,12},{12,14},{14,16},{16,18},{18... | collective-permute-start | bytes 12296 | tf_op jit(solution)/shard_map/ppermute | solution.py:23
  108.2 6.3 %collective-permute-start.14 = (bf16[1,16,32,64]{3,2,1,0:T(8,128)(2,1)S(1)}, bf16[1,16,32,64]{3,2,1,0:T(8,128)(2,1)S(1)}, u32[]{:S(2)}, u32[]{:S(2)}) collective-permute-start(bf16[1,16,32,64]{3,2,1,0:T(8,128)(2,1)S(1)} %copy.210), channel_id=1, source_target_pairs={{0,2},{2,4},{4,6},{6,8},{8,10},{10,12},{12,14},{14,16},{16,18},{18... | collective-permute-start | bytes 196616 | tf_op jit(solution)/shard_map/ppermute | solution.py:35
  111.4 6.2 %collective-permute-start.15 = (bf16[1,16,32,64]{3,2,1,0:T(8,128)(2,1)S(1)}, bf16[1,16,32,64]{3,2,1,0:T(8,128)(2,1)S(1)}, u32[]{:S(2)}, u32[]{:S(2)}) collective-permute-start(bf16[1,16,32,64]{3,2,1,0:T(8,128)(2,1)S(1)} %copy.210), channel_id=1, source_target_pairs={{2,0},{4,2},{6,4},{8,6},{10,8},{12,10},{14,12},{16,14},{18,16},{20... | collective-permute-start | bytes 196616 | tf_op jit(solution)/shard_map/ppermute | solution.py:35
  133.8 12.1 %copy-start.2 = (u32[32]{0:T(128)S(1)}, u32[32]{0:T(128)}, u32[]{:S(2)}) copy-start(u32[32]{0:T(128)} %constant.174) | copy-start | bytes 388
  134.8 8.2 %collective-permute-start.16 = (f32[4,1,8,64]{3,2,1,0:T(8,128)S(1)}, f32[4,1,8,64]{3,2,1,0:T(8,128)S(1)}, u32[]{:S(2)}, u32[]{:S(2)}) collective-permute-start(f32[4,1,8,64]{3,2,1,0:T(8,128)S(1)} %get-tuple-element.84), channel_id=1, source_target_pairs={{0,2},{2,4},{4,6},{6,8},{8,10},{10,12},{12,14},{14,16},{16,18},{18... | collective-permute-start | bytes 24584 | tf_op jit(solution)/shard_map/ppermute | solution.py:23
  141.1 3.4 %collective-permute-start.17 = (f32[4,1,8,64]{3,2,1,0:T(8,128)S(1)}, f32[4,1,8,64]{3,2,1,0:T(8,128)S(1)}, u32[]{:S(2)}, u32[]{:S(2)}) collective-permute-start(f32[4,1,8,64]{3,2,1,0:T(8,128)S(1)} %get-tuple-element.83), channel_id=1, source_target_pairs={{2,0},{4,2},{6,4},{8,6},{10,8},{12,10},{14,12},{16,14},{18,16},{20... | collective-permute-start | bytes 24584 | tf_op jit(solution)/shard_map/ppermute | solution.py:25
Sparse Core Ops, SparseCore 0:
  146.0 23.5 all-reduce.8
where the time goes:
time: 181 us; the launch traced here: 178 us
  starting transfers between devices  58.4 us (32%)
  local copies, waits for them, and re-layouts  46.7 us (26%)
  waiting for transfers between devices  39.5 us (22%)
  between operations  16 us (9%)
  matrix products  11.6 us (6%)
  other arithmetic  5.78 us (3%)
    ppermute x6, starting transfers between devices, extended_2(): lax.ppermute(tail, axis, [(i, (i + 1) % count) for i in range(ends)])  26.4 us
    unnamed x2, waiting for transfers between devices  22.5 us
    another operation x3, local copies, waits for them, and re-layouts  22.3 us
    ppermute x6, starting transfers between devices, shifted(): return lax.ppermute(array, axis, pairs)  17.1 us
    another operation x6, local copies, waits for them, and re-layouts, on_device(): jnp.stack([extended[:, offset:offset + windows] for offset in range(band)...  15.9 us
    ppermute x6, starting transfers between devices, extended_2(): lax.ppermute(head, axis, [((i + 1) % count, i) for i in range(ends)])  14.9 us
    dot_general x3, matrix products, on_device(): jnp.einsum('fwrk,fkc->fwrc', unfolded, all_tables, preferred_element_type...  9.09 us
    ppermute x6, waiting for transfers between devices, shifted(): return lax.ppermute(array, axis, pairs)  8.02 us
  transfers between devices with their start and end apart: 19, of which 12 were waited for; matrix products, arithmetic and copies ran while one was open for 3% of the time, Pallas kernels for 0%

commit v1 on v0

v1 whole, which is shorter than its diff:
```python
import math

import jax
import jax.numpy as jnp
import numpy as np
from jax import lax
from jax.experimental import pallas as pl
from jax.experimental.pallas import tpu as pltpu
from jax.sharding import PartitionSpec as P

WINDOW = 128
COEFS = 64
REACH = 16
STEPS = 3
HALF = WINDOW // 2
F32 = jnp.float32
BF16 = jnp.bfloat16
LANES = 2 * COEFS


def basis_table():
    t = np.arange(2 * WINDOW, dtype=np.float32)[:, None]
    k = np.arange(COEFS, dtype=np.float32)[None, :]
    taper = np.sin(np.float32(math.pi) * (t + np.float32(0.5)) / np.float32(2 * WINDOW))
    wave = np.cos(
        np.float32(math.pi)
        * (k + np.float32(0.5))
        * (t - np.float32(HALF) + np.float32(0.5))
        / np.float32(WINDOW)
    )
    return (taper * np.float32(math.sqrt(2.0 / WINDOW)) * wave).astype(np.float32)


def pair_matrices():
    b = basis_table()
    first = np.zeros((4 * WINDOW, LANES), np.float32)
    first[HALF : HALF + 2 * WINDOW, :COEFS] = b
    first[HALF + WINDOW : HALF + 3 * WINDOW, COEFS:] = b
    forward = np.zeros((3 * WINDOW, LANES), np.float32)
    forward[: 2 * WINDOW, :COEFS] = b
    forward[WINDOW:, COEFS:] = b
    inverse = np.zeros((4 * COEFS, 2 * WINDOW), np.float32)
    inverse[COEFS : 2 * COEFS, :WINDOW] = b[WINDOW:].T
    inverse[2 * COEFS : 3 * COEFS, :WINDOW] = b[:WINDOW].T
    inverse[2 * COEFS : 3 * COEFS, WINDOW:] = b[WINDOW:].T
    inverse[3 * COEFS :, WINDOW:] = b[:WINDOW].T
    return first, forward, inverse


def sin_cos(theta):
    turns = jnp.floor(theta * np.float32(2.0 / math.pi) + np.float32(0.5))
    r = theta - turns * np.float32(1.5703125)
    r = r - turns * np.float32(4.837512969970703e-4)
    r = r - turns * np.float32(7.549789948768648e-8)
    r2 = r * r
    s = r + r * r2 * (
        np.float32(-1.6666654611e-1)
        + r2 * (np.float32(8.3321608736e-3) + r2 * np.float32(-1.9515295891e-4))
    )
    c = 1.0 - 0.5 * r2 + r2 * r2 * (
        np.float32(4.166664568298827e-2)
        + r2 * (np.float32(-1.388731625493765e-3) + r2 * np.float32(2.443315711809948e-5))
    )
    quarter = turns - 4.0 * jnp.floor(turns * 0.25)
    odd = (quarter == 1.0) | (quarter == 3.0)
    sin_v = jnp.where(odd, c, s)
    cos_v = jnp.where(odd, s, c)
    sin_v = jnp.where(quarter >= 2.0, -sin_v, sin_v)
    cos_v = jnp.where((quarter == 1.0) | (quarter == 2.0), -cos_v, cos_v)
    return sin_v, cos_v


def lane_swap(v):
    return pltpu.roll(v, LANES // 2, v.ndim - 1)


def low_lanes(shape):
    return lax.broadcasted_iota(jnp.int32, shape, len(shape) - 1) < LANES // 2


def prep_kernel(wave_ref, slow_ref, index_ref, first_ref, keep_ref, send_ref, both_ref, rows_ref):
    core = lax.rem(lax.axis_index("lat"), 2)
    blocks = wave_ref.shape[-1] // WINDOW
    pairs = blocks // 2
    upper = lax.broadcasted_iota(jnp.int32, (8, wave_ref.shape[-1]), 0) < 4
    for side in range(2):
        halves = []
        for low in range(2):
            near, far = wave_ref[low, 0], wave_ref[low + 2, 0]
            if side == 0:
                halves.append(jnp.where(upper, near, pltpu.roll(far, 4, 0)))
            else:
                halves.append(jnp.where(upper, pltpu.roll(near, 4, 0), far))
        samples = jnp.concatenate(halves, axis=0).astype(BF16)
        zero = jnp.zeros((16, WINDOW), BF16)
        padded = [zero] * 3
        padded += [samples[:, WINDOW * g : WINDOW * (g + 1)] for g in range(blocks)]
        padded += [zero] * 3
        parts = [
            jnp.concatenate([padded[2 * i + j] for i in range(pairs + 2)], axis=0)
            for j in range(4)
        ]
        coefs = jnp.dot(
            jnp.concatenate(parts, axis=1), first_ref[...], preferred_element_type=F32
        )
        both_ref[side] = coefs.reshape(pairs + 2, 16, LANES).astype(BF16)
    keep_ref[...] = both_ref[core]
    send_ref[0 : pairs + 2] = both_ref[1 - core]
    slow = slow_ref[...]
    high = slow.astype(BF16).astype(F32)
    rest = slow - high
    lanes = low_lanes((1, LANES))
    rows_ref[...] = jnp.zeros(rows_ref.shape, F32)
    for n in range(STEPS):
        for g in range(blocks):
            cut = slice(WINDOW * g, WINDOW * (g + 1))
            rows_ref[(2 * n) * blocks + g : (2 * n) * blocks + g + 1, :] = high[n : n + 1, cut]
            rows_ref[(2 * n + 1) * blocks + g : (2 * n + 1) * blocks + g + 1, :] = rest[n : n + 1, cut]
        for q in range(pairs):
            at = 2 * STEPS * blocks + n * pairs + q
            rows_ref[at : at + 1, :] = jnp.where(
                lanes,
                jnp.full((1, LANES), index_ref[n, 2 * q], jnp.int32),
                jnp.full((1, LANES), index_ref[n, 2 * q + 1], jnp.int32),
            ).astype(F32)
    send_ref[pairs + 2 :] = rows_ref[...].reshape(-1, 16, LANES).astype(BF16)


def unit_kernel(keep_ref, sent_ref, got_ref, near_ref, far_a_ref, far_b_ref, last_ref):
    place = lax.axis_index("lat")
    second = lax.rem(place, 2) == 1
    n = keep_ref.shape[0]
    own_c, own_i = keep_ref[...].astype(F32), sent_ref[n:].astype(F32)
    got_c, got_i = got_ref[:n].astype(F32), got_ref[n:].astype(F32)
    b0 = jnp.where(second, got_c, own_c)
    b1 = jnp.where(second, own_c, got_c)
    i0 = jnp.where(second, got_i, own_i)
    i1 = jnp.where(second, own_i, got_i)
    unit = jnp.concatenate([b0[: n - 2], b0[n - 2 :] + b1[:2], b1[2:]], axis=0)
    near_ref[0 : 2 * n - 2] = unit.astype(BF16)
    at = 2 * n - 2
    for step in range(2):
        for part in range(2):
            near_ref[at] = i0[2 * step + part].astype(BF16)
            near_ref[at + 1] = i1[2 * step + part].astype(BF16)
            at += 2
    near_ref[at] = jnp.concatenate([i0[6, :8], i1[6, :8]], axis=0).astype(BF16)
    near_ref[at + 1] = jnp.concatenate([i0[6, 8:], i1[6, 8:]], axis=0).astype(BF16)
    near_ref[at + 2] = jnp.concatenate([i0[7, :8], i1[7, :8]], axis=0).astype(BF16)
    for part in range(2):
        last_ref[2 * part] = i0[4 + part].astype(BF16)
        last_ref[2 * part + 1] = i1[4 + part].astype(BF16)
    even_quad = lax.rem(lax.div(place, 4), 2) == 0
    count = far_a_ref.shape[0] - 3
    base = 2 * n - 2
    for ref, right in ((far_a_ref, even_quad), (far_b_ref, jnp.logical_not(even_quad))):
        start = jnp.where(right, base - count, 0)
        pick = jnp.where(right, 1, 0)
        ref[0:count] = near_ref[pl.ds(start, count)]
        ref[count] = near_ref[base + pick]
        ref[count + 1] = near_ref[base + 2 + pick]
        ref[count + 2] = near_ref[base + 8]


def main_kernel(
    units,
    near_ref,
    last_ref,
    a1_ref,
    b1_ref,
    a2_ref,
    b2_ref,
    table_ref,
    forward_ref,
    inverse_ref,
    scale_ref,
    keep_ref,
    send_ref,
    c_ref,
    p_ref,
    ve_ref,
    vo_ref,
    xe_ref,
    xo_ref,
    slow_ref,
    cos_ref,
    sin_ref,
    pick_ref,
    image_ref,
):
    place = lax.axis_index("lat")
    unit = lax.div(place, 2)
    second = lax.rem(place, 2)
    odd_unit = lax.rem(unit, 2) == 1
    odd_quad = lax.rem(lax.div(place, 4), 2) == 1
    has_l1, has_l2 = unit >= 1, unit >= 2
    has_r1, has_r2 = unit + 1 < units, unit + 2 < units
    pairs = 16
    coef_n = pairs + 2
    far_n = a2_ref.shape[0] - 3
    tables = table_ref.shape[0]

    def valid(flag, v):
        return jnp.where(flag, v, jnp.zeros_like(v))

    def choose(flag, x_ref, y_ref, lo, hi):
        return jnp.where(flag, x_ref[lo:hi], y_ref[lo:hi]).astype(F32)

    base = 26
    own = near_ref[0:coef_n].astype(F32)
    left = valid(has_l1, choose(odd_unit, a1_ref, b1_ref, 0, coef_n))
    right = valid(has_r1, choose(odd_unit, b1_ref, a1_ref, 0, coef_n))
    left2 = valid(has_l2, choose(odd_quad, a2_ref, b2_ref, 0, far_n))
    right2 = valid(has_r2, choose(odd_quad, b2_ref, a2_ref, 0, far_n))
    c_ref[0 : far_n - 2] = left2[: far_n - 2].astype(BF16)
    c_ref[base - 17 : base - 15] = (left2[far_n - 2 :] + jnp.concatenate(
        [valid(has_l2, left[0:1]), left[1:2]], axis=0)).astype(BF16)
    c_ref[base - 15 : base - 1] = left[2 : coef_n - 2].astype(BF16)
    c_ref[base - 1 : base + 1] = (left[coef_n - 2 :] + jnp.concatenate(
        [valid(has_l1, own[0:1]), own[1:2]], axis=0)).astype(BF16)
    c_ref[base + 1 : base + 15] = own[2 : coef_n - 2].astype(BF16)
    c_ref[base + 15 : base + 17] = (right[:2] + jnp.concatenate(
        [own[coef_n - 2 : coef_n - 1], valid(has_r1, own[coef_n - 1 :])], axis=0)).astype(BF16)
    c_ref[base + 17 : base + 31] = right[2 : coef_n - 2].astype(BF16)
    c_ref[base + 31 : base + 33] = (right2[:2] + jnp.concatenate(
        [right[coef_n - 2 : coef_n - 1], valid(has_r2, right[coef_n - 1 :])], axis=0)).astype(BF16)
    c_ref[base + 33 : base + 31 + far_n] = right2[2:].astype(BF16)

    at = coef_n
    far_rows = 48
    for step in range(2):
        lo = at + 4 * step
        for ref_rows, flag, pos in ((0, odd_unit, -32), (1, jnp.logical_not(odd_unit), 32)):
            hi_v = choose(flag, a1_ref, b1_ref, lo, lo + 2)
            lo_v = choose(flag, a1_ref, b1_ref, lo + 2, lo + 4)
            slow_ref[step, far_rows + pos : far_rows + pos + 32] = (hi_v + lo_v).reshape(32, LANES)
        slow_ref[step, far_rows : far_rows + 32] = (
            near_ref[lo : lo + 2].astype(F32) + near_ref[lo + 2 : lo + 4].astype(F32)
        ).reshape(32, LANES)
    for flag, pos in ((odd_quad, -48), (jnp.logical_not(odd_quad), 64)):
        rows = choose(flag, a2_ref, b2_ref, far_n, far_n + 1) + choose(
            flag, a2_ref, b2_ref, far_n + 1, far_n + 2
        )
        slow_ref[0, far_rows + pos : far_rows + pos + 16] = rows[0]
    slow_ref[2, far_rows : far_rows + 32] = (
        last_ref[0:2].astype(F32) + last_ref[2:4].astype(F32)
    ).reshape(32, LANES)

    for step in range(STEPS):
        pos = coef_n + 8 + step
        pick_ref[step, 32:48] = near_ref[pos].astype(F32)
        pick_ref[step, 16:32] = jnp.where(
            has_l1, choose(odd_unit, a1_ref, b1_ref, pos, pos + 1)[0], -1.0)
        pick_ref[step, 48:64] = jnp.where(
            has_r1, choose(odd_unit, b1_ref, a1_ref, pos, pos + 1)[0], -1.0)
    pick_ref[0, 0:16] = jnp.where(
        has_l2, choose(odd_quad, a2_ref, b2_ref, far_n + 2, far_n + 3)[0], -1.0)
    pick_ref[0, 64:80] = jnp.where(
        has_r2, choose(odd_quad, b2_ref, a2_ref, far_n + 2, far_n + 3)[0], -1.0)

    scale = scale_ref[0]
    row8 = lax.broadcasted_iota(jnp.int32, (1, 8, LANES), 1)
    sign = jnp.where(row8 < 4, 1.0, -1.0).astype(F32)
    lane3 = low_lanes((1, 1, LANES))
    lane2 = low_lanes((1, LANES))

    def table_rows(parity):
        zero = jnp.zeros((COEFS, tables * LANES), BF16)
        full = jnp.concatenate([table_ref[t] for t in range(tables)], axis=1)
        return jnp.concatenate([full, zero] if parity == 0 else [zero, full], axis=0)

    plan = (
        dict(lo=-18, hi=34, base=26, first=-17),
        dict(lo=-9, hi=25, base=17, first=-9),
        dict(lo=-1, hi=17, base=9, first=0),
    )
    for step, item in enumerate(plan):
        lo, hi = item["lo"], item["hi"]
        count = hi - lo
        off = item["base"] + lo - 8
        rows = pick_ref[step, lo + 32 : hi + 32]
        swapped = lane_swap(rows)
        for parity, v_ref in ((0, ve_ref), (1, vo_ref)):
            lhs = jnp.concatenate(
                [c_ref[off + k : off + k + count].reshape(count * 16, LANES) for k in range(17)],
                axis=1,
            )
            out = jnp.dot(lhs, table_rows(parity), preferred_element_type=F32)
            pick = jnp.where(lane2, rows, swapped) if parity == 0 else jnp.where(lane2, swapped, rows)
            pick = pick.reshape(count, 1, LANES)
            v = jnp.zeros((count, 16, LANES), F32)
            for t in range(tables):
                v = jnp.where(
                    pick == float(t), out[:, LANES * t : LANES * (t + 1)].reshape(count, 16, LANES), v
                )
            v_ref[0:count] = v
        ve, vo = ve_ref[0:count], vo_ref[0:count]
        x = jnp.where(lane3, ve, lane_swap(vo))
        y = jnp.where(lane3, lane_swap(ve), vo)
        prop = jnp.concatenate(
            [x[:, :8] - sign * y[:, 8:], x[:, 8:] + sign * y[:, :8]], axis=1
        )
        p_ref[0] = jnp.zeros((16, LANES), BF16)
        p_ref[1 : count + 1] = prop.astype(BF16)
        first = item["first"]
        n = hi - first
        o = first - lo
        lhs = jnp.concatenate(
            [p_ref[o : o + n].reshape(n * 16, LANES), p_ref[o + 1 : o + 1 + n].reshape(n * 16, LANES)],
            axis=1,
        )
        back = jnp.dot(lhs, inverse_ref[...], preferred_element_type=F32)
        g0 = 2 * first + far_rows
        before = slow_ref[step, g0 - 1 : g0 - 1 + 2 * n]
        after = slow_ref[step, g0 : g0 + 2 * n]
        if step < 2:
            number = lax.broadcasted_iota(jnp.int32, (2 * n, 1), 0) + 2 * first
            def exists(block):
                inside = (block >= 0) & (block < 32)
                l1 = (block < 0) & (block >= -32) & has_l1
                r1 = (block >= 32) & (block < 64) & has_r1
                l2 = (block < -32) & has_l2
                r2 = (block >= 64) & has_r2
                return inside | l1 | r1 | l2 | r2
            ok = jnp.where(lane2, exists(number - 1).astype(jnp.int32), exists(number).astype(jnp.int32)) > 0
        theta = scale * jnp.where(lane2, lane_swap(before), lane_swap(after))
        sin_v, cos_v = sin_cos(theta)
        if step < 2:
            sin_v = jnp.where(ok, sin_v, 0.0)
            cos_v = jnp.where(ok, cos_v, 0.0)
        cos_ref[0 : 2 * n] = cos_v
        sin_ref[0 : 2 * n] = sin_v
        images = []
        for parity, x_ref in ((0, xe_ref), (1, xo_ref)):
            b = back[:, LANES * parity : LANES * (parity + 1)].reshape(n, 16, LANES)
            c = cos_ref[pl.ds(parity, n, stride=2)].reshape(n, 1, LANES)
            s = sin_ref[pl.ds(parity, n, stride=2)].reshape(n, 1, LANES) * sign
            f0 = c * b[:, :8] - s * b[:, 8:]
            f1 = c * b[:, 8:] + s * b[:, :8]
            if step < 2:
                x_ref[0:n] = jnp.concatenate([f0, f1], axis=1).astype(BF16)
            m = 17 - parity
            f0, f1 = f0[-first : -first + m], f1[-first : -first + m]
            images.append(lane_swap(f0 * pltpu.roll(f0, 4, 1) + f1 * pltpu.roll(f1, 4, 1)))
        even, odd = images
        image_ref[step, 0] = jnp.where(lane3, even[:16], odd)
        image_ref[step, 1] = jnp.where(lane3, odd, even[1:])
        if step < 2:
            if step == 1:
                xe_ref[n] = jnp.zeros((16, LANES), BF16)
                m = n
            else:
                m = n - 1
            lhs = jnp.concatenate(
                [
                    xe_ref[0:m].reshape(m * 16, LANES),
                    xo_ref[0:m].reshape(m * 16, LANES),
                    xe_ref[1 : m + 1].reshape(m * 16, LANES),
                ],
                axis=1,
            )
            coefs = jnp.dot(lhs, forward_ref[...], preferred_element_type=F32).reshape(m, 16, LANES)
            number = lax.broadcasted_iota(jnp.int32, (m, 1, 1), 0) + first
            ok = (
                ((number >= 0) & (number < 16))
                | ((number < 0) & (number >= -16) & has_l1)
                | ((number >= 16) & (number < 32) & has_r1)
                | ((number < -16) & has_l2)
                | ((number >= 32) & has_r2)
            )
            c_ref[0:m] = jnp.where(ok, coefs, 0.0).astype(BF16)
    row3 = row8 < 4
    for ref, half in ((keep_ref, second), (send_ref, 1 - second)):
        for parity in range(2):
            span = pl.ds(8 * half, 8)
            top = jnp.where(row3, image_ref[0, parity, span], image_ref[1, parity, span])
            ref[parity] = jnp.concatenate([top, image_ref[2, parity, span]], axis=1).astype(BF16)


def final_kernel(a_ref, b_ref, out_ref):
    total = a_ref[...].astype(F32) + b_ref[...].astype(F32)
    for parity in range(2):
        for q in range(8):
            cut = slice(WINDOW * (2 * q + parity), WINDOW * (2 * q + parity + 1))
            for n in range(STEPS):
                out_ref[n, :, cut] = total[parity, q, 4 * n : 4 * n + 4]


def matching(size, by, odd):
    pairs = []
    for i in range(size):
        right = (i // by) % 2 == odd
        j = i + by if right else i - by
        pairs.append((i, j if 0 <= j < size else i))
    return pairs


def on_device(wavefield, propagator_table, table_index, slowness, frequency_scale):
    sources = wavefield.shape[2]
    points = wavefield.shape[3]
    lat = lax.axis_size("lat")
    freqs = lax.axis_size("freq")
    pairs = points // (2 * WINDOW)
    first, forward, inverse = (jnp.asarray(m, BF16) for m in pair_matrices())
    vmem = pl.BlockSpec(memory_space=pltpu.VMEM)
    smem = pl.BlockSpec(memory_space=pltpu.SMEM)

    def tiles(n):
        return jax.ShapeDtypeStruct((n, 16, LANES), BF16)

    info = 8
    keep, send = pl.pallas_call(
        prep_kernel,
        out_shape=(tiles(pairs + 2), tiles(pairs + 2 + info)),
        in_specs=[vmem, vmem, smem, vmem],
        out_specs=(vmem, vmem),
        scratch_shapes=[
            pltpu.VMEM((2, pairs + 2, 16, LANES), BF16),
            pltpu.VMEM((info * 16, LANES), F32),
        ],
        name="prep",
    )(wavefield, slowness, table_index, first)
    partner = [(i, i ^ 1) for i in range(lat)]
    got = lax.ppermute(send, "lat", partner)
    near_n = 2 * (pairs + 2) - 2 + 8 + STEPS
    far_n = 11 + 3
    near, far_a, far_b, last = pl.pallas_call(
        unit_kernel,
        out_shape=(tiles(near_n), tiles(far_n), tiles(far_n), tiles(4)),
        in_specs=[vmem] * 3,
        out_specs=(vmem,) * 4,
        name="unit",
    )(keep, send, got)
    a1 = lax.ppermute(near, "lat", matching(lat, 2, 0))
    b1 = lax.ppermute(near, "lat", matching(lat, 2, 1))
    a2 = lax.ppermute(far_a, "lat", matching(lat, 4, 0))
    b2 = lax.ppermute(far_b, "lat", matching(lat, 4, 1))
    image = jax.ShapeDtypeStruct((2, pairs, 16, LANES), BF16)
    own, other = pl.pallas_call(
        lambda *refs: main_kernel(lat // 2, *refs),
        out_shape=(image, image),
        in_specs=[vmem] * 9 + [smem],
        out_specs=(vmem, vmem),
        scratch_shapes=[
            pltpu.VMEM((68, 16, LANES), BF16),
            pltpu.VMEM((53, 16, LANES), BF16),
            pltpu.VMEM((52, 16, LANES), F32),
            pltpu.VMEM((52, 16, LANES), F32),
            pltpu.VMEM((52, 16, LANES), BF16),
            pltpu.VMEM((52, 16, LANES), BF16),
            pltpu.VMEM((STEPS, 128, LANES), F32),
            pltpu.VMEM((104, LANES), F32),
            pltpu.VMEM((104, LANES), F32),
            pltpu.VMEM((STEPS, 80, LANES), F32),
            pltpu.VMEM((STEPS, 2, 16, 8, LANES), F32),
        ],
        name="steps",
    )(near, last, a1, b1, a2, b2, propagator_table[0], forward, inverse, frequency_scale)
    swapped = lax.ppermute(other, "lat", partner)
    core = lax.rem(lax.axis_index("lat"), 2)
    if freqs == 2:
        mine = core == lax.axis_index("freq")
        stay = jnp.where(mine, own, swapped)
        leave = jnp.where(mine, swapped, own)
        come = lax.ppermute(leave, "freq", [(0, 1), (1, 0)])
        return pl.pallas_call(
            final_kernel,
            out_shape=jax.ShapeDtypeStruct((STEPS, sources // 2, points), F32),
            in_specs=[vmem, vmem],
            out_specs=vmem,
            name="total",
        )(stay, come)
    low = jnp.where(core == 0, own, swapped)
    high = jnp.where(core == 0, swapped, own)
    whole = jnp.stack([low, high])[:, :, :, : 4 * STEPS]
    whole = whole.reshape(2, 2, pairs, STEPS, 4, LANES)
    whole = jnp.transpose(whole, (3, 0, 4, 2, 1, 5)).reshape(STEPS, sources, points)
    return lax.psum_scatter(whole, "freq", scatter_dimension=1, tiled=True).astype(F32)


def solution(mesh):
    placed = (
        P(None, "freq", None, "lat"),
        P("freq", None, None, None),
        P(None, "lat"),
        P(None, "lat"),
        P("freq"),
    )
    return jax.shard_map(
        on_device, mesh=mesh, in_specs=placed, out_specs=P(None, "freq", "lat"), check_vma=False
    )
```

time: 181 us -> 40.3 us (0.22); the launches traced: 178 us -> 39.9 us
  starting transfers between devices: 58.4 us -> 10 us
  local copies, waits for them, and re-layouts: 46.7 us -> 1.93 us
  waiting for transfers between devices: 39.5 us -> 8.26 us
  Pallas kernels: 0 us -> 17.5 us
  between operations: 16 us -> 0.7 us
  matrix products: 11.6 us -> 0 us
  other arithmetic: 5.78 us -> 1.47 us
    ppermute x18 -> x7, starting transfers between devices: 58.4 us -> 10 us  [the longest x1 4.4 us: on_device(): b1 = lax.ppermute(near, 'lat', matching(lat, 2, 1))]
    another operation x9 -> x0, local copies, waits for them, and re-layouts: 38.3 us -> none
    unnamed x2 -> x0, waiting for transfers between devices: 22.5 us -> none
    pallas_call x0 -> x4, Pallas kernels: none -> 17.5 us  [the longest x1 12.4 us: on_device(): pl.pallas_call(lambda *refs: main_kernel(lat // 2, *refs), out_shape=(ima...]
    dot_general x12 -> x0, matrix products: 11.6 us -> none  [the longest x3 9.09 us: on_device(): jnp.einsum('fwrk,fkc->fwrc', unfolded, all_tables, preferred_element_type...]
    ppermute x18 -> x7, waiting for transfers between devices: 17 us -> 8.26 us  [the longest x1 2.75 us: on_device(): come = lax.ppermute(leave, 'freq', [(0, 1), (1, 0)])]
    convert_element_type x5 -> x0, other arithmetic: 3.11 us -> none  [the longest x1 1.55 us: on_device(): return lax.psum_scatter(jnp.stack(partials).astype(jnp.bfloat16), 'freq',...]
    scatter-add x6 -> x0, local copies, waits for them, and re-layouts: 2.53 us -> none  [the longest x3 1.88 us: on_device(): back = back.at[..., points - MARGIN:].add(rims[..., 3 * MARGIN:])]
  transfers between devices with their start and end apart: 19 -> 7, of which waited for: 12 -> 5; matrix products, arithmetic and copies ran while one was open for 3% -> 0% of each run, Pallas kernels for 0% -> 0%
where the time goes in v1:
time: 40.3 us; the launch traced here: 39.9 us
  Pallas kernels  17.5 us (43%)
  starting transfers between devices  10 us (25%)
  waiting for transfers between devices  8.26 us (20%)
  local copies, waits for them, and re-layouts  1.93 us (5%)
  other arithmetic  1.47 us (4%)
  between operations  0.7 us (2%)
    pallas_call x1, Pallas kernels, on_device(): pl.pallas_call(lambda *refs: main_kernel(lat // 2, *refs), out_shape=(ima...  12.4 us
    ppermute x1, starting transfers between devices, on_device(): b1 = lax.ppermute(near, 'lat', matching(lat, 2, 1))  4.4 us
    ppermute x1, starting transfers between devices, on_device(): b2 = lax.ppermute(far_b, 'lat', matching(lat, 4, 1))  3.04 us
    ppermute x1, waiting for transfers between devices, on_device(): come = lax.ppermute(leave, 'freq', [(0, 1), (1, 0)])  2.75 us
    unnamed x12, local copies, waits for them, and re-layouts  1.93 us
    pallas_call x1, Pallas kernels, on_device(): pl.pallas_call(prep_kernel, out_shape=(tiles(pairs + 2), tiles(pairs + 2...  1.93 us
    ppermute x1, waiting for transfers between devices, on_device(): b2 = lax.ppermute(far_b, 'lat', matching(lat, 4, 1))  1.93 us
    pallas_call x1, Pallas kernels, on_device(): pl.pallas_call(unit_kernel, out_shape=(tiles(near_n), tiles(far_n), tiles...  1.69 us
  transfers between devices with their start and end apart: 7, of which 5 were waited for; matrix products, arithmetic and copies ran while one was open for 0% of the time, Pallas kernels for 0%

profile of v1, /device:TPU:10, one launch (start us, length us, event | category | flops | bytes accessed | tf_op | source)
XLA Modules:
  0.0 39.9 jit_solution(15343615009541455590)
XLA Ops:
  0.0 1.9 %prep.1 = (bf16[10,16,128]{2,1,0:T(8,128)(2,1)}, bf16[18,16,128]{2,1,0:T(8,128)(2,1)}) custom-call(f32[4,1,8,2048]{3,2,1,0:T(8,128)} %wave_ref.1, f32[3,2048]{1,0:T(4,128)} %slow_ref.1, s32[3,16]{1,0:T(4,128)} %index_ref.1, bf16[512,128]{1,0:T(8,128)(2,1)} %constant.19.clone.first_ref), custom_call_target="tpu_custom_call" | custom-call | tf_op jit(solution)/shard_map/prep/pallas_call | solution.py:412
  1.9 0.0 collective-permute-start
  1.9 1.5 %collective-permute-done.got_ref = bf16[18,16,128]{2,1,0:T(8,128)(2,1)S(1)} collective-permute-done((bf16[18,16,128]{2,1,0:T(8,128)(2,1)}, bf16[18,16,128]{2,1,0:T(8,128)(2,1)S(1)}, u32[]{:S(2)}, u32[]{:S(2)}) %collective-permute-start) | collective-permute-done | bytes 73760 | tf_op jit(solution)/shard_map/ppermute | solution.py:424
  3.4 0.0 copy-start.2
  3.4 0.6 %copy-done.2 = bf16[18,16,128]{2,1,0:T(8,128)(2,1)} copy-done((bf16[18,16,128]{2,1,0:T(8,128)(2,1)}, bf16[18,16,128]{2,1,0:T(8,128)(2,1)S(1)}, u32[]{:S(2)}) %copy-start.2) | copy-done | bytes 73752
  4.0 1.7 %unit.1 = (bf16[29,16,128]{2,1,0:T(8,128)(2,1)}, bf16[14,16,128]{2,1,0:T(8,128)(2,1)}, bf16[14,16,128]{2,1,0:T(8,128)(2,1)}, bf16[4,16,128]{2,1,0:T(8,128)(2,1)}) custom-call(bf16[10,16,128]{2,1,0:T(8,128)(2,1)} %get-tuple-element.13.keep_ref, bf16[18,16,128]{2,1,0:T(8,128)(2,1)} %get-tuple-element.14.sent_ref, bf16[18,16,128]{2,1,0:T(8,128)(2,1)} %copy-done.2), custom_call_target="tpu_custom_call" | custom-call | tf_op jit(solution)/shard_map/unit/pallas_call | solution.py:427
  5.7 0.5 %collective-permute-start.1 = (bf16[29,16,128]{2,1,0:T(8,128)(2,1)}, bf16[29,16,128]{2,1,0:T(8,128)(2,1)S(1)}, u32[]{:S(2)}, u32[]{:S(2)}) collective-permute-start(bf16[29,16,128]{2,1,0:T(8,128)(2,1)} %get-tuple-element.15.refs_0_), channel_id=1, source_target_pairs={{0,4},{2,6},{4,0},{6,2},{8,12},{10,14},{12,8},{14,10},{16,20},{18,... | collective-permute-start | bytes 356360 | tf_op jit(solution)/shard_map/ppermute | solution.py:434
  6.3 4.4 %collective-permute-start.2 = (bf16[29,16,128]{2,1,0:T(8,128)(2,1)}, bf16[29,16,128]{2,1,0:T(8,128)(2,1)S(1)}, u32[]{:S(2)}, u32[]{:S(2)}) collective-permute-start(bf16[29,16,128]{2,1,0:T(8,128)(2,1)} %get-tuple-element.15.refs_0_), channel_id=1, source_target_pairs={{0,0},{2,2},{4,8},{6,10},{8,4},{10,6},{12,16},{14,18},{16,12},{18,... | collective-permute-start | bytes 356360 | tf_op jit(solution)/shard_map/ppermute | solution.py:435
  10.7 0.5 %collective-permute-start.3 = (bf16[14,16,128]{2,1,0:T(8,128)(2,1)}, bf16[14,16,128]{2,1,0:T(8,128)(2,1)S(1)}, u32[]{:S(2)}, u32[]{:S(2)}) collective-permute-start(bf16[14,16,128]{2,1,0:T(8,128)(2,1)} %get-tuple-element.17), channel_id=1, source_target_pairs={{0,8},{2,10},{4,12},{6,14},{8,0},{10,2},{12,4},{14,6},{16,24},{18,... | collective-permute-start | bytes 172040 | tf_op jit(solution)/shard_map/ppermute | solution.py:436
  11.2 3.0 %collective-permute-start.4 = (bf16[14,16,128]{2,1,0:T(8,128)(2,1)}, bf16[14,16,128]{2,1,0:T(8,128)(2,1)S(1)}, u32[]{:S(2)}, u32[]{:S(2)}) collective-permute-start(bf16[14,16,128]{2,1,0:T(8,128)(2,1)} %get-tuple-element.18), channel_id=1, source_target_pairs={{0,0},{2,2},{4,4},{6,6},{8,16},{10,18},{12,20},{14,22},{16,8},{18,... | collective-permute-start | bytes 172040 | tf_op jit(solution)/shard_map/ppermute | solution.py:437
  14.9 0.6 %collective-permute-done.3.refs_4_ = bf16[14,16,128]{2,1,0:T(8,128)(2,1)S(1)} collective-permute-done((bf16[14,16,128]{2,1,0:T(8,128)(2,1)}, bf16[14,16,128]{2,1,0:T(8,128)(2,1)S(1)}, u32[]{:S(2)}, u32[]{:S(2)}) %collective-permute-start.3) | collective-permute-done | bytes 57376 | tf_op jit(solution)/shard_map/ppermute | solution.py:436
  15.5 0.0 copy-start.4
  15.5 1.9 %collective-permute-done.4.refs_5_ = bf16[14,16,128]{2,1,0:T(8,128)(2,1)S(1)} collective-permute-done((bf16[14,16,128]{2,1,0:T(8,128)(2,1)}, bf16[14,16,128]{2,1,0:T(8,128)(2,1)S(1)}, u32[]{:S(2)}, u32[]{:S(2)}) %collective-permute-start.4) | collective-permute-done | bytes 57376 | tf_op jit(solution)/shard_map/ppermute | solution.py:437
  17.4 0.0 copy-start.5
  17.5 0.0 collective-permute-done.1.refs_2_
  17.5 0.0 copy-start
  17.5 0.0 collective-permute-done.2.refs_3_
  17.5 0.0 copy-start.1
  17.5 0.0 copy-done.4
  17.5 0.6 %copy-done.5 = bf16[14,16,128]{2,1,0:T(8,128)(2,1)} copy-done((bf16[14,16,128]{2,1,0:T(8,128)(2,1)}, bf16[14,16,128]{2,1,0:T(8,128)(2,1)S(1)}, u32[]{:S(2)}) %copy-start.5) | copy-done | bytes 57368
  18.1 0.1 copy-done
  18.1 0.0 copy-done.1
  18.2 12.4 %steps.1 = (bf16[2,8,16,128]{3,2,1,0:T(8,128)(2,1)}, bf16[2,8,16,128]{3,2,1,0:T(8,128)(2,1)}) custom-call(bf16[29,16,128]{2,1,0:T(8,128)(2,1)} %get-tuple-element.15.refs_0_, bf16[4,16,128]{2,1,0:T(8,128)(2,1)} %get-tuple-element.16.refs_1_, bf16[29,16,128]{2,1,0:T(8,128)(2,1)} %copy-done, bf16[29,16,128]{2,1,0:T(8,128)(2,1)} %copy-done.1, ...), custom_call_target="tpu_custom_call" | custom-call | tf_op jit(solution)/shard_map/steps/pallas_call | solution.py:439
  30.6 0.0 collective-permute-start.5
  30.6 1.5 %collective-permute-done.5 = bf16[2,8,16,128]{3,2,1,0:T(8,128)(2,1)S(1)} collective-permute-done((bf16[2,8,16,128]{3,2,1,0:T(8,128)(2,1)}, bf16[2,8,16,128]{3,2,1,0:T(8,128)(2,1)S(1)}, u32[]{:S(2)}, u32[]{:S(2)}) %collective-permute-start.5) | collective-permute-done | bytes 65568 | tf_op jit(solution)/shard_map/ppermute | solution.py:459
  32.0 1.5 %broadcast_select_fusion = (bf16[2,8,16,128]{3,2,1,0:T(8,128)(2,1)S(1)}, bf16[2,8,16,128]{3,2,1,0:T(8,128)(2,1)}) fusion(bf16[2,8,16,128]{3,2,1,0:T(8,128)(2,1)S(1)} %collective-permute-done.5, bf16[2,8,16,128]{3,2,1,0:T(8,128)(2,1)} %get-tuple-element.19, pred[]{:T(512)S(6)} %eq.3), kind=kLoop, calls=%fused_computation | loop fusion | flops 65536 | bytes 262145 | tf_op jit(solution)/shard_map/jit(_where)/select_n | solution.py:464
  33.5 1.5 %collective-permute-start.6 = (bf16[2,8,16,128]{3,2,1,0:T(8,128)(2,1)S(1)}, bf16[2,8,16,128]{3,2,1,0:T(8,128)(2,1)S(1)}, u32[]{:S(2)}, u32[]{:S(2)}) collective-permute-start(bf16[2,8,16,128]{3,2,1,0:T(8,128)(2,1)S(1)} %get-tuple-element.21), channel_id=1, source_target_pairs={{0,1},{1,0},{2,3},{3,2},{4,5},{5,4},{6,7},{7,6},{8,9},{9,8},{10,11... | collective-permute-start | bytes 196616 | tf_op jit(solution)/shard_map/ppermute | solution.py:465
  35.0 2.8 %collective-permute-done.6.b_ref = bf16[2,8,16,128]{3,2,1,0:T(8,128)(2,1)S(1)} collective-permute-done((bf16[2,8,16,128]{3,2,1,0:T(8,128)(2,1)S(1)}, bf16[2,8,16,128]{3,2,1,0:T(8,128)(2,1)S(1)}, u32[]{:S(2)}, u32[]{:S(2)}) %collective-permute-start.6) | collective-permute-done | bytes 65568 | tf_op jit(solution)/shard_map/ppermute | solution.py:465
  37.8 0.0 copy-start.3
  37.8 0.6 %copy-done.3 = bf16[2,8,16,128]{3,2,1,0:T(8,128)(2,1)} copy-done((bf16[2,8,16,128]{3,2,1,0:T(8,128)(2,1)}, bf16[2,8,16,128]{3,2,1,0:T(8,128)(2,1)S(1)}, u32[]{:S(2)}) %copy-start.3) | copy-done | bytes 65560
  38.4 1.5 %total.1 = f32[3,4,2048]{2,1,0:T(4,128)} custom-call(bf16[2,8,16,128]{3,2,1,0:T(8,128)(2,1)} %get-tuple-element.22.a_ref, bf16[2,8,16,128]{3,2,1,0:T(8,128)(2,1)} %copy-done.3), custom_call_target="tpu_custom_call" | custom-call | tf_op jit(solution)/shard_map/total/pallas_call | solution.py:466
Async XLA Ops:
  1.9 1.5 %collective-permute-start = (bf16[18,16,128]{2,1,0:T(8,128)(2,1)}, bf16[18,16,128]{2,1,0:T(8,128)(2,1)S(1)}, u32[]{:S(2)}, u32[]{:S(2)}) collective-permute-start(bf16[18,16,128]{2,1,0:T(8,128)(2,1)} %get-tuple-element.14.sent_ref), channel_id=1, source_target_pairs={{0,2},{2,0},{4,6},{6,4},{8,10},{10,8},{12,14},{14,12},{16,18},{18,... | collective-permute-start | bytes 221192 | tf_op jit(solution)/shard_map/ppermute | solution.py:424
  3.4 0.6 %copy-start.2 = (bf16[18,16,128]{2,1,0:T(8,128)(2,1)}, bf16[18,16,128]{2,1,0:T(8,128)(2,1)S(1)}, u32[]{:S(2)}) copy-start(bf16[18,16,128]{2,1,0:T(8,128)(2,1)S(1)} %collective-permute-done.got_ref) | copy-start | bytes 221188
  5.7 11.7 %collective-permute-start.1 = (bf16[29,16,128]{2,1,0:T(8,128)(2,1)}, bf16[29,16,128]{2,1,0:T(8,128)(2,1)S(1)}, u32[]{:S(2)}, u32[]{:S(2)}) collective-permute-start(bf16[29,16,128]{2,1,0:T(8,128)(2,1)} %get-tuple-element.15.refs_0_), channel_id=1, source_target_pairs={{0,4},{2,6},{4,0},{6,2},{8,12},{10,14},{12,8},{14,10},{16,20},{18,... | collective-permute-start | bytes 356360 | tf_op jit(solution)/shard_map/ppermute | solution.py:434
  6.3 11.2 %collective-permute-start.2 = (bf16[29,16,128]{2,1,0:T(8,128)(2,1)}, bf16[29,16,128]{2,1,0:T(8,128)(2,1)S(1)}, u32[]{:S(2)}, u32[]{:S(2)}) collective-permute-start(bf16[29,16,128]{2,1,0:T(8,128)(2,1)} %get-tuple-element.15.refs_0_), channel_id=1, source_target_pairs={{0,0},{2,2},{4,8},{6,10},{8,4},{10,6},{12,16},{14,18},{16,12},{18,... | collective-permute-start | bytes 356360 | tf_op jit(solution)/shard_map/ppermute | solution.py:435
  10.7 4.9 %collective-permute-start.3 = (bf16[14,16,128]{2,1,0:T(8,128)(2,1)}, bf16[14,16,128]{2,1,0:T(8,128)(2,1)S(1)}, u32[]{:S(2)}, u32[]{:S(2)}) collective-permute-start(bf16[14,16,128]{2,1,0:T(8,128)(2,1)} %get-tuple-element.17), channel_id=1, source_target_pairs={{0,8},{2,10},{4,12},{6,14},{8,0},{10,2},{12,4},{14,6},{16,24},{18,... | collective-permute-start | bytes 172040 | tf_op jit(solution)/shard_map/ppermute | solution.py:436
  11.2 6.3 %collective-permute-start.4 = (bf16[14,16,128]{2,1,0:T(8,128)(2,1)}, bf16[14,16,128]{2,1,0:T(8,128)(2,1)S(1)}, u32[]{:S(2)}, u32[]{:S(2)}) collective-permute-start(bf16[14,16,128]{2,1,0:T(8,128)(2,1)} %get-tuple-element.18), channel_id=1, source_target_pairs={{0,0},{2,2},{4,4},{6,6},{8,16},{10,18},{12,20},{14,22},{16,8},{18,... | collective-permute-start | bytes 172040 | tf_op jit(solution)/shard_map/ppermute | solution.py:437
  15.5 2.0 %copy-start.4 = (bf16[14,16,128]{2,1,0:T(8,128)(2,1)}, bf16[14,16,128]{2,1,0:T(8,128)(2,1)S(1)}, u32[]{:S(2)}) copy-start(bf16[14,16,128]{2,1,0:T(8,128)(2,1)S(1)} %collective-permute-done.3.refs_4_) | copy-start | bytes 172036
  17.4 0.6 %copy-start.5 = (bf16[14,16,128]{2,1,0:T(8,128)(2,1)}, bf16[14,16,128]{2,1,0:T(8,128)(2,1)S(1)}, u32[]{:S(2)}) copy-start(bf16[14,16,128]{2,1,0:T(8,128)(2,1)S(1)} %collective-permute-done.4.refs_5_) | copy-start | bytes 172036
  17.5 0.7 %copy-start = (bf16[29,16,128]{2,1,0:T(8,128)(2,1)}, bf16[29,16,128]{2,1,0:T(8,128)(2,1)S(1)}, u32[]{:S(2)}) copy-start(bf16[29,16,128]{2,1,0:T(8,128)(2,1)S(1)} %collective-permute-done.1.refs_2_) | copy-start | bytes 356356
  17.5 0.7 %copy-start.1 = (bf16[29,16,128]{2,1,0:T(8,128)(2,1)}, bf16[29,16,128]{2,1,0:T(8,128)(2,1)S(1)}, u32[]{:S(2)}) copy-start(bf16[29,16,128]{2,1,0:T(8,128)(2,1)S(1)} %collective-permute-done.2.refs_3_) | copy-start | bytes 356356
  30.6 1.5 %collective-permute-start.5 = (bf16[2,8,16,128]{3,2,1,0:T(8,128)(2,1)}, bf16[2,8,16,128]{3,2,1,0:T(8,128)(2,1)S(1)}, u32[]{:S(2)}, u32[]{:S(2)}) collective-permute-start(bf16[2,8,16,128]{3,2,1,0:T(8,128)(2,1)} %get-tuple-element.20), channel_id=1, source_target_pairs={{0,2},{2,0},{4,6},{6,4},{8,10},{10,8},{12,14},{14,12},{16,18},{18,... | collective-permute-start | bytes 196616 | tf_op jit(solution)/shard_map/ppermute | solution.py:459
  33.5 4.3 %collective-permute-start.6 = (bf16[2,8,16,128]{3,2,1,0:T(8,128)(2,1)S(1)}, bf16[2,8,16,128]{3,2,1,0:T(8,128)(2,1)S(1)}, u32[]{:S(2)}, u32[]{:S(2)}) collective-permute-start(bf16[2,8,16,128]{3,2,1,0:T(8,128)(2,1)S(1)} %get-tuple-element.21), channel_id=1, source_target_pairs={{0,1},{1,0},{2,3},{3,2},{4,5},{5,4},{6,7},{7,6},{8,9},{9,8},{10,11... | collective-permute-start | bytes 196616 | tf_op jit(solution)/shard_map/ppermute | solution.py:465
  37.8 0.6 %copy-start.3 = (bf16[2,8,16,128]{3,2,1,0:T(8,128)(2,1)}, bf16[2,8,16,128]{3,2,1,0:T(8,128)(2,1)S(1)}, u32[]{:S(2)}) copy-start(bf16[2,8,16,128]{3,2,1,0:T(8,128)(2,1)S(1)} %collective-permute-done.6.b_ref) | copy-start | bytes 196612

commit v2 on v1

--- a/solution.py
+++ b/solution.py
@@ -418,6 +418,7 @@
             pltpu.VMEM((2, pairs + 2, 16, LANES), BF16),
             pltpu.VMEM((info * 16, LANES), F32),
         ],
+        compiler_params=pltpu.CompilerParams(vmem_limit_bytes=8 << 20),
         name="prep",
     )(wavefield, slowness, table_index, first)
     partner = [(i, i ^ 1) for i in range(lat)]
@@ -429,6 +430,7 @@
         out_shape=(tiles(near_n), tiles(far_n), tiles(far_n), tiles(4)),
         in_specs=[vmem] * 3,
         out_specs=(vmem,) * 4,
+        compiler_params=pltpu.CompilerParams(vmem_limit_bytes=4 << 20),
         name="unit",
     )(keep, send, got)
     a1 = lax.ppermute(near, "lat", matching(lat, 2, 0))
@@ -454,6 +456,7 @@
             pltpu.VMEM((STEPS, 80, LANES), F32),
             pltpu.VMEM((STEPS, 2, 16, 8, LANES), F32),
         ],
+        compiler_params=pltpu.CompilerParams(vmem_limit_bytes=32 << 20),
         name="steps",
     )(near, last, a1, b1, a2, b2, propagator_table[0], forward, inverse, frequency_scale)
     swapped = lax.ppermute(other, "lat", partner)
@@ -468,6 +471,7 @@
             out_shape=jax.ShapeDtypeStruct((STEPS, sources // 2, points), F32),
             in_specs=[vmem, vmem],
             out_specs=vmem,
+            compiler_params=pltpu.CompilerParams(vmem_limit_bytes=4 << 20),
             name="total",
         )(stay, come)
     low = jnp.where(core == 0, own, swapped)

time: 40.3 us -> 37.1 us (0.921)
  Pallas kernels: 17.5 us -> 11.4 us
  local copies, waits for them, and re-layouts: 1.93 us -> 6.7 us
  other arithmetic: 1.47 us -> 0.01 us
  waiting for transfers between devices: 8.26 us -> 7.59 us
    unnamed x12 -> x14, local copies, waits for them, and re-layouts: 1.93 us -> 6.7 us
    pallas_call x1, Pallas kernels: 12.4 us -> 9.87 us  [on_device(): pl.pallas_call(lambda *refs: main_kernel(lat // 2, *refs), out_shape=(ima...]
    pallas_call x1, Pallas kernels: 1.69 us -> 0.06 us  [on_device(): pl.pallas_call(unit_kernel, out_shape=(tiles(near_n), tiles(far_n), tiles...]
    select_n x1, other arithmetic: 1.47 us -> 0.01 us  [on_device(): leave = jnp.where(mine, swapped, own)]
    pallas_call x1, Pallas kernels: 1.93 us -> 0.84 us  [on_device(): pl.pallas_call(prep_kernel, out_shape=(tiles(pairs + 2), tiles(pairs + 2...]
    pallas_call x1, Pallas kernels: 1.53 us -> 0.66 us  [on_device(): pl.pallas_call(final_kernel, out_shape=jax.ShapeDtypeStruct((STEPS, sourc...]
where the time goes in v2:
time: 37.1 us; the launch traced here: 36.7 us
  Pallas kernels  11.4 us (31%)
  starting transfers between devices  10.3 us (28%)
  waiting for transfers between devices  7.59 us (20%)
  local copies, waits for them, and re-layouts  6.7 us (18%)
  between operations  0.71 us (2%)
    pallas_call x1, Pallas kernels, on_device(): pl.pallas_call(lambda *refs: main_kernel(lat // 2, *refs), out_shape=(ima...  9.87 us
    unnamed x14, local copies, waits for them, and re-layouts  6.7 us
    ppermute x1, starting transfers between devices, on_device(): b1 = lax.ppermute(near, 'lat', matching(lat, 2, 1))  4.4 us
    ppermute x1, starting transfers between devices, on_device(): b2 = lax.ppermute(far_b, 'lat', matching(lat, 4, 1))  3.05 us
    ppermute x1, waiting for transfers between devices, on_device(): come = lax.ppermute(leave, 'freq', [(0, 1), (1, 0)])  2.75 us
    ppermute x1, waiting for transfers between devices, on_device(): b2 = lax.ppermute(far_b, 'lat', matching(lat, 4, 1))  1.93 us
    ppermute x1, starting transfers between devices, on_device(): come = lax.ppermute(leave, 'freq', [(0, 1), (1, 0)])  1.58 us
    ppermute x1, waiting for transfers between devices, on_device(): got = lax.ppermute(send, 'lat', partner)  1.25 us
  transfers between devices with their start and end apart: 7, of which 5 were waited for; matrix products, arithmetic and copies ran while one was open for 0% of the time, Pallas kernels for 0%

profile of v2, /device:TPU:10, one launch (start us, length us, event | category | flops | bytes accessed | tf_op | source)
XLA Modules:
  0.0 36.7 jit_solution(5004829180365185121)
XLA Ops:
  0.0 0.0 copy-start.1
  0.0 0.9 %copy-done.1 = f32[4,1,8,2048]{3,2,1,0:T(8,128)S(1)} copy-done((f32[4,1,8,2048]{3,2,1,0:T(8,128)S(1)}, f32[4,1,8,2048]{3,2,1,0:T(8,128)}, u32[]{:S(2)}) %copy-start.1) | copy-done | bytes 262168
  1.0 0.0 copy-start.3
  1.0 0.9 %copy-done.3 = bf16[512,128]{1,0:T(8,128)(2,1)S(1)} copy-done((bf16[512,128]{1,0:T(8,128)(2,1)S(1)}, bf16[512,128]{1,0:T(8,128)(2,1)}, u32[]{:S(2)}) %copy-start.3) | copy-done | bytes 131096
  1.9 0.0 copy-start.5
  1.9 0.8 %copy-done.5 = f32[3,2048]{1,0:T(4,128)S(1)} copy-done((f32[3,2048]{1,0:T(4,128)S(1)}, f32[3,2048]{1,0:T(4,128)}, u32[]{:S(2)}) %copy-start.5) | copy-done | bytes 24600
  2.6 0.0 copy-start.6
  2.6 0.7 %copy-done.6 = s32[3,16]{1,0:T(4,128)S(1)} copy-done((s32[3,16]{1,0:T(4,128)S(1)}, s32[3,16]{1,0:T(4,128)}, u32[]{:S(2)}) %copy-start.6) | copy-done | bytes 216
  3.3 0.8 %prep.1 = (bf16[10,16,128]{2,1,0:T(8,128)(2,1)S(1)}, bf16[18,16,128]{2,1,0:T(8,128)(2,1)S(1)}) custom-call(f32[4,1,8,2048]{3,2,1,0:T(8,128)S(1)} %copy-done.1, f32[3,2048]{1,0:T(4,128)S(1)} %copy-done.5, s32[3,16]{1,0:T(4,128)S(1)} %copy-done.6, bf16[512,128]{1,0:T(8,128)(2,1)S(1)} %copy-done.3), custom_call_target="tpu_custom_call" | custom-call | tf_op jit(solution)/shard_map/prep/pallas_call | solution.py:412
  4.1 0.1 collective-permute-start
  4.2 1.3 %collective-permute-done.got_ref = bf16[18,16,128]{2,1,0:T(8,128)(2,1)S(1)} collective-permute-done((bf16[18,16,128]{2,1,0:T(8,128)(2,1)S(1)}, bf16[18,16,128]{2,1,0:T(8,128)(2,1)S(1)}, u32[]{:S(2)}, u32[]{:S(2)}) %collective-permute-start) | collective-permute-done | bytes 73760 | tf_op jit(solution)/shard_map/ppermute | solution.py:425
  5.5 0.1 unit.1
  5.5 0.6 %collective-permute-start.1 = (bf16[29,16,128]{2,1,0:T(8,128)(2,1)S(1)}, bf16[29,16,128]{2,1,0:T(8,128)(2,1)S(1)}, u32[]{:S(2)}, u32[]{:S(2)}) collective-permute-start(bf16[29,16,128]{2,1,0:T(8,128)(2,1)S(1)} %get-tuple-element.15.refs_0_), channel_id=1, source_target_pairs={{0,4},{2,6},{4,0},{6,2},{8,12},{10,14},{12,8},{14,10},{16,20},{18,... | collective-permute-start | bytes 356360 | tf_op jit(solution)/shard_map/ppermute | solution.py:436
  6.1 4.4 %collective-permute-start.2 = (bf16[29,16,128]{2,1,0:T(8,128)(2,1)S(1)}, bf16[29,16,128]{2,1,0:T(8,128)(2,1)S(1)}, u32[]{:S(2)}, u32[]{:S(2)}) collective-permute-start(bf16[29,16,128]{2,1,0:T(8,128)(2,1)S(1)} %get-tuple-element.15.refs_0_), channel_id=1, source_target_pairs={{0,0},{2,2},{4,8},{6,10},{8,4},{10,6},{12,16},{14,18},{16,12},{18,... | collective-permute-start | bytes 356360 | tf_op jit(solution)/shard_map/ppermute | solution.py:437
  10.5 0.5 %collective-permute-start.3 = (bf16[14,16,128]{2,1,0:T(8,128)(2,1)S(1)}, bf16[14,16,128]{2,1,0:T(8,128)(2,1)S(1)}, u32[]{:S(2)}, u32[]{:S(2)}) collective-permute-start(bf16[14,16,128]{2,1,0:T(8,128)(2,1)S(1)} %get-tuple-element.17), channel_id=1, source_target_pairs={{0,8},{2,10},{4,12},{6,14},{8,0},{10,2},{12,4},{14,6},{16,24},{18,... | collective-permute-start | bytes 172040 | tf_op jit(solution)/shard_map/ppermute | solution.py:438
  11.1 3.0 %collective-permute-start.4 = (bf16[14,16,128]{2,1,0:T(8,128)(2,1)S(1)}, bf16[14,16,128]{2,1,0:T(8,128)(2,1)S(1)}, u32[]{:S(2)}, u32[]{:S(2)}) collective-permute-start(bf16[14,16,128]{2,1,0:T(8,128)(2,1)S(1)} %get-tuple-element.18), channel_id=1, source_target_pairs={{0,0},{2,2},{4,4},{6,6},{8,16},{10,18},{12,20},{14,22},{16,8},{18,... | collective-permute-start | bytes 172040 | tf_op jit(solution)/shard_map/ppermute | solution.py:439
  14.8 0.4 %collective-permute-done.3.refs_4_ = bf16[14,16,128]{2,1,0:T(8,128)(2,1)S(1)} collective-permute-done((bf16[14,16,128]{2,1,0:T(8,128)(2,1)S(1)}, bf16[14,16,128]{2,1,0:T(8,128)(2,1)S(1)}, u32[]{:S(2)}, u32[]{:S(2)}) %collective-permute-start.3) | collective-permute-done | bytes 57376 | tf_op jit(solution)/shard_map/ppermute | solution.py:438
  15.2 1.9 %collective-permute-done.4.refs_5_ = bf16[14,16,128]{2,1,0:T(8,128)(2,1)S(1)} collective-permute-done((bf16[14,16,128]{2,1,0:T(8,128)(2,1)S(1)}, bf16[14,16,128]{2,1,0:T(8,128)(2,1)S(1)}, u32[]{:S(2)}, u32[]{:S(2)}) %collective-permute-start.4) | collective-permute-done | bytes 57376 | tf_op jit(solution)/shard_map/ppermute | solution.py:439
  17.1 0.0 collective-permute-done.1.refs_2_
  17.1 0.0 collective-permute-done.2.refs_3_
  17.1 0.0 copy-start
  17.1 1.6 %copy-done = bf16[1,4,2112,128]{3,2,1,0:T(8,128)(2,1)S(1)} copy-done((bf16[1,4,2112,128]{3,2,1,0:T(8,128)(2,1)S(1)}, bf16[1,4,2112,128]{3,2,1,0:T(8,128)(2,1)}, u32[]{:S(2)}) %copy-start) | copy-done | bytes 2162712
  18.7 0.0 copy-start.2
  18.7 0.9 %copy-done.2 = bf16[256,256]{1,0:T(8,128)(2,1)S(1)} copy-done((bf16[256,256]{1,0:T(8,128)(2,1)S(1)}, bf16[256,256]{1,0:T(8,128)(2,1)}, u32[]{:S(2)}) %copy-start.2) | copy-done | bytes 131096
  19.6 0.0 copy-start.4
  19.6 0.9 %copy-done.4 = bf16[384,128]{1,0:T(8,128)(2,1)S(1)} copy-done((bf16[384,128]{1,0:T(8,128)(2,1)S(1)}, bf16[384,128]{1,0:T(8,128)(2,1)}, u32[]{:S(2)}) %copy-start.4) | copy-done | bytes 98328
  20.5 9.9 %steps.1 = (bf16[2,8,16,128]{3,2,1,0:T(8,128)(2,1)S(1)}, bf16[2,8,16,128]{3,2,1,0:T(8,128)(2,1)S(1)}) custom-call(bf16[29,16,128]{2,1,0:T(8,128)(2,1)S(1)} %get-tuple-element.15.refs_0_, bf16[4,16,128]{2,1,0:T(8,128)(2,1)S(1)} %get-tuple-element.16.refs_1_, bf16[29,16,128]{2,1,0:T(8,128)(2,1)S(1)} %collective-permute-done.1.refs_2_, ...), custom_call_target="tpu_custom_call" | custom-call | tf_op jit(solution)/shard_map/steps/pallas_call | solution.py:441
  30.4 0.1 collective-permute-start.5
  30.5 1.2 %collective-permute-done.5 = bf16[2,8,16,128]{3,2,1,0:T(8,128)(2,1)S(1)} collective-permute-done((bf16[2,8,16,128]{3,2,1,0:T(8,128)(2,1)S(1)}, bf16[2,8,16,128]{3,2,1,0:T(8,128)(2,1)S(1)}, u32[]{:S(2)}, u32[]{:S(2)}) %collective-permute-start.5) | collective-permute-done | bytes 65568 | tf_op jit(solution)/shard_map/ppermute | solution.py:462
  31.7 1.6 %collective-permute-start.6 = (bf16[2,8,16,128]{3,2,1,0:T(8,128)(2,1)S(1)}, bf16[2,8,16,128]{3,2,1,0:T(8,128)(2,1)S(1)}, u32[]{:S(2)}, u32[]{:S(2)}) collective-permute-start(bf16[2,8,16,128]{3,2,1,0:T(8,128)(2,1)S(1)} %get-tuple-element.21), channel_id=1, source_target_pairs={{0,1},{1,0},{2,3},{3,2},{4,5},{5,4},{6,7},{7,6},{8,9},{9,8},{10,11... | collective-permute-start | bytes 196616 | tf_op jit(solution)/shard_map/ppermute | solution.py:468
  33.3 2.7 %collective-permute-done.6.b_ref = bf16[2,8,16,128]{3,2,1,0:T(8,128)(2,1)S(1)} collective-permute-done((bf16[2,8,16,128]{3,2,1,0:T(8,128)(2,1)S(1)}, bf16[2,8,16,128]{3,2,1,0:T(8,128)(2,1)S(1)}, u32[]{:S(2)}, u32[]{:S(2)}) %collective-permute-start.6) | collective-permute-done | bytes 65568 | tf_op jit(solution)/shard_map/ppermute | solution.py:468
  36.1 0.7 %total.1 = f32[3,4,2048]{2,1,0:T(4,128)} custom-call(bf16[2,8,16,128]{3,2,1,0:T(8,128)(2,1)S(1)} %get-tuple-element.22.a_ref, bf16[2,8,16,128]{3,2,1,0:T(8,128)(2,1)S(1)} %collective-permute-done.6.b_ref), custom_call_target="tpu_custom_call" | custom-call | tf_op jit(solution)/shard_map/total/pallas_call | solution.py:469
  (1 shorter events, 0.0 us)
Async XLA Ops:
  0.0 0.9 %copy-start.1 = (f32[4,1,8,2048]{3,2,1,0:T(8,128)S(1)}, f32[4,1,8,2048]{3,2,1,0:T(8,128)}, u32[]{:S(2)}) copy-start(f32[4,1,8,2048]{3,2,1,0:T(8,128)} %wave_ref.1) | copy-start | bytes 786436
  1.0 0.9 %copy-start.3 = (bf16[512,128]{1,0:T(8,128)(2,1)S(1)}, bf16[512,128]{1,0:T(8,128)(2,1)}, u32[]{:S(2)}) copy-start(bf16[512,128]{1,0:T(8,128)(2,1)} %constant.19.clone.first_ref) | copy-start | bytes 393220
  1.9 0.8 %copy-start.5 = (f32[3,2048]{1,0:T(4,128)S(1)}, f32[3,2048]{1,0:T(4,128)}, u32[]{:S(2)}) copy-start(f32[3,2048]{1,0:T(4,128)} %slow_ref.1) | copy-start | bytes 73732
  2.6 0.7 %copy-start.6 = (s32[3,16]{1,0:T(4,128)S(1)}, s32[3,16]{1,0:T(4,128)}, u32[]{:S(2)}) copy-start(s32[3,16]{1,0:T(4,128)} %index_ref.1) | copy-start | bytes 580
  4.1 1.3 %collective-permute-start = (bf16[18,16,128]{2,1,0:T(8,128)(2,1)S(1)}, bf16[18,16,128]{2,1,0:T(8,128)(2,1)S(1)}, u32[]{:S(2)}, u32[]{:S(2)}) collective-permute-start(bf16[18,16,128]{2,1,0:T(8,128)(2,1)S(1)} %get-tuple-element.14.sent_ref), channel_id=1, source_target_pairs={{0,2},{2,0},{4,6},{6,4},{8,10},{10,8},{12,14},{14,12},{16,18},{18,... | collective-permute-start | bytes 221192 | tf_op jit(solution)/shard_map/ppermute | solution.py:425
  5.5 11.6 %collective-permute-start.1 = (bf16[29,16,128]{2,1,0:T(8,128)(2,1)S(1)}, bf16[29,16,128]{2,1,0:T(8,128)(2,1)S(1)}, u32[]{:S(2)}, u32[]{:S(2)}) collective-permute-start(bf16[29,16,128]{2,1,0:T(8,128)(2,1)S(1)} %get-tuple-element.15.refs_0_), channel_id=1, source_target_pairs={{0,4},{2,6},{4,0},{6,2},{8,12},{10,14},{12,8},{14,10},{16,20},{18,... | collective-permute-start | bytes 356360 | tf_op jit(solution)/shard_map/ppermute | solution.py:436
  6.1 11.0 %collective-permute-start.2 = (bf16[29,16,128]{2,1,0:T(8,128)(2,1)S(1)}, bf16[29,16,128]{2,1,0:T(8,128)(2,1)S(1)}, u32[]{:S(2)}, u32[]{:S(2)}) collective-permute-start(bf16[29,16,128]{2,1,0:T(8,128)(2,1)S(1)} %get-tuple-element.15.refs_0_), channel_id=1, source_target_pairs={{0,0},{2,2},{4,8},{6,10},{8,4},{10,6},{12,16},{14,18},{16,12},{18,... | collective-permute-start | bytes 356360 | tf_op jit(solution)/shard_map/ppermute | solution.py:437
  10.5 4.6 %collective-permute-start.3 = (bf16[14,16,128]{2,1,0:T(8,128)(2,1)S(1)}, bf16[14,16,128]{2,1,0:T(8,128)(2,1)S(1)}, u32[]{:S(2)}, u32[]{:S(2)}) collective-permute-start(bf16[14,16,128]{2,1,0:T(8,128)(2,1)S(1)} %get-tuple-element.17), channel_id=1, source_target_pairs={{0,8},{2,10},{4,12},{6,14},{8,0},{10,2},{12,4},{14,6},{16,24},{18,... | collective-permute-start | bytes 172040 | tf_op jit(solution)/shard_map/ppermute | solution.py:438
  11.1 6.1 %collective-permute-start.4 = (bf16[14,16,128]{2,1,0:T(8,128)(2,1)S(1)}, bf16[14,16,128]{2,1,0:T(8,128)(2,1)S(1)}, u32[]{:S(2)}, u32[]{:S(2)}) collective-permute-start(bf16[14,16,128]{2,1,0:T(8,128)(2,1)S(1)} %get-tuple-element.18), channel_id=1, source_target_pairs={{0,0},{2,2},{4,4},{6,6},{8,16},{10,18},{12,20},{14,22},{16,8},{18,... | collective-permute-start | bytes 172040 | tf_op jit(solution)/shard_map/ppermute | solution.py:439
  17.1 1.6 %copy-start = (bf16[1,4,2112,128]{3,2,1,0:T(8,128)(2,1)S(1)}, bf16[1,4,2112,128]{3,2,1,0:T(8,128)(2,1)}, u32[]{:S(2)}) copy-start(bf16[1,4,2112,128]{3,2,1,0:T(8,128)(2,1)} %param.9) | copy-start | bytes 6488068
  18.7 0.9 %copy-start.2 = (bf16[256,256]{1,0:T(8,128)(2,1)S(1)}, bf16[256,256]{1,0:T(8,128)(2,1)}, u32[]{:S(2)}) copy-start(bf16[256,256]{1,0:T(8,128)(2,1)} %constant.21.clone.refs_8_) | copy-start | bytes 393220
  19.6 0.9 %copy-start.4 = (bf16[384,128]{1,0:T(8,128)(2,1)S(1)}, bf16[384,128]{1,0:T(8,128)(2,1)}, u32[]{:S(2)}) copy-start(bf16[384,128]{1,0:T(8,128)(2,1)} %constant.20.clone.refs_7_) | copy-start | bytes 294916
  30.4 1.3 %collective-permute-start.5 = (bf16[2,8,16,128]{3,2,1,0:T(8,128)(2,1)S(1)}, bf16[2,8,16,128]{3,2,1,0:T(8,128)(2,1)S(1)}, u32[]{:S(2)}, u32[]{:S(2)}) collective-permute-start(bf16[2,8,16,128]{3,2,1,0:T(8,128)(2,1)S(1)} %get-tuple-element.20), channel_id=1, source_target_pairs={{0,2},{2,0},{4,6},{6,4},{8,10},{10,8},{12,14},{14,12},{16,18},{18,... | collective-permute-start | bytes 196616 | tf_op jit(solution)/shard_map/ppermute | solution.py:462
  31.7 4.3 %collective-permute-start.6 = (bf16[2,8,16,128]{3,2,1,0:T(8,128)(2,1)S(1)}, bf16[2,8,16,128]{3,2,1,0:T(8,128)(2,1)S(1)}, u32[]{:S(2)}, u32[]{:S(2)}) collective-permute-start(bf16[2,8,16,128]{3,2,1,0:T(8,128)(2,1)S(1)} %get-tuple-element.21), channel_id=1, source_target_pairs={{0,1},{1,0},{2,3},{3,2},{4,5},{5,4},{6,7},{7,6},{8,9},{9,8},{10,11... | collective-permute-start | bytes 196616 | tf_op jit(solution)/shard_map/ppermute | solution.py:468

commit v3 on v2

--- a/solution.py
+++ b/solution.py
@@ -78,10 +78,59 @@
     return lax.broadcasted_iota(jnp.int32, shape, len(shape) - 1) < LANES // 2
 
 
-def prep_kernel(wave_ref, slow_ref, index_ref, first_ref, keep_ref, send_ref, both_ref, rows_ref):
+def prep_kernel(
+    wave_hbm,
+    slow_hbm,
+    index_hbm,
+    first_hbm,
+    keep_ref,
+    send_ref,
+    wave_ref,
+    slow_ref,
+    index_ref,
+    first_ref,
+    both_ref,
+    rows_ref,
+    sems,
+):
+    copies = [
+        pltpu.make_async_copy(source, target, sems.at[i])
+        for i, (source, target) in enumerate(
+            (
+                (wave_hbm, wave_ref),
+                (first_hbm, first_ref),
+                (slow_hbm, slow_ref),
+                (index_hbm, index_ref),
+            )
+        )
+    ]
+    for copy in copies:
+        copy.start()
     core = lax.rem(lax.axis_index("lat"), 2)
+    copies[2].wait()
+    copies[3].wait()
     blocks = wave_ref.shape[-1] // WINDOW
     pairs = blocks // 2
+    slow = slow_ref[...]
+    high = slow.astype(BF16).astype(F32)
+    rest = slow - high
+    lanes = low_lanes((1, LANES))
+    rows_ref[...] = jnp.zeros(rows_ref.shape, F32)
+    for n in range(STEPS):
+        for g in range(blocks):
+            cut = slice(WINDOW * g, WINDOW * (g + 1))
+            rows_ref[(2 * n) * blocks + g : (2 * n) * blocks + g + 1, :] = high[n : n + 1, cut]
+            rows_ref[(2 * n + 1) * blocks + g : (2 * n + 1) * blocks + g + 1, :] = rest[n : n + 1, cut]
+        for q in range(pairs):
+            at = 2 * STEPS * blocks + n * pairs + q
+            rows_ref[at : at + 1, :] = jnp.where(
+                lanes,
+                jnp.full((1, LANES), index_ref[n, 2 * q], jnp.int32),
+                jnp.full((1, LANES), index_ref[n, 2 * q + 1], jnp.int32),
+            ).astype(F32)
+    send_ref[pairs + 2 :] = rows_ref[...].reshape(-1, 16, LANES).astype(BF16)
+    copies[0].wait()
+    copies[1].wait()
     upper = lax.broadcasted_iota(jnp.int32, (8, wave_ref.shape[-1]), 0) < 4
     for side in range(2):
         halves = []
@@ -106,24 +155,6 @@
         both_ref[side] = coefs.reshape(pairs + 2, 16, LANES).astype(BF16)
     keep_ref[...] = both_ref[core]
     send_ref[0 : pairs + 2] = both_ref[1 - core]
-    slow = slow_ref[...]
-    high = slow.astype(BF16).astype(F32)
-    rest = slow - high
-    lanes = low_lanes((1, LANES))
-    rows_ref[...] = jnp.zeros(rows_ref.shape, F32)
-    for n in range(STEPS):
-        for g in range(blocks):
-            cut = slice(WINDOW * g, WINDOW * (g + 1))
-            rows_ref[(2 * n) * blocks + g : (2 * n) * blocks + g + 1, :] = high[n : n + 1, cut]
-            rows_ref[(2 * n + 1) * blocks + g : (2 * n + 1) * blocks + g + 1, :] = rest[n : n + 1, cut]
-        for q in range(pairs):
-            at = 2 * STEPS * blocks + n * pairs + q
-            rows_ref[at : at + 1, :] = jnp.where(
-                lanes,
-                jnp.full((1, LANES), index_ref[n, 2 * q], jnp.int32),
-                jnp.full((1, LANES), index_ref[n, 2 * q + 1], jnp.int32),
-            ).astype(F32)
-    send_ref[pairs + 2 :] = rows_ref[...].reshape(-1, 16, LANES).astype(BF16)
 
 
 def unit_kernel(keep_ref, sent_ref, got_ref, near_ref, far_a_ref, far_b_ref, last_ref):
@@ -404,6 +435,7 @@
     first, forward, inverse = (jnp.asarray(m, BF16) for m in pair_matrices())
     vmem = pl.BlockSpec(memory_space=pltpu.VMEM)
     smem = pl.BlockSpec(memory_space=pltpu.SMEM)
+    hbm = pl.BlockSpec(memory_space=pltpu.HBM)
 
     def tiles(n):
         return jax.ShapeDtypeStruct((n, 16, LANES), BF16)
@@ -412,15 +444,26 @@
     keep, send = pl.pallas_call(
         prep_kernel,
         out_shape=(tiles(pairs + 2), tiles(pairs + 2 + info)),
-        in_specs=[vmem, vmem, smem, vmem],
+        in_specs=[hbm] * 4,
         out_specs=(vmem, vmem),
         scratch_shapes=[
+            pltpu.VMEM(wavefield.shape, F32),
+            pltpu.VMEM(slowness.shape, F32),
+            pltpu.SMEM(table_index.shape, jnp.int32),
+            pltpu.VMEM(first.shape, BF16),
             pltpu.VMEM((2, pairs + 2, 16, LANES), BF16),
             pltpu.VMEM((info * 16, LANES), F32),
+            pltpu.SemaphoreType.DMA((4,)),
         ],
         compiler_params=pltpu.CompilerParams(vmem_limit_bytes=8 << 20),
+        cost_estimate=pl.CostEstimate(flops=10**9, bytes_accessed=10**7, transcendentals=0),
         name="prep",
-    )(wavefield, slowness, table_index, first)
+    )(
+        *(
+            pltpu.with_memory_space_constraint(x, pltpu.HBM)
+            for x in (wavefield, slowness, table_index, first)
+        )
+    )
     partner = [(i, i ^ 1) for i in range(lat)]
     got = lax.ppermute(send, "lat", partner)
     near_n = 2 * (pairs + 2) - 2 + 8 + STEPS

time: 37.1 us -> 30.8 us (0.83)
  local copies, waits for them, and re-layouts: 6.7 us -> 0.01 us
  Pallas kernels: 11.4 us -> 12 us
    unnamed x14 -> x6, local copies, waits for them, and re-layouts: 6.7 us -> 0.01 us
    pallas_call x1, Pallas kernels: 0.84 us -> 1.43 us  [on_device(): pl.pallas_call(prep_kernel, out_shape=(tiles(pairs + 2), tiles(pairs + 2...]
where the time goes in v3:
time: 30.8 us; the launch traced here: 30.7 us
  Pallas kernels  12 us (39%)
  starting transfers between devices  10.3 us (33%)
  waiting for transfers between devices  7.6 us (25%)
  between operations  0.74 us (2%)
    pallas_call x1, Pallas kernels, on_device(): pl.pallas_call(lambda *refs: main_kernel(lat // 2, *refs), out_shape=(ima...  9.87 us
    ppermute x1, starting transfers between devices, on_device(): b1 = lax.ppermute(near, 'lat', matching(lat, 2, 1))  4.4 us
    ppermute x1, starting transfers between devices, on_device(): b2 = lax.ppermute(far_b, 'lat', matching(lat, 4, 1))  3.05 us
    ppermute x1, waiting for transfers between devices, on_device(): come = lax.ppermute(leave, 'freq', [(0, 1), (1, 0)])  2.75 us
    ppermute x1, waiting for transfers between devices, on_device(): b2 = lax.ppermute(far_b, 'lat', matching(lat, 4, 1))  1.93 us
    ppermute x1, starting transfers between devices, on_device(): come = lax.ppermute(leave, 'freq', [(0, 1), (1, 0)])  1.58 us
    pallas_call x1, Pallas kernels, on_device(): pl.pallas_call(prep_kernel, out_shape=(tiles(pairs + 2), tiles(pairs + 2...  1.43 us
    ppermute x1, waiting for transfers between devices, on_device(): got = lax.ppermute(send, 'lat', partner)  1.25 us
  transfers between devices with their start and end apart: 7, of which 5 were waited for; matrix products, arithmetic and copies ran while one was open for 0% of the time, Pallas kernels for 0%

profile of v3, /device:TPU:10, one launch (start us, length us, event | category | flops | bytes accessed | tf_op | source)
XLA Modules:
  0.0 30.7 jit_solution(1075757650228372877)
XLA Ops:
  0.0 0.0 copy-start.2
  0.0 0.0 copy-start.1
  0.0 0.0 copy-start
  0.0 1.4 %prep.1 = (bf16[10,16,128]{2,1,0:T(8,128)(2,1)S(1)}, bf16[18,16,128]{2,1,0:T(8,128)(2,1)S(1)}) custom-call(f32[4,1,8,2048]{3,2,1,0:T(8,128)} %wave_hbm.1, f32[3,2048]{1,0:T(4,128)} %slow_hbm.1, s32[3,16]{1,0:T(4,128)} %index_hbm.1, bf16[512,128]{1,0:T(8,128)(2,1)} %constant.19.clone.first_hbm), custom_call_target="tpu_custom_call" | custom-call | flops 1000000000 | bytes 10000000 | tf_op jit(solution)/shard_map/prep/pallas_call | solution.py:444
  1.5 0.1 collective-permute-start
  1.5 1.3 %collective-permute-done.got_ref = bf16[18,16,128]{2,1,0:T(8,128)(2,1)S(1)} collective-permute-done((bf16[18,16,128]{2,1,0:T(8,128)(2,1)S(1)}, bf16[18,16,128]{2,1,0:T(8,128)(2,1)S(1)}, u32[]{:S(2)}, u32[]{:S(2)}) %collective-permute-start) | collective-permute-done | bytes 73760 | tf_op jit(solution)/shard_map/ppermute | solution.py:468
  2.8 0.1 unit.1
  2.8 0.6 %collective-permute-start.1 = (bf16[29,16,128]{2,1,0:T(8,128)(2,1)S(1)}, bf16[29,16,128]{2,1,0:T(8,128)(2,1)S(1)}, u32[]{:S(2)}, u32[]{:S(2)}) collective-permute-start(bf16[29,16,128]{2,1,0:T(8,128)(2,1)S(1)} %get-tuple-element.15.refs_0_), channel_id=1, source_target_pairs={{0,4},{2,6},{4,0},{6,2},{8,12},{10,14},{12,8},{14,10},{16,20},{18,... | collective-permute-start | bytes 356360 | tf_op jit(solution)/shard_map/ppermute | solution.py:479
  3.4 4.4 %collective-permute-start.2 = (bf16[29,16,128]{2,1,0:T(8,128)(2,1)S(1)}, bf16[29,16,128]{2,1,0:T(8,128)(2,1)S(1)}, u32[]{:S(2)}, u32[]{:S(2)}) collective-permute-start(bf16[29,16,128]{2,1,0:T(8,128)(2,1)S(1)} %get-tuple-element.15.refs_0_), channel_id=1, source_target_pairs={{0,0},{2,2},{4,8},{6,10},{8,4},{10,6},{12,16},{14,18},{16,12},{18,... | collective-permute-start | bytes 356360 | tf_op jit(solution)/shard_map/ppermute | solution.py:480
  7.8 0.5 %collective-permute-start.3 = (bf16[14,16,128]{2,1,0:T(8,128)(2,1)S(1)}, bf16[14,16,128]{2,1,0:T(8,128)(2,1)S(1)}, u32[]{:S(2)}, u32[]{:S(2)}) collective-permute-start(bf16[14,16,128]{2,1,0:T(8,128)(2,1)S(1)} %get-tuple-element.17), channel_id=1, source_target_pairs={{0,8},{2,10},{4,12},{6,14},{8,0},{10,2},{12,4},{14,6},{16,24},{18,... | collective-permute-start | bytes 172040 | tf_op jit(solution)/shard_map/ppermute | solution.py:481
  8.4 3.0 %collective-permute-start.4 = (bf16[14,16,128]{2,1,0:T(8,128)(2,1)S(1)}, bf16[14,16,128]{2,1,0:T(8,128)(2,1)S(1)}, u32[]{:S(2)}, u32[]{:S(2)}) collective-permute-start(bf16[14,16,128]{2,1,0:T(8,128)(2,1)S(1)} %get-tuple-element.18), channel_id=1, source_target_pairs={{0,0},{2,2},{4,4},{6,6},{8,16},{10,18},{12,20},{14,22},{16,8},{18,... | collective-permute-start | bytes 172040 | tf_op jit(solution)/shard_map/ppermute | solution.py:482
  12.1 0.4 %collective-permute-done.3.refs_4_ = bf16[14,16,128]{2,1,0:T(8,128)(2,1)S(1)} collective-permute-done((bf16[14,16,128]{2,1,0:T(8,128)(2,1)S(1)}, bf16[14,16,128]{2,1,0:T(8,128)(2,1)S(1)}, u32[]{:S(2)}, u32[]{:S(2)}) %collective-permute-start.3) | collective-permute-done | bytes 57376 | tf_op jit(solution)/shard_map/ppermute | solution.py:481
  12.5 1.9 %collective-permute-done.4.refs_5_ = bf16[14,16,128]{2,1,0:T(8,128)(2,1)S(1)} collective-permute-done((bf16[14,16,128]{2,1,0:T(8,128)(2,1)S(1)}, bf16[14,16,128]{2,1,0:T(8,128)(2,1)S(1)}, u32[]{:S(2)}, u32[]{:S(2)}) %collective-permute-start.4) | collective-permute-done | bytes 57376 | tf_op jit(solution)/shard_map/ppermute | solution.py:482
  14.4 0.0 collective-permute-done.1.refs_2_
  14.4 0.0 collective-permute-done.2.refs_3_
  14.4 0.0 copy-done.2
  14.4 0.0 copy-done.1
  14.4 0.0 copy-done
  14.5 9.9 %steps.1 = (bf16[2,8,16,128]{3,2,1,0:T(8,128)(2,1)S(1)}, bf16[2,8,16,128]{3,2,1,0:T(8,128)(2,1)S(1)}) custom-call(bf16[29,16,128]{2,1,0:T(8,128)(2,1)S(1)} %get-tuple-element.15.refs_0_, bf16[4,16,128]{2,1,0:T(8,128)(2,1)S(1)} %get-tuple-element.16.refs_1_, bf16[29,16,128]{2,1,0:T(8,128)(2,1)S(1)} %collective-permute-done.1.refs_2_, ...), custom_call_target="tpu_custom_call" | custom-call | tf_op jit(solution)/shard_map/steps/pallas_call | solution.py:484
  24.3 0.1 collective-permute-start.5
  24.4 1.2 %collective-permute-done.5 = bf16[2,8,16,128]{3,2,1,0:T(8,128)(2,1)S(1)} collective-permute-done((bf16[2,8,16,128]{3,2,1,0:T(8,128)(2,1)S(1)}, bf16[2,8,16,128]{3,2,1,0:T(8,128)(2,1)S(1)}, u32[]{:S(2)}, u32[]{:S(2)}) %collective-permute-start.5) | collective-permute-done | bytes 65568 | tf_op jit(solution)/shard_map/ppermute | solution.py:505
  25.7 1.6 %collective-permute-start.6 = (bf16[2,8,16,128]{3,2,1,0:T(8,128)(2,1)S(1)}, bf16[2,8,16,128]{3,2,1,0:T(8,128)(2,1)S(1)}, u32[]{:S(2)}, u32[]{:S(2)}) collective-permute-start(bf16[2,8,16,128]{3,2,1,0:T(8,128)(2,1)S(1)} %get-tuple-element.21), channel_id=1, source_target_pairs={{0,1},{1,0},{2,3},{3,2},{4,5},{5,4},{6,7},{7,6},{8,9},{9,8},{10,11... | collective-permute-start | bytes 196616 | tf_op jit(solution)/shard_map/ppermute | solution.py:511
  27.3 2.7 %collective-permute-done.6.b_ref = bf16[2,8,16,128]{3,2,1,0:T(8,128)(2,1)S(1)} collective-permute-done((bf16[2,8,16,128]{3,2,1,0:T(8,128)(2,1)S(1)}, bf16[2,8,16,128]{3,2,1,0:T(8,128)(2,1)S(1)}, u32[]{:S(2)}, u32[]{:S(2)}) %collective-permute-start.6) | collective-permute-done | bytes 65568 | tf_op jit(solution)/shard_map/ppermute | solution.py:511
  30.0 0.7 %total.1 = f32[3,4,2048]{2,1,0:T(4,128)} custom-call(bf16[2,8,16,128]{3,2,1,0:T(8,128)(2,1)S(1)} %get-tuple-element.22.a_ref, bf16[2,8,16,128]{3,2,1,0:T(8,128)(2,1)S(1)} %collective-permute-done.6.b_ref), custom_call_target="tpu_custom_call" | custom-call | tf_op jit(solution)/shard_map/total/pallas_call | solution.py:512
  (1 shorter events, 0.0 us)
Async XLA Ops:
  0.0 14.4 %copy-start.2 = (bf16[384,128]{1,0:T(8,128)(2,1)S(1)}, bf16[384,128]{1,0:T(8,128)(2,1)}, u32[]{:S(2)}) copy-start(bf16[384,128]{1,0:T(8,128)(2,1)} %constant.20.clone.refs_7_) | copy-start | bytes 294916
  0.0 14.4 %copy-start.1 = (bf16[256,256]{1,0:T(8,128)(2,1)S(1)}, bf16[256,256]{1,0:T(8,128)(2,1)}, u32[]{:S(2)}) copy-start(bf16[256,256]{1,0:T(8,128)(2,1)} %constant.21.clone.refs_8_) | copy-start | bytes 393220
  0.0 14.4 %copy-start = (bf16[1,4,2112,128]{3,2,1,0:T(8,128)(2,1)S(1)}, bf16[1,4,2112,128]{3,2,1,0:T(8,128)(2,1)}, u32[]{:S(2)}) copy-start(bf16[1,4,2112,128]{3,2,1,0:T(8,128)(2,1)} %param.9) | copy-start | bytes 6488068
  1.5 1.3 %collective-permute-start = (bf16[18,16,128]{2,1,0:T(8,128)(2,1)S(1)}, bf16[18,16,128]{2,1,0:T(8,128)(2,1)S(1)}, u32[]{:S(2)}, u32[]{:S(2)}) collective-permute-start(bf16[18,16,128]{2,1,0:T(8,128)(2,1)S(1)} %get-tuple-element.14.sent_ref), channel_id=1, source_target_pairs={{0,2},{2,0},{4,6},{6,4},{8,10},{10,8},{12,14},{14,12},{16,18},{18,... | collective-permute-start | bytes 221192 | tf_op jit(solution)/shard_map/ppermute | solution.py:468
  2.8 11.6 %collective-permute-start.1 = (bf16[29,16,128]{2,1,0:T(8,128)(2,1)S(1)}, bf16[29,16,128]{2,1,0:T(8,128)(2,1)S(1)}, u32[]{:S(2)}, u32[]{:S(2)}) collective-permute-start(bf16[29,16,128]{2,1,0:T(8,128)(2,1)S(1)} %get-tuple-element.15.refs_0_), channel_id=1, source_target_pairs={{0,4},{2,6},{4,0},{6,2},{8,12},{10,14},{12,8},{14,10},{16,20},{18,... | collective-permute-start | bytes 356360 | tf_op jit(solution)/shard_map/ppermute | solution.py:479
  3.4 11.0 %collective-permute-start.2 = (bf16[29,16,128]{2,1,0:T(8,128)(2,1)S(1)}, bf16[29,16,128]{2,1,0:T(8,128)(2,1)S(1)}, u32[]{:S(2)}, u32[]{:S(2)}) collective-permute-start(bf16[29,16,128]{2,1,0:T(8,128)(2,1)S(1)} %get-tuple-element.15.refs_0_), channel_id=1, source_target_pairs={{0,0},{2,2},{4,8},{6,10},{8,4},{10,6},{12,16},{14,18},{16,12},{18,... | collective-permute-start | bytes 356360 | tf_op jit(solution)/shard_map/ppermute | solution.py:480
  7.8 4.6 %collective-permute-start.3 = (bf16[14,16,128]{2,1,0:T(8,128)(2,1)S(1)}, bf16[14,16,128]{2,1,0:T(8,128)(2,1)S(1)}, u32[]{:S(2)}, u32[]{:S(2)}) collective-permute-start(bf16[14,16,128]{2,1,0:T(8,128)(2,1)S(1)} %get-tuple-element.17), channel_id=1, source_target_pairs={{0,8},{2,10},{4,12},{6,14},{8,0},{10,2},{12,4},{14,6},{16,24},{18,... | collective-permute-start | bytes 172040 | tf_op jit(solution)/shard_map/ppermute | solution.py:481
  8.4 6.1 %collective-permute-start.4 = (bf16[14,16,128]{2,1,0:T(8,128)(2,1)S(1)}, bf16[14,16,128]{2,1,0:T(8,128)(2,1)S(1)}, u32[]{:S(2)}, u32[]{:S(2)}) collective-permute-start(bf16[14,16,128]{2,1,0:T(8,128)(2,1)S(1)} %get-tuple-element.18), channel_id=1, source_target_pairs={{0,0},{2,2},{4,4},{6,6},{8,16},{10,18},{12,20},{14,22},{16,8},{18,... | collective-permute-start | bytes 172040 | tf_op jit(solution)/shard_map/ppermute | solution.py:482
  24.3 1.3 %collective-permute-start.5 = (bf16[2,8,16,128]{3,2,1,0:T(8,128)(2,1)S(1)}, bf16[2,8,16,128]{3,2,1,0:T(8,128)(2,1)S(1)}, u32[]{:S(2)}, u32[]{:S(2)}) collective-permute-start(bf16[2,8,16,128]{3,2,1,0:T(8,128)(2,1)S(1)} %get-tuple-element.20), channel_id=1, source_target_pairs={{0,2},{2,0},{4,6},{6,4},{8,10},{10,8},{12,14},{14,12},{16,18},{18,... | collective-permute-start | bytes 196616 | tf_op jit(solution)/shard_map/ppermute | solution.py:505
  25.7 4.3 %collective-permute-start.6 = (bf16[2,8,16,128]{3,2,1,0:T(8,128)(2,1)S(1)}, bf16[2,8,16,128]{3,2,1,0:T(8,128)(2,1)S(1)}, u32[]{:S(2)}, u32[]{:S(2)}) collective-permute-start(bf16[2,8,16,128]{3,2,1,0:T(8,128)(2,1)S(1)} %get-tuple-element.21), channel_id=1, source_target_pairs={{0,1},{1,0},{2,3},{3,2},{4,5},{5,4},{6,7},{7,6},{8,9},{9,8},{10,11... | collective-permute-start | bytes 196616 | tf_op jit(solution)/shard_map/ppermute | solution.py:511

commit v4 on v3

--- a/solution.py
+++ b/solution.py
@@ -157,7 +157,7 @@
     send_ref[0 : pairs + 2] = both_ref[1 - core]
 
 
-def unit_kernel(keep_ref, sent_ref, got_ref, near_ref, far_a_ref, far_b_ref, last_ref):
+def unit_kernel(keep_ref, sent_ref, got_ref, scale_ref, near_ref, far_a_ref, far_b_ref, last_ref):
     place = lax.axis_index("lat")
     second = lax.rem(place, 2) == 1
     n = keep_ref.shape[0]
@@ -170,17 +170,18 @@
     unit = jnp.concatenate([b0[: n - 2], b0[n - 2 :] + b1[:2], b1[2:]], axis=0)
     near_ref[0 : 2 * n - 2] = unit.astype(BF16)
     at = 2 * n - 2
-    for step in range(2):
-        for part in range(2):
-            near_ref[at] = i0[2 * step + part].astype(BF16)
-            near_ref[at + 1] = i1[2 * step + part].astype(BF16)
-            at += 2
+    for step in range(STEPS):
+        ref, to = (near_ref, at) if step < 2 else (last_ref, 0)
+        for block, info in enumerate((i0, i1)):
+            theta = scale_ref[0] * (info[2 * step] + info[2 * step + 1])
+            high = theta.astype(BF16)
+            ref[to + block] = high
+            ref[to + 2 + block] = (theta - high.astype(F32)).astype(BF16)
+        if step < 2:
+            at += 4
     near_ref[at] = jnp.concatenate([i0[6, :8], i1[6, :8]], axis=0).astype(BF16)
     near_ref[at + 1] = jnp.concatenate([i0[6, 8:], i1[6, 8:]], axis=0).astype(BF16)
     near_ref[at + 2] = jnp.concatenate([i0[7, :8], i1[7, :8]], axis=0).astype(BF16)
-    for part in range(2):
-        last_ref[2 * part] = i0[4 + part].astype(BF16)
-        last_ref[2 * part + 1] = i1[4 + part].astype(BF16)
     even_quad = lax.rem(lax.div(place, 4), 2) == 0
     count = far_a_ref.shape[0] - 3
     base = 2 * n - 2
@@ -191,6 +192,89 @@
         ref[count] = near_ref[base + pick]
         ref[count + 1] = near_ref[base + 2 + pick]
         ref[count + 2] = near_ref[base + 8]
+
+
+def sign_rows():
+    row = lax.broadcasted_iota(jnp.int32, (1, 8, LANES), 1)
+    return jnp.where(row < 4, 1.0, -1.0).astype(F32)
+
+
+def valid(flag, v):
+    return jnp.where(flag, v, jnp.zeros_like(v))
+
+
+def choose(flag, x_ref, y_ref, lo, hi):
+    return jnp.where(flag, x_ref[lo:hi], y_ref[lo:hi]).astype(F32)
+
+
+def middle_coefs(c_ref, at, near_ref, left, right, has_l1, has_r1, coef_n):
+    own = near_ref[0:coef_n].astype(F32)
+    c_ref[at - 15 : at - 1] = left[2 : coef_n - 2].astype(BF16)
+    c_ref[at - 1 : at + 1] = (
+        left[coef_n - 2 :] + jnp.concatenate([valid(has_l1, own[0:1]), own[1:2]], axis=0)
+    ).astype(BF16)
+    c_ref[at + 1 : at + 15] = own[2 : coef_n - 2].astype(BF16)
+    c_ref[at + 15 : at + 17] = (
+        right[:2]
+        + jnp.concatenate([own[coef_n - 2 : coef_n - 1], valid(has_r1, own[coef_n - 1 :])], axis=0)
+    ).astype(BF16)
+    c_ref[at + 17 : at + 31] = right[2 : coef_n - 2].astype(BF16)
+
+
+def band_product(c_ref, parts, rows, table_ref, ve_ref, vo_ref):
+    tables = table_ref.shape[0]
+    count = sum(n for _, n in parts)
+    lane2, lane3 = low_lanes((1, LANES)), low_lanes((1, 1, LANES))
+    sign = sign_rows()
+    swapped = lane_swap(rows)
+    zero = jnp.zeros((COEFS, tables * LANES), BF16)
+    for parity, v_ref in ((0, ve_ref), (1, vo_ref)):
+        lhs = jnp.concatenate(
+            [
+                jnp.concatenate([c_ref[o + k : o + k + n] for o, n in parts], axis=0).reshape(
+                    count * 16, LANES
+                )
+                for k in range(REACH + 1)
+            ],
+            axis=1,
+        )
+        full = jnp.concatenate([table_ref[t] for t in range(tables)], axis=1)
+        rhs = jnp.concatenate([full, zero] if parity == 0 else [zero, full], axis=0)
+        out = jnp.dot(lhs, rhs, preferred_element_type=F32)
+        pick = jnp.where(lane2, rows, swapped) if parity == 0 else jnp.where(lane2, swapped, rows)
+        pick = pick.reshape(count, 1, LANES)
+        v = jnp.zeros((count, 16, LANES), F32)
+        for t in range(tables):
+            part = out[:, LANES * t : LANES * (t + 1)].reshape(count, 16, LANES)
+            v = jnp.where(pick == float(t), part, v)
+        v_ref[0:count] = v
+    ve, vo = ve_ref[0:count], vo_ref[0:count]
+    x = jnp.where(lane3, ve, lane_swap(vo))
+    y = jnp.where(lane3, lane_swap(ve), vo)
+    return jnp.concatenate(
+        [x[:, :8] - sign * y[:, 8:], x[:, 8:] + sign * y[:, :8]], axis=1
+    ).astype(BF16)
+
+
+INNER = (-7, 23)
+
+
+def inner_kernel(units, near_ref, a1_ref, b1_ref, table_ref, out_ref, c_ref, ve_ref, vo_ref, pick_ref):
+    unit = lax.div(lax.axis_index("lat"), 2)
+    odd_unit = lax.rem(unit, 2) == 1
+    has_l1, has_r1 = unit >= 1, unit + 1 < units
+    coef_n = 18
+    left = valid(has_l1, choose(odd_unit, a1_ref, b1_ref, 0, coef_n))
+    right = valid(has_r1, choose(odd_unit, b1_ref, a1_ref, 0, coef_n))
+    middle_coefs(c_ref, 15, near_ref, left, right, has_l1, has_r1, coef_n)
+    pos = coef_n + 8
+    pick_ref[0:16] = jnp.where(has_l1, choose(odd_unit, a1_ref, b1_ref, pos, pos + 1)[0], -1.0)
+    pick_ref[16:32] = near_ref[pos].astype(F32)
+    pick_ref[32:48] = jnp.where(has_r1, choose(odd_unit, b1_ref, a1_ref, pos, pos + 1)[0], -1.0)
+    lo, hi = INNER
+    out_ref[...] = band_product(
+        c_ref, ((lo - 8 + 15, hi - lo),), pick_ref[lo + 16 : hi + 16], table_ref, ve_ref, vo_ref
+    )
 
 
 def main_kernel(
@@ -204,7 +288,7 @@
     table_ref,
     forward_ref,
     inverse_ref,
-    scale_ref,
+    inner_ref,
     keep_ref,
     send_ref,
     c_ref,
@@ -229,16 +313,8 @@
     pairs = 16
     coef_n = pairs + 2
     far_n = a2_ref.shape[0] - 3
-    tables = table_ref.shape[0]
-
-    def valid(flag, v):
-        return jnp.where(flag, v, jnp.zeros_like(v))
-
-    def choose(flag, x_ref, y_ref, lo, hi):
-        return jnp.where(flag, x_ref[lo:hi], y_ref[lo:hi]).astype(F32)
 
     base = 26
-    own = near_ref[0:coef_n].astype(F32)
     left = valid(has_l1, choose(odd_unit, a1_ref, b1_ref, 0, coef_n))
     right = valid(has_r1, choose(odd_unit, b1_ref, a1_ref, 0, coef_n))
     left2 = valid(has_l2, choose(odd_quad, a2_ref, b2_ref, 0, far_n))
@@ -246,13 +322,7 @@
     c_ref[0 : far_n - 2] = left2[: far_n - 2].astype(BF16)
     c_ref[base - 17 : base - 15] = (left2[far_n - 2 :] + jnp.concatenate(
         [valid(has_l2, left[0:1]), left[1:2]], axis=0)).astype(BF16)
-    c_ref[base - 15 : base - 1] = left[2 : coef_n - 2].astype(BF16)
-    c_ref[base - 1 : base + 1] = (left[coef_n - 2 :] + jnp.concatenate(
-        [valid(has_l1, own[0:1]), own[1:2]], axis=0)).astype(BF16)
-    c_ref[base + 1 : base + 15] = own[2 : coef_n - 2].astype(BF16)
-    c_ref[base + 15 : base + 17] = (right[:2] + jnp.concatenate(
-        [own[coef_n - 2 : coef_n - 1], valid(has_r1, own[coef_n - 1 :])], axis=0)).astype(BF16)
-    c_ref[base + 17 : base + 31] = right[2 : coef_n - 2].astype(BF16)
+    middle_coefs(c_ref, base, near_ref, left, right, has_l1, has_r1, coef_n)
     c_ref[base + 31 : base + 33] = (right2[:2] + jnp.concatenate(
         [right[coef_n - 2 : coef_n - 1], valid(has_r2, right[coef_n - 1 :])], axis=0)).astype(BF16)
     c_ref[base + 33 : base + 31 + far_n] = right2[2:].astype(BF16)
@@ -289,16 +359,10 @@
     pick_ref[0, 64:80] = jnp.where(
         has_r2, choose(odd_quad, b2_ref, a2_ref, far_n + 2, far_n + 3)[0], -1.0)
 
-    scale = scale_ref[0]
-    row8 = lax.broadcasted_iota(jnp.int32, (1, 8, LANES), 1)
-    sign = jnp.where(row8 < 4, 1.0, -1.0).astype(F32)
+    sign = sign_rows()
+    row3 = lax.broadcasted_iota(jnp.int32, (1, 8, LANES), 1) < 4
     lane3 = low_lanes((1, 1, LANES))
     lane2 = low_lanes((1, LANES))
-
-    def table_rows(parity):
-        zero = jnp.zeros((COEFS, tables * LANES), BF16)
-        full = jnp.concatenate([table_ref[t] for t in range(tables)], axis=1)
-        return jnp.concatenate([full, zero] if parity == 0 else [zero, full], axis=0)
 
     plan = (
         dict(lo=-18, hi=34, base=26, first=-17),
@@ -308,31 +372,22 @@
     for step, item in enumerate(plan):
         lo, hi = item["lo"], item["hi"]
         count = hi - lo
-        off = item["base"] + lo - 8
-        rows = pick_ref[step, lo + 32 : hi + 32]
-        swapped = lane_swap(rows)
-        for parity, v_ref in ((0, ve_ref), (1, vo_ref)):
-            lhs = jnp.concatenate(
-                [c_ref[off + k : off + k + count].reshape(count * 16, LANES) for k in range(17)],
-                axis=1,
-            )
-            out = jnp.dot(lhs, table_rows(parity), preferred_element_type=F32)
-            pick = jnp.where(lane2, rows, swapped) if parity == 0 else jnp.where(lane2, swapped, rows)
-            pick = pick.reshape(count, 1, LANES)
-            v = jnp.zeros((count, 16, LANES), F32)
-            for t in range(tables):
-                v = jnp.where(
-                    pick == float(t), out[:, LANES * t : LANES * (t + 1)].reshape(count, 16, LANES), v
-                )
-            v_ref[0:count] = v
-        ve, vo = ve_ref[0:count], vo_ref[0:count]
-        x = jnp.where(lane3, ve, lane_swap(vo))
-        y = jnp.where(lane3, lane_swap(ve), vo)
-        prop = jnp.concatenate(
-            [x[:, :8] - sign * y[:, 8:], x[:, 8:] + sign * y[:, :8]], axis=1
-        )
         p_ref[0] = jnp.zeros((16, LANES), BF16)
-        p_ref[1 : count + 1] = prop.astype(BF16)
+        if step == 0:
+            parts = ((lo, INNER[0] - lo), (INNER[1], hi - INNER[1]))
+            p_ref[1 + INNER[0] - lo : 1 + INNER[1] - lo] = inner_ref[...]
+        else:
+            parts = ((lo, count),)
+        rows = jnp.concatenate(
+            [pick_ref[step, a + 32 : a + 32 + m] for a, m in parts], axis=0
+        )
+        out = band_product(
+            c_ref, [(item["base"] + a - 8, m) for a, m in parts], rows, table_ref, ve_ref, vo_ref
+        )
+        done = 0
+        for a, m in parts:
+            p_ref[1 + a - lo : 1 + a - lo + m] = out[done : done + m]
+            done += m
         first = item["first"]
         n = hi - first
         o = first - lo
@@ -354,7 +409,7 @@
                 r2 = (block >= 64) & has_r2
                 return inside | l1 | r1 | l2 | r2
             ok = jnp.where(lane2, exists(number - 1).astype(jnp.int32), exists(number).astype(jnp.int32)) > 0
-        theta = scale * jnp.where(lane2, lane_swap(before), lane_swap(after))
+        theta = jnp.where(lane2, lane_swap(before), lane_swap(after))
         sin_v, cos_v = sin_cos(theta)
         if step < 2:
             sin_v = jnp.where(ok, sin_v, 0.0)
@@ -400,7 +455,6 @@
                 | ((number >= 32) & has_r2)
             )
             c_ref[0:m] = jnp.where(ok, coefs, 0.0).astype(BF16)
-    row3 = row8 < 4
     for ref, half in ((keep_ref, second), (send_ref, 1 - second)):
         for parity in range(2):
             span = pl.ds(8 * half, 8)
@@ -434,8 +488,8 @@
     pairs = points // (2 * WINDOW)
     first, forward, inverse = (jnp.asarray(m, BF16) for m in pair_matrices())
     vmem = pl.BlockSpec(memory_space=pltpu.VMEM)
+    hbm = pl.BlockSpec(memory_space=pltpu.HBM)
     smem = pl.BlockSpec(memory_space=pltpu.SMEM)
-    hbm = pl.BlockSpec(memory_space=pltpu.HBM)
 
     def tiles(n):
         return jax.ShapeDtypeStruct((n, 16, LANES), BF16)
@@ -471,26 +525,43 @@
     near, far_a, far_b, last = pl.pallas_call(
         unit_kernel,
         out_shape=(tiles(near_n), tiles(far_n), tiles(far_n), tiles(4)),
-        in_specs=[vmem] * 3,
+        in_specs=[vmem] * 3 + [smem],
         out_specs=(vmem,) * 4,
         compiler_params=pltpu.CompilerParams(vmem_limit_bytes=4 << 20),
         name="unit",
-    )(keep, send, got)
+    )(keep, send, got, frequency_scale)
     a1 = lax.ppermute(near, "lat", matching(lat, 2, 0))
     b1 = lax.ppermute(near, "lat", matching(lat, 2, 1))
     a2 = lax.ppermute(far_a, "lat", matching(lat, 4, 0))
     b2 = lax.ppermute(far_b, "lat", matching(lat, 4, 1))
+    inner_n = INNER[1] - INNER[0]
+    table = propagator_table[0]
+    inner = pl.pallas_call(
+        lambda *refs: inner_kernel(lat // 2, *refs),
+        out_shape=tiles(inner_n),
+        in_specs=[vmem] * 4,
+        out_specs=vmem,
+        scratch_shapes=[
+            pltpu.VMEM((46, 16, LANES), BF16),
+            pltpu.VMEM((inner_n, 16, LANES), F32),
+            pltpu.VMEM((inner_n, 16, LANES), F32),
+            pltpu.VMEM((48, LANES), F32),
+        ],
+        compiler_params=pltpu.CompilerParams(vmem_limit_bytes=24 << 20),
+        cost_estimate=pl.CostEstimate(flops=2 * 10**9, bytes_accessed=10**7, transcendentals=0),
+        name="inner",
+    )(near, a1, b1, table)
     image = jax.ShapeDtypeStruct((2, pairs, 16, LANES), BF16)
     own, other = pl.pallas_call(
         lambda *refs: main_kernel(lat // 2, *refs),
         out_shape=(image, image),
-        in_specs=[vmem] * 9 + [smem],
+        in_specs=[vmem] * 10,
         out_specs=(vmem, vmem),
         scratch_shapes=[
             pltpu.VMEM((68, 16, LANES), BF16),
             pltpu.VMEM((53, 16, LANES), BF16),
-            pltpu.VMEM((52, 16, LANES), F32),
-            pltpu.VMEM((52, 16, LANES), F32),
+            pltpu.VMEM((34, 16, LANES), F32),
+            pltpu.VMEM((34, 16, LANES), F32),
             pltpu.VMEM((52, 16, LANES), BF16),
             pltpu.VMEM((52, 16, LANES), BF16),
             pltpu.VMEM((STEPS, 128, LANES), F32),
@@ -501,7 +572,7 @@
         ],
         compiler_params=pltpu.CompilerParams(vmem_limit_bytes=32 << 20),
         name="steps",
-    )(near, last, a1, b1, a2, b2, propagator_table[0], forward, inverse, frequency_scale)
+    )(near, last, a1, b1, a2, b2, table, forward, inverse, inner)
     swapped = lax.ppermute(other, "lat", partner)
     core = lax.rem(lax.axis_index("lat"), 2)
     if freqs == 2:

time: 30.8 us -> 29.4 us (0.955)
  the two profiles are of different devices: /device:TPU:10 before, /device:TPU:28 now
where the time goes in v4:
time: 29.4 us; the launch traced here: 29.2 us
  Pallas kernels  12.2 us (41%)
  waiting for transfers between devices  10.5 us (36%)
  starting transfers between devices  5.75 us (20%)
  between operations  0.75 us (3%)
    pallas_call x1, Pallas kernels, on_device(): pl.pallas_call(lambda *refs: main_kernel(lat // 2, *refs), out_shape=(ima...  7.47 us
    ppermute x1, waiting for transfers between devices, on_device(): b1 = lax.ppermute(near, 'lat', matching(lat, 2, 1))  4.61 us
    ppermute x1, waiting for transfers between devices, on_device(): come = lax.ppermute(leave, 'freq', [(0, 1), (1, 0)])  3.76 us
    pallas_call x1, Pallas kernels, on_device(): pl.pallas_call(lambda *refs: inner_kernel(lat // 2, *refs), out_shape=til...  2.57 us
    ppermute x1, starting transfers between devices, on_device(): b1 = lax.ppermute(near, 'lat', matching(lat, 2, 1))  2.32 us
    ppermute x1, starting transfers between devices, on_device(): a1 = lax.ppermute(near, 'lat', matching(lat, 2, 0))  1.56 us
    pallas_call x1, Pallas kernels, on_device(): pl.pallas_call(prep_kernel, out_shape=(tiles(pairs + 2), tiles(pairs + 2...  1.42 us
    ppermute x1, waiting for transfers between devices, on_device(): swapped = lax.ppermute(other, 'lat', partner)  1.23 us
  transfers between devices with their start and end apart: 7, of which 5 were waited for; matrix products, arithmetic and copies ran while one was open for 0% of the time, Pallas kernels for 9%

profile of v4, /device:TPU:28, one launch (start us, length us, event | category | flops | bytes accessed | tf_op | source)
XLA Modules:
  0.0 29.2 jit_solution(16327944166383245017)
XLA Ops:
  0.0 0.0 copy-start
  0.0 1.4 %prep.1 = (bf16[10,16,128]{2,1,0:T(8,128)(2,1)S(1)}, bf16[18,16,128]{2,1,0:T(8,128)(2,1)S(1)}) custom-call(f32[4,1,8,2048]{3,2,1,0:T(8,128)} %wave_hbm.1, f32[3,2048]{1,0:T(4,128)} %slow_hbm.1, s32[3,16]{1,0:T(4,128)} %index_hbm.1, bf16[512,128]{1,0:T(8,128)(2,1)} %constant.19.clone.first_hbm), custom_call_target="tpu_custom_call" | custom-call | flops 1000000000 | bytes 10000000 | tf_op jit(solution)/shard_map/prep/pallas_call | solution.py:498
  1.4 0.1 collective-permute-start
  2.2 0.6 %collective-permute-done.got_ref = bf16[18,16,128]{2,1,0:T(8,128)(2,1)S(1)} collective-permute-done((bf16[18,16,128]{2,1,0:T(8,128)(2,1)S(1)}, bf16[18,16,128]{2,1,0:T(8,128)(2,1)S(1)}, u32[]{:S(2)}, u32[]{:S(2)}) %collective-permute-start) | collective-permute-done | bytes 73760 | tf_op jit(solution)/shard_map/ppermute | solution.py:522
  2.8 0.1 unit.1
  2.8 1.6 %collective-permute-start.1 = (bf16[29,16,128]{2,1,0:T(8,128)(2,1)S(1)}, bf16[29,16,128]{2,1,0:T(8,128)(2,1)S(1)}, u32[]{:S(2)}, u32[]{:S(2)}) collective-permute-start(bf16[29,16,128]{2,1,0:T(8,128)(2,1)S(1)} %get-tuple-element.15.refs_0_), channel_id=1, source_target_pairs={{0,4},{2,6},{4,0},{6,2},{8,12},{10,14},{12,8},{14,10},{16,20},{18,... | collective-permute-start | bytes 356360 | tf_op jit(solution)/shard_map/ppermute | solution.py:533
  4.4 2.3 %collective-permute-start.2 = (bf16[29,16,128]{2,1,0:T(8,128)(2,1)S(1)}, bf16[29,16,128]{2,1,0:T(8,128)(2,1)S(1)}, u32[]{:S(2)}, u32[]{:S(2)}) collective-permute-start(bf16[29,16,128]{2,1,0:T(8,128)(2,1)S(1)} %get-tuple-element.15.refs_0_), channel_id=1, source_target_pairs={{0,0},{2,2},{4,8},{6,10},{8,4},{10,6},{12,16},{14,18},{16,12},{18,... | collective-permute-start | bytes 356360 | tf_op jit(solution)/shard_map/ppermute | solution.py:534
  6.7 0.5 %collective-permute-start.3 = (bf16[14,16,128]{2,1,0:T(8,128)(2,1)S(1)}, bf16[14,16,128]{2,1,0:T(8,128)(2,1)S(1)}, u32[]{:S(2)}, u32[]{:S(2)}) collective-permute-start(bf16[14,16,128]{2,1,0:T(8,128)(2,1)S(1)} %get-tuple-element.17), channel_id=1, source_target_pairs={{0,8},{2,10},{4,12},{6,14},{8,0},{10,2},{12,4},{14,6},{16,24},{18,... | collective-permute-start | bytes 172040 | tf_op jit(solution)/shard_map/ppermute | solution.py:535
  7.2 0.7 %collective-permute-start.4 = (bf16[14,16,128]{2,1,0:T(8,128)(2,1)S(1)}, bf16[14,16,128]{2,1,0:T(8,128)(2,1)S(1)}, u32[]{:S(2)}, u32[]{:S(2)}) collective-permute-start(bf16[14,16,128]{2,1,0:T(8,128)(2,1)S(1)} %get-tuple-element.18), channel_id=1, source_target_pairs={{0,0},{2,2},{4,4},{6,6},{8,16},{10,18},{12,20},{14,22},{16,8},{18,... | collective-permute-start | bytes 172040 | tf_op jit(solution)/shard_map/ppermute | solution.py:536
  7.9 0.3 %collective-permute-done.1.refs_1_.refs_2_ = bf16[29,16,128]{2,1,0:T(8,128)(2,1)S(1)} collective-permute-done((bf16[29,16,128]{2,1,0:T(8,128)(2,1)S(1)}, bf16[29,16,128]{2,1,0:T(8,128)(2,1)S(1)}, u32[]{:S(2)}, u32[]{:S(2)}) %collective-permute-start.1) | collective-permute-done | bytes 118816 | tf_op jit(solution)/shard_map/ppermute | solution.py:533
  8.2 4.6 %collective-permute-done.2.refs_2_.refs_3_ = bf16[29,16,128]{2,1,0:T(8,128)(2,1)S(1)} collective-permute-done((bf16[29,16,128]{2,1,0:T(8,128)(2,1)S(1)}, bf16[29,16,128]{2,1,0:T(8,128)(2,1)S(1)}, u32[]{:S(2)}, u32[]{:S(2)}) %collective-permute-start.2) | collective-permute-done | bytes 118816 | tf_op jit(solution)/shard_map/ppermute | solution.py:534
  12.8 0.0 copy-done
  12.8 0.0 copy-start.1
  12.8 0.0 copy-start.2
  12.8 2.6 %inner.1.refs_9_ = bf16[30,16,128]{2,1,0:T(8,128)(2,1)S(1)} custom-call(bf16[29,16,128]{2,1,0:T(8,128)(2,1)S(1)} %get-tuple-element.15.refs_0_, bf16[29,16,128]{2,1,0:T(8,128)(2,1)S(1)} %collective-permute-done.1.refs_1_.refs_2_, bf16[29,16,128]{2,1,0:T(8,128)(2,1)S(1)} %collective-permute-done.2.refs_2_.refs_3_, bf16[4,2112,128]{2,1,0:T(8,128)(2,1)S(1)} %bitcast.1), custom_call_target="tpu_custom_call" | custom-call | flops 2000000000 | bytes 10000000 | tf_op jit(solution)/shard_map/inner/pallas_call | solution.py:539
  15.4 0.0 collective-permute-done.3.refs_4_
  15.4 0.0 collective-permute-done.4.refs_5_
  15.4 0.0 copy-done.1
  15.4 0.0 copy-done.2
  15.4 7.5 %steps.1 = (bf16[2,8,16,128]{3,2,1,0:T(8,128)(2,1)S(1)}, bf16[2,8,16,128]{3,2,1,0:T(8,128)(2,1)S(1)}) custom-call(bf16[29,16,128]{2,1,0:T(8,128)(2,1)S(1)} %get-tuple-element.15.refs_0_, bf16[4,16,128]{2,1,0:T(8,128)(2,1)S(1)} %get-tuple-element.16.refs_1_, bf16[29,16,128]{2,1,0:T(8,128)(2,1)S(1)} %collective-permute-done.1.refs_1_.refs_2_, ...), custom_call_target="tpu_custom_call" | custom-call | tf_op jit(solution)/shard_map/steps/pallas_call | solution.py:555
  22.9 0.1 collective-permute-start.5
  23.0 1.2 %collective-permute-done.5 = bf16[2,8,16,128]{3,2,1,0:T(8,128)(2,1)S(1)} collective-permute-done((bf16[2,8,16,128]{3,2,1,0:T(8,128)(2,1)S(1)}, bf16[2,8,16,128]{3,2,1,0:T(8,128)(2,1)S(1)}, u32[]{:S(2)}, u32[]{:S(2)}) %collective-permute-start.5) | collective-permute-done | bytes 65568 | tf_op jit(solution)/shard_map/ppermute | solution.py:576
  24.2 0.6 %collective-permute-start.6 = (bf16[2,8,16,128]{3,2,1,0:T(8,128)(2,1)S(1)}, bf16[2,8,16,128]{3,2,1,0:T(8,128)(2,1)S(1)}, u32[]{:S(2)}, u32[]{:S(2)}) collective-permute-start(bf16[2,8,16,128]{3,2,1,0:T(8,128)(2,1)S(1)} %get-tuple-element.21), channel_id=1, source_target_pairs={{0,1},{1,0},{2,3},{3,2},{4,5},{5,4},{6,7},{7,6},{8,9},{9,8},{10,11... | collective-permute-start | bytes 196616 | tf_op jit(solution)/shard_map/ppermute | solution.py:582
  24.8 3.8 %collective-permute-done.6.b_ref = bf16[2,8,16,128]{3,2,1,0:T(8,128)(2,1)S(1)} collective-permute-done((bf16[2,8,16,128]{3,2,1,0:T(8,128)(2,1)S(1)}, bf16[2,8,16,128]{3,2,1,0:T(8,128)(2,1)S(1)}, u32[]{:S(2)}, u32[]{:S(2)}) %collective-permute-start.6) | collective-permute-done | bytes 65568 | tf_op jit(solution)/shard_map/ppermute | solution.py:582
  28.6 0.7 %total.1 = f32[3,4,2048]{2,1,0:T(4,128)} custom-call(bf16[2,8,16,128]{3,2,1,0:T(8,128)(2,1)S(1)} %get-tuple-element.22.a_ref, bf16[2,8,16,128]{3,2,1,0:T(8,128)(2,1)S(1)} %collective-permute-done.6.b_ref), custom_call_target="tpu_custom_call" | custom-call | tf_op jit(solution)/shard_map/total/pallas_call | solution.py:583
  (1 shorter events, 0.0 us)
Async XLA Ops:
  0.0 12.8 %copy-start = (bf16[1,4,2112,128]{3,2,1,0:T(8,128)(2,1)S(1)}, bf16[1,4,2112,128]{3,2,1,0:T(8,128)(2,1)}, u32[]{:S(2)}) copy-start(bf16[1,4,2112,128]{3,2,1,0:T(8,128)(2,1)} %param.9) | copy-start | bytes 6488068
  1.4 1.3 %collective-permute-start = (bf16[18,16,128]{2,1,0:T(8,128)(2,1)S(1)}, bf16[18,16,128]{2,1,0:T(8,128)(2,1)S(1)}, u32[]{:S(2)}, u32[]{:S(2)}) collective-permute-start(bf16[18,16,128]{2,1,0:T(8,128)(2,1)S(1)} %get-tuple-element.14.sent_ref), channel_id=1, source_target_pairs={{0,2},{2,0},{4,6},{6,4},{8,10},{10,8},{12,14},{14,12},{16,18},{18,... | collective-permute-start | bytes 221192 | tf_op jit(solution)/shard_map/ppermute | solution.py:522
  2.8 5.4 %collective-permute-start.1 = (bf16[29,16,128]{2,1,0:T(8,128)(2,1)S(1)}, bf16[29,16,128]{2,1,0:T(8,128)(2,1)S(1)}, u32[]{:S(2)}, u32[]{:S(2)}) collective-permute-start(bf16[29,16,128]{2,1,0:T(8,128)(2,1)S(1)} %get-tuple-element.15.refs_0_), channel_id=1, source_target_pairs={{0,4},{2,6},{4,0},{6,2},{8,12},{10,14},{12,8},{14,10},{16,20},{18,... | collective-permute-start | bytes 356360 | tf_op jit(solution)/shard_map/ppermute | solution.py:533
  4.4 8.4 %collective-permute-start.2 = (bf16[29,16,128]{2,1,0:T(8,128)(2,1)S(1)}, bf16[29,16,128]{2,1,0:T(8,128)(2,1)S(1)}, u32[]{:S(2)}, u32[]{:S(2)}) collective-permute-start(bf16[29,16,128]{2,1,0:T(8,128)(2,1)S(1)} %get-tuple-element.15.refs_0_), channel_id=1, source_target_pairs={{0,0},{2,2},{4,8},{6,10},{8,4},{10,6},{12,16},{14,18},{16,12},{18,... | collective-permute-start | bytes 356360 | tf_op jit(solution)/shard_map/ppermute | solution.py:534
  6.7 8.7 %collective-permute-start.3 = (bf16[14,16,128]{2,1,0:T(8,128)(2,1)S(1)}, bf16[14,16,128]{2,1,0:T(8,128)(2,1)S(1)}, u32[]{:S(2)}, u32[]{:S(2)}) collective-permute-start(bf16[14,16,128]{2,1,0:T(8,128)(2,1)S(1)} %get-tuple-element.17), channel_id=1, source_target_pairs={{0,8},{2,10},{4,12},{6,14},{8,0},{10,2},{12,4},{14,6},{16,24},{18,... | collective-permute-start | bytes 172040 | tf_op jit(solution)/shard_map/ppermute | solution.py:535
  7.2 8.2 %collective-permute-start.4 = (bf16[14,16,128]{2,1,0:T(8,128)(2,1)S(1)}, bf16[14,16,128]{2,1,0:T(8,128)(2,1)S(1)}, u32[]{:S(2)}, u32[]{:S(2)}) collective-permute-start(bf16[14,16,128]{2,1,0:T(8,128)(2,1)S(1)} %get-tuple-element.18), channel_id=1, source_target_pairs={{0,0},{2,2},{4,4},{6,6},{8,16},{10,18},{12,20},{14,22},{16,8},{18,... | collective-permute-start | bytes 172040 | tf_op jit(solution)/shard_map/ppermute | solution.py:536
  12.8 2.6 %copy-start.1 = (bf16[256,256]{1,0:T(8,128)(2,1)S(1)}, bf16[256,256]{1,0:T(8,128)(2,1)}, u32[]{:S(2)}) copy-start(bf16[256,256]{1,0:T(8,128)(2,1)} %constant.21.clone.refs_8_) | copy-start | bytes 393220
  12.8 2.6 %copy-start.2 = (bf16[384,128]{1,0:T(8,128)(2,1)S(1)}, bf16[384,128]{1,0:T(8,128)(2,1)}, u32[]{:S(2)}) copy-start(bf16[384,128]{1,0:T(8,128)(2,1)} %constant.20.clone.refs_7_) | copy-start | bytes 294916
  22.9 1.3 %collective-permute-start.5 = (bf16[2,8,16,128]{3,2,1,0:T(8,128)(2,1)S(1)}, bf16[2,8,16,128]{3,2,1,0:T(8,128)(2,1)S(1)}, u32[]{:S(2)}, u32[]{:S(2)}) collective-permute-start(bf16[2,8,16,128]{3,2,1,0:T(8,128)(2,1)S(1)} %get-tuple-element.20), channel_id=1, source_target_pairs={{0,2},{2,0},{4,6},{6,4},{8,10},{10,8},{12,14},{14,12},{16,18},{18,... | collective-permute-start | bytes 196616 | tf_op jit(solution)/shard_map/ppermute | solution.py:576
  24.2 4.3 %collective-permute-start.6 = (bf16[2,8,16,128]{3,2,1,0:T(8,128)(2,1)S(1)}, bf16[2,8,16,128]{3,2,1,0:T(8,128)(2,1)S(1)}, u32[]{:S(2)}, u32[]{:S(2)}) collective-permute-start(bf16[2,8,16,128]{3,2,1,0:T(8,128)(2,1)S(1)} %get-tuple-element.21), channel_id=1, source_target_pairs={{0,1},{1,0},{2,3},{3,2},{4,5},{5,4},{6,7},{7,6},{8,9},{9,8},{10,11... | collective-permute-start | bytes 196616 | tf_op jit(solution)/shard_map/ppermute | solution.py:582

commit v5 on v4

--- a/solution.py
+++ b/solution.py
@@ -7,6 +7,7 @@
 from jax.experimental import pallas as pl
 from jax.experimental.pallas import tpu as pltpu
 from jax.sharding import PartitionSpec as P
+
 
 WINDOW = 128
 COEFS = 64
@@ -173,7 +174,7 @@
     for step in range(STEPS):
         ref, to = (near_ref, at) if step < 2 else (last_ref, 0)
         for block, info in enumerate((i0, i1)):
-            theta = scale_ref[0] * (info[2 * step] + info[2 * step + 1])
+            theta = scale_ref[...] * (info[2 * step] + info[2 * step + 1])
             high = theta.astype(BF16)
             ref[to + block] = high
             ref[to + 2 + block] = (theta - high.astype(F32)).astype(BF16)
@@ -207,73 +208,97 @@
     return jnp.where(flag, x_ref[lo:hi], y_ref[lo:hi]).astype(F32)
 
 
-def middle_coefs(c_ref, at, near_ref, left, right, has_l1, has_r1, coef_n):
+def middle_coefs(near_ref, left, right, has_l1, has_r1, coef_n):
     own = near_ref[0:coef_n].astype(F32)
-    c_ref[at - 15 : at - 1] = left[2 : coef_n - 2].astype(BF16)
-    c_ref[at - 1 : at + 1] = (
-        left[coef_n - 2 :] + jnp.concatenate([valid(has_l1, own[0:1]), own[1:2]], axis=0)
-    ).astype(BF16)
-    c_ref[at + 1 : at + 15] = own[2 : coef_n - 2].astype(BF16)
-    c_ref[at + 15 : at + 17] = (
+    return [
+        left[2 : coef_n - 2],
+        left[coef_n - 2 :] + jnp.concatenate([valid(has_l1, own[0:1]), own[1:2]], axis=0),
+        own[2 : coef_n - 2],
         right[:2]
-        + jnp.concatenate([own[coef_n - 2 : coef_n - 1], valid(has_r1, own[coef_n - 1 :])], axis=0)
-    ).astype(BF16)
-    c_ref[at + 17 : at + 31] = right[2 : coef_n - 2].astype(BF16)
-
-
-def band_product(c_ref, parts, rows, table_ref, ve_ref, vo_ref):
-    tables = table_ref.shape[0]
+        + jnp.concatenate([own[coef_n - 2 : coef_n - 1], valid(has_r1, own[coef_n - 1 :])], axis=0),
+        right[2 : coef_n - 2],
+    ]
+
+
+def put_coefs(x_ref, coefs):
+    n = coefs.shape[0]
+    coefs = coefs.astype(BF16).astype(F32)
+    real, imag = coefs[:, :8], coefs[:, 8:]
+    source = lax.broadcasted_iota(jnp.int32, (1, 8, LANES), 1) < 4
+    kinds = (real + imag, jnp.where(source, real, imag), jnp.where(source, imag, real))
+    for kind, x in enumerate(kinds):
+        x_ref[kind, 0, 0 : n // 2] = x.reshape(n // 2, 16, LANES).astype(BF16)
+        x_ref[kind, 1, 0 : n // 2 - 1] = x[1 : n - 1].reshape(n // 2 - 1, 16, LANES).astype(BF16)
+
+
+def weight_kernel(table_ref, w_ref):
+    for duo in range(table_ref.shape[0] // 2):
+        a, b = table_ref[2 * duo], table_ref[2 * duo + 1]
+        low = low_lanes(a.shape)
+        real = jnp.where(low, a, jnp.concatenate([b[:, COEFS:], b[:, :COEFS]], axis=1))
+        imag = jnp.where(low, jnp.concatenate([a[:, COEFS:], a[:, :COEFS]], axis=1), b)
+        w_ref[0, duo] = real
+        w_ref[1, duo] = imag - real
+        w_ref[2, duo] = imag + real
+
+
+def band_product(x_ref, parts, rows, w_ref, k_ref):
     count = sum(n for _, n in parts)
     lane2, lane3 = low_lanes((1, LANES)), low_lanes((1, 1, LANES))
-    sign = sign_rows()
-    swapped = lane_swap(rows)
-    zero = jnp.zeros((COEFS, tables * LANES), BF16)
-    for parity, v_ref in ((0, ve_ref), (1, vo_ref)):
-        lhs = jnp.concatenate(
-            [
-                jnp.concatenate([c_ref[o + k : o + k + n] for o, n in parts], axis=0).reshape(
-                    count * 16, LANES
-                )
-                for k in range(REACH + 1)
-            ],
-            axis=1,
-        )
-        full = jnp.concatenate([table_ref[t] for t in range(tables)], axis=1)
-        rhs = jnp.concatenate([full, zero] if parity == 0 else [zero, full], axis=0)
+    half = jnp.floor(rows * 0.5)
+    even = (rows - 2.0 * half) == 0.0
+    direct = jnp.where(lane2, even.astype(F32), 1.0 - even.astype(F32)).reshape(count, 1, LANES)
+    upper = half.reshape(count, 1, LANES)
+    upper_swap = lane_swap(half).reshape(count, 1, LANES)
+    exists = rows.reshape(count, 1, LANES) >= 0.0
+    zero = jnp.zeros((COEFS, 2 * LANES), BF16)
+
+    def band(kind, k):
+        pieces = [
+            x_ref[kind, (o + k) % 2, (o + k) // 2 : (o + k) // 2 + n // 2] for o, n in parts
+        ]
+        return jnp.concatenate(pieces, axis=0).reshape(count * 8, LANES)
+
+    for kind in range(3):
+        lhs = jnp.concatenate([band(kind, k) for k in range(REACH + 1)], axis=1)
+        full = jnp.concatenate([w_ref[kind, 0], w_ref[kind, 1]], axis=1)
+        rhs = jnp.concatenate(
+            [jnp.concatenate([full, zero], axis=0), jnp.concatenate([zero, full], axis=0)], axis=1
+        )
         out = jnp.dot(lhs, rhs, preferred_element_type=F32)
-        pick = jnp.where(lane2, rows, swapped) if parity == 0 else jnp.where(lane2, swapped, rows)
-        pick = pick.reshape(count, 1, LANES)
-        v = jnp.zeros((count, 16, LANES), F32)
-        for t in range(tables):
-            part = out[:, LANES * t : LANES * (t + 1)].reshape(count, 16, LANES)
-            v = jnp.where(pick == float(t), part, v)
-        v_ref[0:count] = v
-    ve, vo = ve_ref[0:count], vo_ref[0:count]
-    x = jnp.where(lane3, ve, lane_swap(vo))
-    y = jnp.where(lane3, lane_swap(ve), vo)
-    return jnp.concatenate(
-        [x[:, :8] - sign * y[:, 8:], x[:, 8:] + sign * y[:, :8]], axis=1
-    ).astype(BF16)
-
-
-INNER = (-7, 23)
-
-
-def inner_kernel(units, near_ref, a1_ref, b1_ref, table_ref, out_ref, c_ref, ve_ref, vo_ref, pick_ref):
+        e0, e1, o0, o1 = (
+            out[:, LANES * t : LANES * (t + 1)].reshape(count, 8, LANES) for t in range(4)
+        )
+        u = jnp.where(upper > 0.0, jnp.where(lane3, e1, o1), jnp.where(lane3, e0, o0))
+        w = jnp.where(upper_swap > 0.0, jnp.where(lane3, o1, e1), jnp.where(lane3, o0, e0))
+        k_ref[kind, 0:count] = jnp.where(direct > 0.0, u, lane_swap(w))
+    first, second, third = (k_ref[kind, 0:count] for kind in range(3))
+    source = lax.broadcasted_iota(jnp.int32, (1, 8, LANES), 1) < 4
+    real = first + jnp.where(source, -third, second)
+    imag = first + jnp.where(source, second, -third)
+    both = jnp.concatenate([real, imag], axis=1)
+    return jnp.where(exists, both, 0.0).astype(BF16)
+
+
+INNER = (-6, 22)
+
+
+def inner_kernel(units, near_ref, a1_ref, b1_ref, w_ref, out_ref, x_ref, k_ref, pick_ref):
     unit = lax.div(lax.axis_index("lat"), 2)
     odd_unit = lax.rem(unit, 2) == 1
     has_l1, has_r1 = unit >= 1, unit + 1 < units
     coef_n = 18
     left = valid(has_l1, choose(odd_unit, a1_ref, b1_ref, 0, coef_n))
     right = valid(has_r1, choose(odd_unit, b1_ref, a1_ref, 0, coef_n))
-    middle_coefs(c_ref, 15, near_ref, left, right, has_l1, has_r1, coef_n)
+    middle = middle_coefs(near_ref, left, right, has_l1, has_r1, coef_n)
+    put_coefs(x_ref, jnp.concatenate(middle, axis=0))
     pos = coef_n + 8
     pick_ref[0:16] = jnp.where(has_l1, choose(odd_unit, a1_ref, b1_ref, pos, pos + 1)[0], -1.0)
     pick_ref[16:32] = near_ref[pos].astype(F32)
     pick_ref[32:48] = jnp.where(has_r1, choose(odd_unit, b1_ref, a1_ref, pos, pos + 1)[0], -1.0)
     lo, hi = INNER
     out_ref[...] = band_product(
-        c_ref, ((lo - 8 + 15, hi - lo),), pick_ref[lo + 16 : hi + 16], table_ref, ve_ref, vo_ref
+        x_ref, ((lo - 8 + 15, hi - lo),), pick_ref[lo + 16 : hi + 16], w_ref, k_ref
     )
 
 
@@ -285,16 +310,15 @@
     b1_ref,
     a2_ref,
     b2_ref,
-    table_ref,
+    w_ref,
     forward_ref,
     inverse_ref,
     inner_ref,
     keep_ref,
     send_ref,
-    c_ref,
+    x_ref,
     p_ref,
-    ve_ref,
-    vo_ref,
+    k_ref,
     xe_ref,
     xo_ref,
     slow_ref,
@@ -314,24 +338,29 @@
     coef_n = pairs + 2
     far_n = a2_ref.shape[0] - 3
 
-    base = 26
     left = valid(has_l1, choose(odd_unit, a1_ref, b1_ref, 0, coef_n))
     right = valid(has_r1, choose(odd_unit, b1_ref, a1_ref, 0, coef_n))
     left2 = valid(has_l2, choose(odd_quad, a2_ref, b2_ref, 0, far_n))
     right2 = valid(has_r2, choose(odd_quad, b2_ref, a2_ref, 0, far_n))
-    c_ref[0 : far_n - 2] = left2[: far_n - 2].astype(BF16)
-    c_ref[base - 17 : base - 15] = (left2[far_n - 2 :] + jnp.concatenate(
-        [valid(has_l2, left[0:1]), left[1:2]], axis=0)).astype(BF16)
-    middle_coefs(c_ref, base, near_ref, left, right, has_l1, has_r1, coef_n)
-    c_ref[base + 31 : base + 33] = (right2[:2] + jnp.concatenate(
-        [right[coef_n - 2 : coef_n - 1], valid(has_r2, right[coef_n - 1 :])], axis=0)).astype(BF16)
-    c_ref[base + 33 : base + 31 + far_n] = right2[2:].astype(BF16)
+    near_left = jnp.concatenate([valid(has_l2, left[0:1]), left[1:2]], axis=0)
+    near_right = jnp.concatenate(
+        [right[coef_n - 2 : coef_n - 1], valid(has_r2, right[coef_n - 1 :])], axis=0
+    )
+    put_coefs(
+        x_ref,
+        jnp.concatenate(
+            [left2[: far_n - 2], left2[far_n - 2 :] + near_left]
+            + middle_coefs(near_ref, left, right, has_l1, has_r1, coef_n)
+            + [right2[:2] + near_right, right2[2:]],
+            axis=0,
+        ),
+    )
 
     at = coef_n
     far_rows = 48
     for step in range(2):
         lo = at + 4 * step
-        for ref_rows, flag, pos in ((0, odd_unit, -32), (1, jnp.logical_not(odd_unit), 32)):
+        for flag, pos in ((odd_unit, -32), (jnp.logical_not(odd_unit), 32)):
             hi_v = choose(flag, a1_ref, b1_ref, lo, lo + 2)
             lo_v = choose(flag, a1_ref, b1_ref, lo + 2, lo + 4)
             slow_ref[step, far_rows + pos : far_rows + pos + 32] = (hi_v + lo_v).reshape(32, LANES)
@@ -382,7 +411,7 @@
             [pick_ref[step, a + 32 : a + 32 + m] for a, m in parts], axis=0
         )
         out = band_product(
-            c_ref, [(item["base"] + a - 8, m) for a, m in parts], rows, table_ref, ve_ref, vo_ref
+            x_ref, [(item["base"] + a - 8, m) for a, m in parts], rows, w_ref, k_ref
         )
         done = 0
         for a, m in parts:
@@ -401,6 +430,7 @@
         after = slow_ref[step, g0 : g0 + 2 * n]
         if step < 2:
             number = lax.broadcasted_iota(jnp.int32, (2 * n, 1), 0) + 2 * first
+
             def exists(block):
                 inside = (block >= 0) & (block < 32)
                 l1 = (block < 0) & (block >= -32) & has_l1
@@ -408,6 +438,7 @@
                 l2 = (block < -32) & has_l2
                 r2 = (block >= 64) & has_r2
                 return inside | l1 | r1 | l2 | r2
+
             ok = jnp.where(lane2, exists(number - 1).astype(jnp.int32), exists(number).astype(jnp.int32)) > 0
         theta = jnp.where(lane2, lane_swap(before), lane_swap(after))
         sin_v, cos_v = sin_cos(theta)
@@ -417,14 +448,14 @@
         cos_ref[0 : 2 * n] = cos_v
         sin_ref[0 : 2 * n] = sin_v
         images = []
-        for parity, x_ref in ((0, xe_ref), (1, xo_ref)):
+        for parity, sample_ref in ((0, xe_ref), (1, xo_ref)):
             b = back[:, LANES * parity : LANES * (parity + 1)].reshape(n, 16, LANES)
             c = cos_ref[pl.ds(parity, n, stride=2)].reshape(n, 1, LANES)
             s = sin_ref[pl.ds(parity, n, stride=2)].reshape(n, 1, LANES) * sign
             f0 = c * b[:, :8] - s * b[:, 8:]
             f1 = c * b[:, 8:] + s * b[:, :8]
             if step < 2:
-                x_ref[0:n] = jnp.concatenate([f0, f1], axis=1).astype(BF16)
+                sample_ref[0:n] = jnp.concatenate([f0, f1], axis=1).astype(BF16)
             m = 17 - parity
             f0, f1 = f0[-first : -first + m], f1[-first : -first + m]
             images.append(lane_swap(f0 * pltpu.roll(f0, 4, 1) + f1 * pltpu.roll(f1, 4, 1)))
@@ -454,21 +485,33 @@
                 | ((number < -16) & has_l2)
                 | ((number >= 32) & has_r2)
             )
-            c_ref[0:m] = jnp.where(ok, coefs, 0.0).astype(BF16)
+            put_coefs(x_ref, jnp.where(ok, coefs, 0.0))
     for ref, half in ((keep_ref, second), (send_ref, 1 - second)):
-        for parity in range(2):
-            span = pl.ds(8 * half, 8)
-            top = jnp.where(row3, image_ref[0, parity, span], image_ref[1, parity, span])
-            ref[parity] = jnp.concatenate([top, image_ref[2, parity, span]], axis=1).astype(BF16)
+        span = pl.ds(8 * half, 8)
+        tops = [
+            jnp.where(row3, image_ref[0, parity, span], image_ref[1, parity, span])
+            for parity in range(2)
+        ]
+        ref[0:8] = jnp.concatenate(tops, axis=1).astype(BF16)
+        last = jnp.where(row3, image_ref[2, 0, span], image_ref[2, 1, span])
+        ref[8:12] = last.reshape(4, 16, LANES).astype(BF16)
+
+
+def image_rows(tiles, step, block):
+    q, parity = divmod(block, 2)
+    if step < 2:
+        row = 8 * parity + 4 * step
+        return tiles[q, row : row + 4]
+    row = 8 * (q % 2) + 4 * parity
+    return tiles[8 + q // 2, row : row + 4]
 
 
 def final_kernel(a_ref, b_ref, out_ref):
     total = a_ref[...].astype(F32) + b_ref[...].astype(F32)
-    for parity in range(2):
-        for q in range(8):
-            cut = slice(WINDOW * (2 * q + parity), WINDOW * (2 * q + parity + 1))
-            for n in range(STEPS):
-                out_ref[n, :, cut] = total[parity, q, 4 * n : 4 * n + 4]
+    for block in range(out_ref.shape[-1] // WINDOW):
+        cut = slice(WINDOW * block, WINDOW * (block + 1))
+        for n in range(STEPS):
+            out_ref[n, :, cut] = image_rows(total, n, block)
 
 
 def matching(size, by, odd):
@@ -489,7 +532,6 @@
     first, forward, inverse = (jnp.asarray(m, BF16) for m in pair_matrices())
     vmem = pl.BlockSpec(memory_space=pltpu.VMEM)
     hbm = pl.BlockSpec(memory_space=pltpu.HBM)
-    smem = pl.BlockSpec(memory_space=pltpu.SMEM)
 
     def tiles(n):
         return jax.ShapeDtypeStruct((n, 16, LANES), BF16)
@@ -525,43 +567,49 @@
     near, far_a, far_b, last = pl.pallas_call(
         unit_kernel,
         out_shape=(tiles(near_n), tiles(far_n), tiles(far_n), tiles(4)),
-        in_specs=[vmem] * 3 + [smem],
+        in_specs=[vmem] * 4,
         out_specs=(vmem,) * 4,
         compiler_params=pltpu.CompilerParams(vmem_limit_bytes=4 << 20),
         name="unit",
-    )(keep, send, got, frequency_scale)
+    )(keep, send, got, frequency_scale[None])
     a1 = lax.ppermute(near, "lat", matching(lat, 2, 0))
     b1 = lax.ppermute(near, "lat", matching(lat, 2, 1))
     a2 = lax.ppermute(far_a, "lat", matching(lat, 4, 0))
     b2 = lax.ppermute(far_b, "lat", matching(lat, 4, 1))
     inner_n = INNER[1] - INNER[0]
     table = propagator_table[0]
+    weights = pl.pallas_call(
+        weight_kernel,
+        out_shape=jax.ShapeDtypeStruct((3, table.shape[0] // 2) + table.shape[1:], BF16),
+        in_specs=[vmem],
+        out_specs=vmem,
+        compiler_params=pltpu.CompilerParams(vmem_limit_bytes=16 << 20),
+        cost_estimate=pl.CostEstimate(flops=10**8, bytes_accessed=10**7, transcendentals=0),
+        name="weights",
+    )(table)
     inner = pl.pallas_call(
         lambda *refs: inner_kernel(lat // 2, *refs),
         out_shape=tiles(inner_n),
         in_specs=[vmem] * 4,
         out_specs=vmem,
         scratch_shapes=[
-            pltpu.VMEM((46, 16, LANES), BF16),
-            pltpu.VMEM((inner_n, 16, LANES), F32),
-            pltpu.VMEM((inner_n, 16, LANES), F32),
+            pltpu.VMEM((3, 2, 23, 16, LANES), BF16),
+            pltpu.VMEM((3, inner_n, 8, LANES), F32),
             pltpu.VMEM((48, LANES), F32),
         ],
         compiler_params=pltpu.CompilerParams(vmem_limit_bytes=24 << 20),
         cost_estimate=pl.CostEstimate(flops=2 * 10**9, bytes_accessed=10**7, transcendentals=0),
         name="inner",
-    )(near, a1, b1, table)
-    image = jax.ShapeDtypeStruct((2, pairs, 16, LANES), BF16)
+    )(near, a1, b1, weights)
     own, other = pl.pallas_call(
         lambda *refs: main_kernel(lat // 2, *refs),
-        out_shape=(image, image),
+        out_shape=(tiles(12),) * 2,
         in_specs=[vmem] * 10,
-        out_specs=(vmem, vmem),
+        out_specs=(vmem,) * 2,
         scratch_shapes=[
-            pltpu.VMEM((68, 16, LANES), BF16),
+            pltpu.VMEM((3, 2, 34, 16, LANES), BF16),
             pltpu.VMEM((53, 16, LANES), BF16),
-            pltpu.VMEM((34, 16, LANES), F32),
-            pltpu.VMEM((34, 16, LANES), F32),
+            pltpu.VMEM((3, 34, 8, LANES), F32),
             pltpu.VMEM((52, 16, LANES), BF16),
             pltpu.VMEM((52, 16, LANES), BF16),
             pltpu.VMEM((STEPS, 128, LANES), F32),
@@ -572,7 +620,7 @@
         ],
         compiler_params=pltpu.CompilerParams(vmem_limit_bytes=32 << 20),
         name="steps",
-    )(near, last, a1, b1, a2, b2, table, forward, inverse, inner)
+    )(near, last, a1, b1, a2, b2, weights, forward, inverse, inner)
     swapped = lax.ppermute(other, "lat", partner)
     core = lax.rem(lax.axis_index("lat"), 2)
     if freqs == 2:
@@ -583,16 +631,18 @@
         return pl.pallas_call(
             final_kernel,
             out_shape=jax.ShapeDtypeStruct((STEPS, sources // 2, points), F32),
-            in_specs=[vmem, vmem],
+            in_specs=[vmem] * 2,
             out_specs=vmem,
             compiler_params=pltpu.CompilerParams(vmem_limit_bytes=4 << 20),
             name="total",
         )(stay, come)
-    low = jnp.where(core == 0, own, swapped)
-    high = jnp.where(core == 0, swapped, own)
-    whole = jnp.stack([low, high])[:, :, :, : 4 * STEPS]
-    whole = whole.reshape(2, 2, pairs, STEPS, 4, LANES)
-    whole = jnp.transpose(whole, (3, 0, 4, 2, 1, 5)).reshape(STEPS, sources, points)
+    parts = [jnp.where(core == 0, own, swapped), jnp.where(core == 0, swapped, own)]
+    rows = [
+        [jnp.stack([image_rows(p, n, b) for b in range(2 * pairs)], axis=1) for p in parts]
+        for n in range(STEPS)
+    ]
+    whole = jnp.stack([jnp.concatenate(r, axis=0) for r in rows])
+    whole = whole.reshape(STEPS, sources, points)
     return lax.psum_scatter(whole, "freq", scatter_dimension=1, tiled=True).astype(F32)
 
 
@@ -604,6 +654,7 @@
         P(None, "lat"),
         P("freq"),
     )
+
     return jax.shard_map(
         on_device, mesh=mesh, in_specs=placed, out_specs=P(None, "freq", "lat"), check_vma=False
     )

time: 29.4 us -> 28 us (0.952)
  the two profiles are of different devices: /device:TPU:28 before, /device:TPU:10 now
where the time goes in v5:
time: 28 us; the launch traced here: 27.8 us
  Pallas kernels  11.2 us (40%)
  starting transfers between devices  10.5 us (38%)
  waiting for transfers between devices  5.44 us (19%)
  between operations  0.76 us (3%)
    pallas_call x1, Pallas kernels, on_device(): pl.pallas_call(lambda *refs: main_kernel(lat // 2, *refs), out_shape=(til...  6.37 us
    ppermute x1, starting transfers between devices, on_device(): b1 = lax.ppermute(near, 'lat', matching(lat, 2, 1))  4.4 us
    ppermute x1, starting transfers between devices, on_device(): b2 = lax.ppermute(far_b, 'lat', matching(lat, 4, 1))  3.2 us
    ppermute x1, waiting for transfers between devices, on_device(): come = lax.ppermute(leave, 'freq', [(0, 1), (1, 0)])  2.56 us
    pallas_call x1, Pallas kernels, on_device(): pl.pallas_call(lambda *refs: inner_kernel(lat // 2, *refs), out_shape=til...  1.89 us
    ppermute x1, starting transfers between devices, on_device(): come = lax.ppermute(leave, 'freq', [(0, 1), (1, 0)])  1.59 us
    pallas_call x1, Pallas kernels, on_device(): pl.pallas_call(prep_kernel, out_shape=(tiles(pairs + 2), tiles(pairs + 2...  1.42 us
    ppermute x1, waiting for transfers between devices, on_device(): swapped = lax.ppermute(other, 'lat', partner)  1.21 us
  transfers between devices with their start and end apart: 7, of which 4 were waited for; matrix products, arithmetic and copies ran while one was open for 0% of the time, Pallas kernels for 9%

profile of v5, /device:TPU:10, one launch (start us, length us, event | category | flops | bytes accessed | tf_op | source)
XLA Modules:
  0.0 27.8 jit_solution(779362130067429728)
XLA Ops:
  0.0 0.0 copy-start
  0.0 1.4 %prep.1 = (bf16[10,16,128]{2,1,0:T(8,128)(2,1)S(1)}, bf16[18,16,128]{2,1,0:T(8,128)(2,1)S(1)}) custom-call(f32[4,1,8,2048]{3,2,1,0:T(8,128)} %wave_hbm.1, f32[3,2048]{1,0:T(4,128)} %slow_hbm.1, s32[3,16]{1,0:T(4,128)} %index_hbm.1, bf16[512,128]{1,0:T(8,128)(2,1)} %constant.19.clone.first_hbm), custom_call_target="tpu_custom_call" | custom-call | flops 1000000000 | bytes 10000000 | tf_op jit(solution)/shard_map/prep/pallas_call | solution.py:540
  1.4 0.1 collective-permute-start
  2.2 0.6 %collective-permute-done.got_ref = bf16[18,16,128]{2,1,0:T(8,128)(2,1)S(1)} collective-permute-done((bf16[18,16,128]{2,1,0:T(8,128)(2,1)S(1)}, bf16[18,16,128]{2,1,0:T(8,128)(2,1)S(1)}, u32[]{:S(2)}, u32[]{:S(2)}) %collective-permute-start) | collective-permute-done | bytes 73760 | tf_op jit(solution)/shard_map/ppermute | solution.py:564
  2.8 0.1 unit.1
  2.9 0.6 %collective-permute-start.1 = (bf16[29,16,128]{2,1,0:T(8,128)(2,1)S(1)}, bf16[29,16,128]{2,1,0:T(8,128)(2,1)S(1)}, u32[]{:S(2)}, u32[]{:S(2)}) collective-permute-start(bf16[29,16,128]{2,1,0:T(8,128)(2,1)S(1)} %get-tuple-element.15.refs_0_), channel_id=1, source_target_pairs={{0,4},{2,6},{4,0},{6,2},{8,12},{10,14},{12,8},{14,10},{16,20},{18,... | collective-permute-start | bytes 356360 | tf_op jit(solution)/shard_map/ppermute | solution.py:575
  3.5 4.4 %collective-permute-start.2 = (bf16[29,16,128]{2,1,0:T(8,128)(2,1)S(1)}, bf16[29,16,128]{2,1,0:T(8,128)(2,1)S(1)}, u32[]{:S(2)}, u32[]{:S(2)}) collective-permute-start(bf16[29,16,128]{2,1,0:T(8,128)(2,1)S(1)} %get-tuple-element.15.refs_0_), channel_id=1, source_target_pairs={{0,0},{2,2},{4,8},{6,10},{8,4},{10,6},{12,16},{14,18},{16,12},{18,... | collective-permute-start | bytes 356360 | tf_op jit(solution)/shard_map/ppermute | solution.py:576
  7.9 0.0 copy-done
  7.9 0.7 %weights.1.refs_3_.refs_6_ = bf16[3,2,2112,128]{3,2,1,0:T(8,128)(2,1)S(1)} custom-call(bf16[4,2112,128]{2,1,0:T(8,128)(2,1)S(1)} %bitcast.3), custom_call_target="tpu_custom_call" | custom-call | flops 100000000 | bytes 10000000 | tf_op jit(solution)/shard_map/weights/pallas_call | solution.py:581
  8.6 0.5 %collective-permute-start.3 = (bf16[14,16,128]{2,1,0:T(8,128)(2,1)S(1)}, bf16[14,16,128]{2,1,0:T(8,128)(2,1)S(1)}, u32[]{:S(2)}, u32[]{:S(2)}) collective-permute-start(bf16[14,16,128]{2,1,0:T(8,128)(2,1)S(1)} %get-tuple-element.17), channel_id=1, source_target_pairs={{0,8},{2,10},{4,12},{6,14},{8,0},{10,2},{12,4},{14,6},{16,24},{18,... | collective-permute-start | bytes 172040 | tf_op jit(solution)/shard_map/ppermute | solution.py:577
  9.1 0.0 copy-start.1
  9.1 0.0 copy-start.2
  9.1 3.2 %collective-permute-start.4 = (bf16[14,16,128]{2,1,0:T(8,128)(2,1)S(1)}, bf16[14,16,128]{2,1,0:T(8,128)(2,1)S(1)}, u32[]{:S(2)}, u32[]{:S(2)}) collective-permute-start(bf16[14,16,128]{2,1,0:T(8,128)(2,1)S(1)} %get-tuple-element.18), channel_id=1, source_target_pairs={{0,0},{2,2},{4,4},{6,6},{8,16},{10,18},{12,20},{14,22},{16,8},{18,... | collective-permute-start | bytes 172040 | tf_op jit(solution)/shard_map/ppermute | solution.py:578
  12.3 0.0 collective-permute-done.1.refs_1_.refs_2_
  12.4 0.0 collective-permute-done.2.refs_2_.refs_3_
  12.4 1.9 %inner.1.refs_9_ = bf16[28,16,128]{2,1,0:T(8,128)(2,1)S(1)} custom-call(bf16[29,16,128]{2,1,0:T(8,128)(2,1)S(1)} %get-tuple-element.15.refs_0_, bf16[29,16,128]{2,1,0:T(8,128)(2,1)S(1)} %collective-permute-done.1.refs_1_.refs_2_, bf16[29,16,128]{2,1,0:T(8,128)(2,1)S(1)} %collective-permute-done.2.refs_2_.refs_3_, ...), custom_call_target="tpu_custom_call" | custom-call | flops 2000000000 | bytes 10000000 | tf_op jit(solution)/shard_map/inner/pallas_call | solution.py:590
  14.3 0.0 collective-permute-done.3.refs_4_
  14.3 1.1 %collective-permute-done.4.refs_5_ = bf16[14,16,128]{2,1,0:T(8,128)(2,1)S(1)} collective-permute-done((bf16[14,16,128]{2,1,0:T(8,128)(2,1)S(1)}, bf16[14,16,128]{2,1,0:T(8,128)(2,1)S(1)}, u32[]{:S(2)}, u32[]{:S(2)}) %collective-permute-start.4) | collective-permute-done | bytes 57376 | tf_op jit(solution)/shard_map/ppermute | solution.py:578
  15.3 0.0 copy-done.1
  15.3 0.0 copy-done.2
  15.3 6.4 %steps.1 = (bf16[12,16,128]{2,1,0:T(8,128)(2,1)S(1)}, bf16[12,16,128]{2,1,0:T(8,128)(2,1)S(1)}) custom-call(bf16[29,16,128]{2,1,0:T(8,128)(2,1)S(1)} %get-tuple-element.15.refs_0_, bf16[4,16,128]{2,1,0:T(8,128)(2,1)S(1)} %get-tuple-element.16.refs_1_, bf16[29,16,128]{2,1,0:T(8,128)(2,1)S(1)} %collective-permute-done.1.refs_1_.refs_2_, ...), custom_call_target="tpu_custom_call" | custom-call | tf_op jit(solution)/shard_map/steps/pallas_call | solution.py:604
  21.7 0.1 collective-permute-start.5
  21.8 1.2 %collective-permute-done.5 = bf16[12,16,128]{2,1,0:T(8,128)(2,1)S(1)} collective-permute-done((bf16[12,16,128]{2,1,0:T(8,128)(2,1)S(1)}, bf16[12,16,128]{2,1,0:T(8,128)(2,1)S(1)}, u32[]{:S(2)}, u32[]{:S(2)}) %collective-permute-start.5) | collective-permute-done | bytes 49184 | tf_op jit(solution)/shard_map/ppermute | solution.py:624
  23.0 1.6 %collective-permute-start.6 = (bf16[12,16,128]{2,1,0:T(8,128)(2,1)S(1)}, bf16[12,16,128]{2,1,0:T(8,128)(2,1)S(1)}, u32[]{:S(2)}, u32[]{:S(2)}) collective-permute-start(bf16[12,16,128]{2,1,0:T(8,128)(2,1)S(1)} %get-tuple-element.21), channel_id=1, source_target_pairs={{0,1},{1,0},{2,3},{3,2},{4,5},{5,4},{6,7},{7,6},{8,9},{9,8},{10,11... | collective-permute-start | bytes 147464 | tf_op jit(solution)/shard_map/ppermute | solution.py:630
  24.6 2.6 %collective-permute-done.6.b_ref = bf16[12,16,128]{2,1,0:T(8,128)(2,1)S(1)} collective-permute-done((bf16[12,16,128]{2,1,0:T(8,128)(2,1)S(1)}, bf16[12,16,128]{2,1,0:T(8,128)(2,1)S(1)}, u32[]{:S(2)}, u32[]{:S(2)}) %collective-permute-start.6) | collective-permute-done | bytes 49184 | tf_op jit(solution)/shard_map/ppermute | solution.py:630
  27.2 0.7 %total.1 = f32[3,4,2048]{2,1,0:T(4,128)} custom-call(bf16[12,16,128]{2,1,0:T(8,128)(2,1)S(1)} %get-tuple-element.22.a_ref, bf16[12,16,128]{2,1,0:T(8,128)(2,1)S(1)} %collective-permute-done.6.b_ref), custom_call_target="tpu_custom_call" | custom-call | tf_op jit(solution)/shard_map/total/pallas_call | solution.py:631
  (1 shorter events, 0.0 us)
Async XLA Ops:
  0.0 7.9 %copy-start = (bf16[1,4,2112,128]{3,2,1,0:T(8,128)(2,1)S(1)}, bf16[1,4,2112,128]{3,2,1,0:T(8,128)(2,1)}, u32[]{:S(2)}) copy-start(bf16[1,4,2112,128]{3,2,1,0:T(8,128)(2,1)} %param.9) | copy-start | bytes 6488068
  1.4 1.3 %collective-permute-start = (bf16[18,16,128]{2,1,0:T(8,128)(2,1)S(1)}, bf16[18,16,128]{2,1,0:T(8,128)(2,1)S(1)}, u32[]{:S(2)}, u32[]{:S(2)}) collective-permute-start(bf16[18,16,128]{2,1,0:T(8,128)(2,1)S(1)} %get-tuple-element.14.sent_ref), channel_id=1, source_target_pairs={{0,2},{2,0},{4,6},{6,4},{8,10},{10,8},{12,14},{14,12},{16,18},{18,... | collective-permute-start | bytes 221192 | tf_op jit(solution)/shard_map/ppermute | solution.py:564
  2.9 9.5 %collective-permute-start.1 = (bf16[29,16,128]{2,1,0:T(8,128)(2,1)S(1)}, bf16[29,16,128]{2,1,0:T(8,128)(2,1)S(1)}, u32[]{:S(2)}, u32[]{:S(2)}) collective-permute-start(bf16[29,16,128]{2,1,0:T(8,128)(2,1)S(1)} %get-tuple-element.15.refs_0_), channel_id=1, source_target_pairs={{0,4},{2,6},{4,0},{6,2},{8,12},{10,14},{12,8},{14,10},{16,20},{18,... | collective-permute-start | bytes 356360 | tf_op jit(solution)/shard_map/ppermute | solution.py:575
  3.5 8.9 %collective-permute-start.2 = (bf16[29,16,128]{2,1,0:T(8,128)(2,1)S(1)}, bf16[29,16,128]{2,1,0:T(8,128)(2,1)S(1)}, u32[]{:S(2)}, u32[]{:S(2)}) collective-permute-start(bf16[29,16,128]{2,1,0:T(8,128)(2,1)S(1)} %get-tuple-element.15.refs_0_), channel_id=1, source_target_pairs={{0,0},{2,2},{4,8},{6,10},{8,4},{10,6},{12,16},{14,18},{16,12},{18,... | collective-permute-start | bytes 356360 | tf_op jit(solution)/shard_map/ppermute | solution.py:576
  8.6 5.6 %collective-permute-start.3 = (bf16[14,16,128]{2,1,0:T(8,128)(2,1)S(1)}, bf16[14,16,128]{2,1,0:T(8,128)(2,1)S(1)}, u32[]{:S(2)}, u32[]{:S(2)}) collective-permute-start(bf16[14,16,128]{2,1,0:T(8,128)(2,1)S(1)} %get-tuple-element.17), channel_id=1, source_target_pairs={{0,8},{2,10},{4,12},{6,14},{8,0},{10,2},{12,4},{14,6},{16,24},{18,... | collective-permute-start | bytes 172040 | tf_op jit(solution)/shard_map/ppermute | solution.py:577
  9.1 6.2 %copy-start.1 = (bf16[256,256]{1,0:T(8,128)(2,1)S(1)}, bf16[256,256]{1,0:T(8,128)(2,1)}, u32[]{:S(2)}) copy-start(bf16[256,256]{1,0:T(8,128)(2,1)} %constant.21.clone.refs_8_) | copy-start | bytes 393220
  9.1 6.2 %copy-start.2 = (bf16[384,128]{1,0:T(8,128)(2,1)S(1)}, bf16[384,128]{1,0:T(8,128)(2,1)}, u32[]{:S(2)}) copy-start(bf16[384,128]{1,0:T(8,128)(2,1)} %constant.20.clone.refs_7_) | copy-start | bytes 294916
  9.1 6.2 %collective-permute-start.4 = (bf16[14,16,128]{2,1,0:T(8,128)(2,1)S(1)}, bf16[14,16,128]{2,1,0:T(8,128)(2,1)S(1)}, u32[]{:S(2)}, u32[]{:S(2)}) collective-permute-start(bf16[14,16,128]{2,1,0:T(8,128)(2,1)S(1)} %get-tuple-element.18), channel_id=1, source_target_pairs={{0,0},{2,2},{4,4},{6,6},{8,16},{10,18},{12,20},{14,22},{16,8},{18,... | collective-permute-start | bytes 172040 | tf_op jit(solution)/shard_map/ppermute | solution.py:578
  21.7 1.3 %collective-permute-start.5 = (bf16[12,16,128]{2,1,0:T(8,128)(2,1)S(1)}, bf16[12,16,128]{2,1,0:T(8,128)(2,1)S(1)}, u32[]{:S(2)}, u32[]{:S(2)}) collective-permute-start(bf16[12,16,128]{2,1,0:T(8,128)(2,1)S(1)} %get-tuple-element.20), channel_id=1, source_target_pairs={{0,2},{2,0},{4,6},{6,4},{8,10},{10,8},{12,14},{14,12},{16,18},{18,... | collective-permute-start | bytes 147464 | tf_op jit(solution)/shard_map/ppermute | solution.py:624
  23.0 4.2 %collective-permute-start.6 = (bf16[12,16,128]{2,1,0:T(8,128)(2,1)S(1)}, bf16[12,16,128]{2,1,0:T(8,128)(2,1)S(1)}, u32[]{:S(2)}, u32[]{:S(2)}) collective-permute-start(bf16[12,16,128]{2,1,0:T(8,128)(2,1)S(1)} %get-tuple-element.21), channel_id=1, source_target_pairs={{0,1},{1,0},{2,3},{3,2},{4,5},{5,4},{6,7},{7,6},{8,9},{9,8},{10,11... | collective-permute-start | bytes 147464 | tf_op jit(solution)/shard_map/ppermute | solution.py:630

commit v6 on v5

--- a/solution.py
+++ b/solution.py
@@ -158,7 +158,7 @@
     send_ref[0 : pairs + 2] = both_ref[1 - core]
 
 
-def unit_kernel(keep_ref, sent_ref, got_ref, scale_ref, near_ref, far_a_ref, far_b_ref, last_ref):
+def unit_kernel(keep_ref, sent_ref, got_ref, scale_ref, near_ref, far_a_ref, far_b_ref, own_ref):
     place = lax.axis_index("lat")
     second = lax.rem(place, 2) == 1
     n = keep_ref.shape[0]
@@ -169,30 +169,31 @@
     i0 = jnp.where(second, got_i, own_i)
     i1 = jnp.where(second, own_i, got_i)
     unit = jnp.concatenate([b0[: n - 2], b0[n - 2 :] + b1[:2], b1[2:]], axis=0)
-    near_ref[0 : 2 * n - 2] = unit.astype(BF16)
-    at = 2 * n - 2
+    near_ref[0] = jnp.where(low_lanes((16, LANES)), unit[2 * n - 3], unit[0]).astype(BF16)
+    near_ref[1 : 2 * n - 3] = unit[1 : 2 * n - 3].astype(BF16)
+    at = 2 * n - 3
+    phases = []
     for step in range(STEPS):
-        ref, to = (near_ref, at) if step < 2 else (last_ref, 0)
         for block, info in enumerate((i0, i1)):
             theta = scale_ref[...] * (info[2 * step] + info[2 * step + 1])
-            high = theta.astype(BF16)
-            ref[to + block] = high
-            ref[to + 2 + block] = (theta - high.astype(F32)).astype(BF16)
-        if step < 2:
-            at += 4
+            own_ref[step, 16 * block : 16 * block + 16] = theta
+            turns = jnp.floor(theta * np.float32(0.5 / math.pi) + np.float32(0.5))
+            theta = theta - turns * np.float32(6.28125)
+            theta = theta - turns * np.float32(2.0 * math.pi - 6.28125)
+            phases.append(theta)
+            if step < 2:
+                near_ref[at + 2 * step + block] = theta.astype(BF16)
+    at += 4
     near_ref[at] = jnp.concatenate([i0[6, :8], i1[6, :8]], axis=0).astype(BF16)
     near_ref[at + 1] = jnp.concatenate([i0[6, 8:], i1[6, 8:]], axis=0).astype(BF16)
     near_ref[at + 2] = jnp.concatenate([i0[7, :8], i1[7, :8]], axis=0).astype(BF16)
     even_quad = lax.rem(lax.div(place, 4), 2) == 0
-    count = far_a_ref.shape[0] - 3
-    base = 2 * n - 2
+    count = far_a_ref.shape[0] - 1
+    top = jnp.concatenate([phases[1][8:], i1[6, :8]], axis=0)
+    bottom = jnp.concatenate([phases[0][:8], i0[6, :8]], axis=0)
     for ref, right in ((far_a_ref, even_quad), (far_b_ref, jnp.logical_not(even_quad))):
-        start = jnp.where(right, base - count, 0)
-        pick = jnp.where(right, 1, 0)
-        ref[0:count] = near_ref[pl.ds(start, count)]
-        ref[count] = near_ref[base + pick]
-        ref[count + 1] = near_ref[base + 2 + pick]
-        ref[count + 2] = near_ref[base + 8]
+        ref[0:count] = jnp.where(right, unit[2 * n - 2 - count :], unit[:count]).astype(BF16)
+        ref[count] = jnp.where(right, top, bottom).astype(BF16)
 
 
 def sign_rows():
@@ -208,8 +209,16 @@
     return jnp.where(flag, x_ref[lo:hi], y_ref[lo:hi]).astype(F32)
 
 
+def whole_unit(tiles):
+    low = low_lanes((1, 16, LANES))
+    edge = tiles[0:1]
+    return jnp.concatenate(
+        [jnp.where(low, 0.0, edge), tiles[1:], jnp.where(low, edge, 0.0)], axis=0
+    )
+
+
 def middle_coefs(near_ref, left, right, has_l1, has_r1, coef_n):
-    own = near_ref[0:coef_n].astype(F32)
+    own = whole_unit(near_ref[0 : coef_n - 1].astype(F32))
     return [
         left[2 : coef_n - 2],
         left[coef_n - 2 :] + jnp.concatenate([valid(has_l1, own[0:1]), own[1:2]], axis=0),
@@ -288,11 +297,11 @@
     odd_unit = lax.rem(unit, 2) == 1
     has_l1, has_r1 = unit >= 1, unit + 1 < units
     coef_n = 18
-    left = valid(has_l1, choose(odd_unit, a1_ref, b1_ref, 0, coef_n))
-    right = valid(has_r1, choose(odd_unit, b1_ref, a1_ref, 0, coef_n))
+    left = valid(has_l1, whole_unit(choose(odd_unit, a1_ref, b1_ref, 0, coef_n - 1)))
+    right = valid(has_r1, whole_unit(choose(odd_unit, b1_ref, a1_ref, 0, coef_n - 1)))
     middle = middle_coefs(near_ref, left, right, has_l1, has_r1, coef_n)
     put_coefs(x_ref, jnp.concatenate(middle, axis=0))
-    pos = coef_n + 8
+    pos = coef_n + 3
     pick_ref[0:16] = jnp.where(has_l1, choose(odd_unit, a1_ref, b1_ref, pos, pos + 1)[0], -1.0)
     pick_ref[16:32] = near_ref[pos].astype(F32)
     pick_ref[32:48] = jnp.where(has_r1, choose(odd_unit, b1_ref, a1_ref, pos, pos + 1)[0], -1.0)
@@ -305,7 +314,7 @@
 def main_kernel(
     units,
     near_ref,
-    last_ref,
+    own_ref,
     a1_ref,
     b1_ref,
     a2_ref,
@@ -336,10 +345,10 @@
     has_r1, has_r2 = unit + 1 < units, unit + 2 < units
     pairs = 16
     coef_n = pairs + 2
-    far_n = a2_ref.shape[0] - 3
-
-    left = valid(has_l1, choose(odd_unit, a1_ref, b1_ref, 0, coef_n))
-    right = valid(has_r1, choose(odd_unit, b1_ref, a1_ref, 0, coef_n))
+    far_n = a2_ref.shape[0] - 1
+
+    left = valid(has_l1, whole_unit(choose(odd_unit, a1_ref, b1_ref, 0, coef_n - 1)))
+    right = valid(has_r1, whole_unit(choose(odd_unit, b1_ref, a1_ref, 0, coef_n - 1)))
     left2 = valid(has_l2, choose(odd_quad, a2_ref, b2_ref, 0, far_n))
     right2 = valid(has_r2, choose(odd_quad, b2_ref, a2_ref, 0, far_n))
     near_left = jnp.concatenate([valid(has_l2, left[0:1]), left[1:2]], axis=0)
@@ -356,37 +365,28 @@
         ),
     )
 
-    at = coef_n
     far_rows = 48
+    for step in range(STEPS):
+        slow_ref[step, far_rows : far_rows + 32] = own_ref[step]
     for step in range(2):
-        lo = at + 4 * step
+        lo = coef_n - 1 + 2 * step
         for flag, pos in ((odd_unit, -32), (jnp.logical_not(odd_unit), 32)):
-            hi_v = choose(flag, a1_ref, b1_ref, lo, lo + 2)
-            lo_v = choose(flag, a1_ref, b1_ref, lo + 2, lo + 4)
-            slow_ref[step, far_rows + pos : far_rows + pos + 32] = (hi_v + lo_v).reshape(32, LANES)
-        slow_ref[step, far_rows : far_rows + 32] = (
-            near_ref[lo : lo + 2].astype(F32) + near_ref[lo + 2 : lo + 4].astype(F32)
-        ).reshape(32, LANES)
-    for flag, pos in ((odd_quad, -48), (jnp.logical_not(odd_quad), 64)):
-        rows = choose(flag, a2_ref, b2_ref, far_n, far_n + 1) + choose(
-            flag, a2_ref, b2_ref, far_n + 1, far_n + 2
-        )
-        slow_ref[0, far_rows + pos : far_rows + pos + 16] = rows[0]
-    slow_ref[2, far_rows : far_rows + 32] = (
-        last_ref[0:2].astype(F32) + last_ref[2:4].astype(F32)
-    ).reshape(32, LANES)
+            rows = choose(flag, a1_ref, b1_ref, lo, lo + 2)
+            slow_ref[step, far_rows + pos : far_rows + pos + 32] = rows.reshape(32, LANES)
+    before2 = choose(odd_quad, a2_ref, b2_ref, far_n, far_n + 1)[0]
+    after2 = choose(odd_quad, b2_ref, a2_ref, far_n, far_n + 1)[0]
+    slow_ref[0, far_rows - 40 : far_rows - 32] = before2[:8]
+    slow_ref[0, far_rows + 64 : far_rows + 72] = after2[:8]
 
     for step in range(STEPS):
-        pos = coef_n + 8 + step
+        pos = coef_n + 3 + step
         pick_ref[step, 32:48] = near_ref[pos].astype(F32)
         pick_ref[step, 16:32] = jnp.where(
             has_l1, choose(odd_unit, a1_ref, b1_ref, pos, pos + 1)[0], -1.0)
         pick_ref[step, 48:64] = jnp.where(
             has_r1, choose(odd_unit, b1_ref, a1_ref, pos, pos + 1)[0], -1.0)
-    pick_ref[0, 0:16] = jnp.where(
-        has_l2, choose(odd_quad, a2_ref, b2_ref, far_n + 2, far_n + 3)[0], -1.0)
-    pick_ref[0, 64:80] = jnp.where(
-        has_r2, choose(odd_quad, b2_ref, a2_ref, far_n + 2, far_n + 3)[0], -1.0)
+    pick_ref[0, 8:16] = jnp.where(has_l2, before2[8:], -1.0)
+    pick_ref[0, 64:72] = jnp.where(has_r2, after2[8:], -1.0)
 
     sign = sign_rows()
     row3 = lax.broadcasted_iota(jnp.int32, (1, 8, LANES), 1) < 4
@@ -519,7 +519,7 @@
     for i in range(size):
         right = (i // by) % 2 == odd
         j = i + by if right else i - by
-        pairs.append((i, j if 0 <= j < size else i))
+        pairs.append((i, j if 0 <= j < size else i ^ 1))
     return pairs
 
 
@@ -562,11 +562,16 @@
     )
     partner = [(i, i ^ 1) for i in range(lat)]
     got = lax.ppermute(send, "lat", partner)
-    near_n = 2 * (pairs + 2) - 2 + 8 + STEPS
-    far_n = 11 + 3
-    near, far_a, far_b, last = pl.pallas_call(
+    near_n = 2 * (pairs + 2) - 3 + 4 + STEPS
+    far_n = 11 + 1
+    near, far_a, far_b, phases = pl.pallas_call(
         unit_kernel,
-        out_shape=(tiles(near_n), tiles(far_n), tiles(far_n), tiles(4)),
+        out_shape=(
+            tiles(near_n),
+            tiles(far_n),
+            tiles(far_n),
+            jax.ShapeDtypeStruct((STEPS, 4 * pairs, LANES), F32),
+        ),
         in_specs=[vmem] * 4,
         out_specs=(vmem,) * 4,
         compiler_params=pltpu.CompilerParams(vmem_limit_bytes=4 << 20),
@@ -620,7 +625,7 @@
         ],
         compiler_params=pltpu.CompilerParams(vmem_limit_bytes=32 << 20),
         name="steps",
-    )(near, last, a1, b1, a2, b2, weights, forward, inverse, inner)
+    )(near, phases, a1, b1, a2, b2, weights, forward, inverse, inner)
     swapped = lax.ppermute(other, "lat", partner)
     core = lax.rem(lax.axis_index("lat"), 2)
     if freqs == 2:

time: 28 us -> 24.9 us (0.89)
  the two profiles are of different devices: /device:TPU:10 before, /device:TPU:28 now
where the time goes in v6:
time: 24.9 us; the launch traced here: 24.8 us
  Pallas kernels  11.1 us (45%)
  waiting for transfers between devices  9.77 us (39%)
  starting transfers between devices  3.17 us (13%)
  between operations  0.75 us (3%)
    pallas_call x1, Pallas kernels, on_device(): pl.pallas_call(lambda *refs: main_kernel(lat // 2, *refs), out_shape=(til...  6.32 us
    ppermute x1, waiting for transfers between devices, on_device(): come = lax.ppermute(leave, 'freq', [(0, 1), (1, 0)])  3.63 us
    ppermute x1, waiting for transfers between devices, on_device(): b1 = lax.ppermute(near, 'lat', matching(lat, 2, 1))  2.64 us
    pallas_call x1, Pallas kernels, on_device(): pl.pallas_call(lambda *refs: inner_kernel(lat // 2, *refs), out_shape=til...  1.85 us
    ppermute x1, waiting for transfers between devices, on_device(): a1 = lax.ppermute(near, 'lat', matching(lat, 2, 0))  1.68 us
    ppermute x1, starting transfers between devices, on_device(): a1 = lax.ppermute(near, 'lat', matching(lat, 2, 0))  1.56 us
    pallas_call x1, Pallas kernels, on_device(): pl.pallas_call(prep_kernel, out_shape=(tiles(pairs + 2), tiles(pairs + 2...  1.42 us
    ppermute x1, waiting for transfers between devices, on_device(): swapped = lax.ppermute(other, 'lat', partner)  1.21 us
  transfers between devices with their start and end apart: 7, of which 5 were waited for; matrix products, arithmetic and copies ran while one was open for 0% of the time, Pallas kernels for 10%

profile of v6, /device:TPU:28, one launch (start us, length us, event | category | flops | bytes accessed | tf_op | source)
XLA Modules:
  0.0 24.8 jit_solution(6261278520056444239)
XLA Ops:
  0.0 0.0 copy-start
  0.0 1.4 %prep.1 = (bf16[10,16,128]{2,1,0:T(8,128)(2,1)S(1)}, bf16[18,16,128]{2,1,0:T(8,128)(2,1)S(1)}) custom-call(f32[4,1,8,2048]{3,2,1,0:T(8,128)} %wave_hbm.1, f32[3,2048]{1,0:T(4,128)} %slow_hbm.1, s32[3,16]{1,0:T(4,128)} %index_hbm.1, bf16[512,128]{1,0:T(8,128)(2,1)} %constant.19.clone.first_hbm), custom_call_target="tpu_custom_call" | custom-call | flops 1000000000 | bytes 10000000 | tf_op jit(solution)/shard_map/prep/pallas_call | solution.py:540
  1.4 0.1 collective-permute-start
  2.2 0.6 %collective-permute-done.got_ref = bf16[18,16,128]{2,1,0:T(8,128)(2,1)S(1)} collective-permute-done((bf16[18,16,128]{2,1,0:T(8,128)(2,1)S(1)}, bf16[18,16,128]{2,1,0:T(8,128)(2,1)S(1)}, u32[]{:S(2)}, u32[]{:S(2)}) %collective-permute-start) | collective-permute-done | bytes 73760 | tf_op jit(solution)/shard_map/ppermute | solution.py:564
  2.8 0.1 unit.1
  2.9 1.6 %collective-permute-start.1 = (bf16[24,16,128]{2,1,0:T(8,128)(2,1)S(1)}, bf16[24,16,128]{2,1,0:T(8,128)(2,1)S(1)}, u32[]{:S(2)}, u32[]{:S(2)}) collective-permute-start(bf16[24,16,128]{2,1,0:T(8,128)(2,1)S(1)} %get-tuple-element.15.refs_0_), channel_id=1, source_target_pairs={{0,4},{2,6},{4,0},{6,2},{8,12},{10,14},{12,8},{14,10},{16,20},{18,... | collective-permute-start | bytes 294920 | tf_op jit(solution)/shard_map/ppermute | solution.py:580
  4.4 0.4 %collective-permute-start.2 = (bf16[24,16,128]{2,1,0:T(8,128)(2,1)S(1)}, bf16[24,16,128]{2,1,0:T(8,128)(2,1)S(1)}, u32[]{:S(2)}, u32[]{:S(2)}) collective-permute-start(bf16[24,16,128]{2,1,0:T(8,128)(2,1)S(1)} %get-tuple-element.15.refs_0_), channel_id=1, source_target_pairs={{0,2},{2,0},{4,8},{6,10},{8,4},{10,6},{12,16},{14,18},{16,12},{18,... | collective-permute-start | bytes 294920 | tf_op jit(solution)/shard_map/ppermute | solution.py:581
  4.8 0.0 copy-done
  4.8 0.7 %weights.1.refs_3_.refs_6_ = bf16[3,2,2112,128]{3,2,1,0:T(8,128)(2,1)S(1)} custom-call(bf16[4,2112,128]{2,1,0:T(8,128)(2,1)S(1)} %bitcast.3), custom_call_target="tpu_custom_call" | custom-call | flops 100000000 | bytes 10000000 | tf_op jit(solution)/shard_map/weights/pallas_call | solution.py:586
  5.6 0.5 %collective-permute-start.3 = (bf16[12,16,128]{2,1,0:T(8,128)(2,1)S(1)}, bf16[12,16,128]{2,1,0:T(8,128)(2,1)S(1)}, u32[]{:S(2)}, u32[]{:S(2)}) collective-permute-start(bf16[12,16,128]{2,1,0:T(8,128)(2,1)S(1)} %get-tuple-element.17), channel_id=1, source_target_pairs={{0,8},{2,10},{4,12},{6,14},{8,0},{10,2},{12,4},{14,6},{16,24},{18,... | collective-permute-start | bytes 147464 | tf_op jit(solution)/shard_map/ppermute | solution.py:582
  6.1 0.0 copy-start.1
  6.1 0.0 copy-start.2
  6.1 0.0 collective-permute-start.4
  6.1 1.7 %collective-permute-done.1.refs_1_.refs_2_ = bf16[24,16,128]{2,1,0:T(8,128)(2,1)S(1)} collective-permute-done((bf16[24,16,128]{2,1,0:T(8,128)(2,1)S(1)}, bf16[24,16,128]{2,1,0:T(8,128)(2,1)S(1)}, u32[]{:S(2)}, u32[]{:S(2)}) %collective-permute-start.1) | collective-permute-done | bytes 98336 | tf_op jit(solution)/shard_map/ppermute | solution.py:580
  7.8 2.6 %collective-permute-done.2.refs_2_.refs_3_ = bf16[24,16,128]{2,1,0:T(8,128)(2,1)S(1)} collective-permute-done((bf16[24,16,128]{2,1,0:T(8,128)(2,1)S(1)}, bf16[24,16,128]{2,1,0:T(8,128)(2,1)S(1)}, u32[]{:S(2)}, u32[]{:S(2)}) %collective-permute-start.2) | collective-permute-done | bytes 98336 | tf_op jit(solution)/shard_map/ppermute | solution.py:581
  10.4 1.9 %inner.1.refs_9_ = bf16[28,16,128]{2,1,0:T(8,128)(2,1)S(1)} custom-call(bf16[24,16,128]{2,1,0:T(8,128)(2,1)S(1)} %get-tuple-element.15.refs_0_, bf16[24,16,128]{2,1,0:T(8,128)(2,1)S(1)} %collective-permute-done.1.refs_1_.refs_2_, bf16[24,16,128]{2,1,0:T(8,128)(2,1)S(1)} %collective-permute-done.2.refs_2_.refs_3_, ...), custom_call_target="tpu_custom_call" | custom-call | flops 2000000000 | bytes 10000000 | tf_op jit(solution)/shard_map/inner/pallas_call | solution.py:595
  12.3 0.0 collective-permute-done.3.refs_4_
  12.3 0.0 collective-permute-done.4.refs_5_
  12.3 0.0 copy-done.1
  12.3 0.0 copy-done.2
  12.3 6.3 %steps.1 = (bf16[12,16,128]{2,1,0:T(8,128)(2,1)S(1)}, bf16[12,16,128]{2,1,0:T(8,128)(2,1)S(1)}) custom-call(bf16[24,16,128]{2,1,0:T(8,128)(2,1)S(1)} %get-tuple-element.15.refs_0_, f32[3,32,128]{2,1,0:T(8,128)S(1)} %get-tuple-element.16.refs_1_, bf16[24,16,128]{2,1,0:T(8,128)(2,1)S(1)} %collective-permute-done.1.refs_1_.refs_2_, ...), custom_call_target="tpu_custom_call" | custom-call | tf_op jit(solution)/shard_map/steps/pallas_call | solution.py:609
  18.6 0.1 collective-permute-start.5
  18.7 1.2 %collective-permute-done.5 = bf16[12,16,128]{2,1,0:T(8,128)(2,1)S(1)} collective-permute-done((bf16[12,16,128]{2,1,0:T(8,128)(2,1)S(1)}, bf16[12,16,128]{2,1,0:T(8,128)(2,1)S(1)}, u32[]{:S(2)}, u32[]{:S(2)}) %collective-permute-start.5) | collective-permute-done | bytes 49184 | tf_op jit(solution)/shard_map/ppermute | solution.py:629
  20.0 0.5 %collective-permute-start.6 = (bf16[12,16,128]{2,1,0:T(8,128)(2,1)S(1)}, bf16[12,16,128]{2,1,0:T(8,128)(2,1)S(1)}, u32[]{:S(2)}, u32[]{:S(2)}) collective-permute-start(bf16[12,16,128]{2,1,0:T(8,128)(2,1)S(1)} %get-tuple-element.21), channel_id=1, source_target_pairs={{0,1},{1,0},{2,3},{3,2},{4,5},{5,4},{6,7},{7,6},{8,9},{9,8},{10,11... | collective-permute-start | bytes 147464 | tf_op jit(solution)/shard_map/ppermute | solution.py:635
  20.5 3.6 %collective-permute-done.6.b_ref = bf16[12,16,128]{2,1,0:T(8,128)(2,1)S(1)} collective-permute-done((bf16[12,16,128]{2,1,0:T(8,128)(2,1)S(1)}, bf16[12,16,128]{2,1,0:T(8,128)(2,1)S(1)}, u32[]{:S(2)}, u32[]{:S(2)}) %collective-permute-start.6) | collective-permute-done | bytes 49184 | tf_op jit(solution)/shard_map/ppermute | solution.py:635
  24.1 0.7 %total.1 = f32[3,4,2048]{2,1,0:T(4,128)} custom-call(bf16[12,16,128]{2,1,0:T(8,128)(2,1)S(1)} %get-tuple-element.22.a_ref, bf16[12,16,128]{2,1,0:T(8,128)(2,1)S(1)} %collective-permute-done.6.b_ref), custom_call_target="tpu_custom_call" | custom-call | tf_op jit(solution)/shard_map/total/pallas_call | solution.py:636
  (1 shorter events, 0.0 us)
Async XLA Ops:
  0.0 4.8 %copy-start = (bf16[1,4,2112,128]{3,2,1,0:T(8,128)(2,1)S(1)}, bf16[1,4,2112,128]{3,2,1,0:T(8,128)(2,1)}, u32[]{:S(2)}) copy-start(bf16[1,4,2112,128]{3,2,1,0:T(8,128)(2,1)} %param.9) | copy-start | bytes 6488068
  1.4 1.3 %collective-permute-start = (bf16[18,16,128]{2,1,0:T(8,128)(2,1)S(1)}, bf16[18,16,128]{2,1,0:T(8,128)(2,1)S(1)}, u32[]{:S(2)}, u32[]{:S(2)}) collective-permute-start(bf16[18,16,128]{2,1,0:T(8,128)(2,1)S(1)} %get-tuple-element.14.sent_ref), channel_id=1, source_target_pairs={{0,2},{2,0},{4,6},{6,4},{8,10},{10,8},{12,14},{14,12},{16,18},{18,... | collective-permute-start | bytes 221192 | tf_op jit(solution)/shard_map/ppermute | solution.py:564
  2.9 4.9 %collective-permute-start.1 = (bf16[24,16,128]{2,1,0:T(8,128)(2,1)S(1)}, bf16[24,16,128]{2,1,0:T(8,128)(2,1)S(1)}, u32[]{:S(2)}, u32[]{:S(2)}) collective-permute-start(bf16[24,16,128]{2,1,0:T(8,128)(2,1)S(1)} %get-tuple-element.15.refs_0_), channel_id=1, source_target_pairs={{0,4},{2,6},{4,0},{6,2},{8,12},{10,14},{12,8},{14,10},{16,20},{18,... | collective-permute-start | bytes 294920 | tf_op jit(solution)/shard_map/ppermute | solution.py:580
  4.4 6.0 %collective-permute-start.2 = (bf16[24,16,128]{2,1,0:T(8,128)(2,1)S(1)}, bf16[24,16,128]{2,1,0:T(8,128)(2,1)S(1)}, u32[]{:S(2)}, u32[]{:S(2)}) collective-permute-start(bf16[24,16,128]{2,1,0:T(8,128)(2,1)S(1)} %get-tuple-element.15.refs_0_), channel_id=1, source_target_pairs={{0,2},{2,0},{4,8},{6,10},{8,4},{10,6},{12,16},{14,18},{16,12},{18,... | collective-permute-start | bytes 294920 | tf_op jit(solution)/shard_map/ppermute | solution.py:581
  5.6 6.7 %collective-permute-start.3 = (bf16[12,16,128]{2,1,0:T(8,128)(2,1)S(1)}, bf16[12,16,128]{2,1,0:T(8,128)(2,1)S(1)}, u32[]{:S(2)}, u32[]{:S(2)}) collective-permute-start(bf16[12,16,128]{2,1,0:T(8,128)(2,1)S(1)} %get-tuple-element.17), channel_id=1, source_target_pairs={{0,8},{2,10},{4,12},{6,14},{8,0},{10,2},{12,4},{14,6},{16,24},{18,... | collective-permute-start | bytes 147464 | tf_op jit(solution)/shard_map/ppermute | solution.py:582
  6.1 6.2 %copy-start.1 = (bf16[256,256]{1,0:T(8,128)(2,1)S(1)}, bf16[256,256]{1,0:T(8,128)(2,1)}, u32[]{:S(2)}) copy-start(bf16[256,256]{1,0:T(8,128)(2,1)} %constant.21.clone.refs_8_) | copy-start | bytes 393220
  6.1 6.2 %copy-start.2 = (bf16[384,128]{1,0:T(8,128)(2,1)S(1)}, bf16[384,128]{1,0:T(8,128)(2,1)}, u32[]{:S(2)}) copy-start(bf16[384,128]{1,0:T(8,128)(2,1)} %constant.20.clone.refs_7_) | copy-start | bytes 294916
  6.1 6.2 %collective-permute-start.4 = (bf16[12,16,128]{2,1,0:T(8,128)(2,1)S(1)}, bf16[12,16,128]{2,1,0:T(8,128)(2,1)S(1)}, u32[]{:S(2)}, u32[]{:S(2)}) collective-permute-start(bf16[12,16,128]{2,1,0:T(8,128)(2,1)S(1)} %get-tuple-element.18), channel_id=1, source_target_pairs={{0,2},{2,0},{4,6},{6,4},{8,16},{10,18},{12,20},{14,22},{16,8},{18,... | collective-permute-start | bytes 147464 | tf_op jit(solution)/shard_map/ppermute | solution.py:583
  18.6 1.3 %collective-permute-start.5 = (bf16[12,16,128]{2,1,0:T(8,128)(2,1)S(1)}, bf16[12,16,128]{2,1,0:T(8,128)(2,1)S(1)}, u32[]{:S(2)}, u32[]{:S(2)}) collective-permute-start(bf16[12,16,128]{2,1,0:T(8,128)(2,1)S(1)} %get-tuple-element.20), channel_id=1, source_target_pairs={{0,2},{2,0},{4,6},{6,4},{8,10},{10,8},{12,14},{14,12},{16,18},{18,... | collective-permute-start | bytes 147464 | tf_op jit(solution)/shard_map/ppermute | solution.py:629
  20.0 4.2 %collective-permute-start.6 = (bf16[12,16,128]{2,1,0:T(8,128)(2,1)S(1)}, bf16[12,16,128]{2,1,0:T(8,128)(2,1)S(1)}, u32[]{:S(2)}, u32[]{:S(2)}) collective-permute-start(bf16[12,16,128]{2,1,0:T(8,128)(2,1)S(1)} %get-tuple-element.21), channel_id=1, source_target_pairs={{0,1},{1,0},{2,3},{3,2},{4,5},{5,4},{6,7},{7,6},{8,9},{9,8},{10,11... | collective-permute-start | bytes 147464 | tf_op jit(solution)/shard_map/ppermute | solution.py:635

commit v7 on v6

--- a/solution.py
+++ b/solution.py
@@ -324,6 +324,7 @@
     inverse_ref,
     inner_ref,
     keep_ref,
+    first_ref,
     send_ref,
     x_ref,
     p_ref,
@@ -486,7 +487,12 @@
                 | ((number >= 32) & has_r2)
             )
             put_coefs(x_ref, jnp.where(ok, coefs, 0.0))
-    for ref, half in ((keep_ref, second), (send_ref, 1 - second)):
+    swap_first = lax.axis_index("freq") == second
+    for ref, half in (
+        (keep_ref, second),
+        (first_ref, jnp.where(swap_first, 1 - second, second)),
+        (send_ref, 1 - second),
+    ):
         span = pl.ds(8 * half, 8)
         tops = [
             jnp.where(row3, image_ref[0, parity, span], image_ref[1, parity, span])
@@ -506,8 +512,10 @@
     return tiles[8 + q // 2, row : row + 4]
 
 
-def final_kernel(a_ref, b_ref, out_ref):
-    total = a_ref[...].astype(F32) + b_ref[...].astype(F32)
+def final_kernel(own_ref, a_ref, b_ref, out_ref):
+    straight = lax.rem(lax.axis_index("lat"), 2) == lax.axis_index("freq")
+    first = jnp.where(straight, own_ref[...], b_ref[...]).astype(F32)
+    total = first + a_ref[...].astype(F32)
     for block in range(out_ref.shape[-1] // WINDOW):
         cut = slice(WINDOW * block, WINDOW * (block + 1))
         for n in range(STEPS):
@@ -606,11 +614,11 @@
         cost_estimate=pl.CostEstimate(flops=2 * 10**9, bytes_accessed=10**7, transcendentals=0),
         name="inner",
     )(near, a1, b1, weights)
-    own, other = pl.pallas_call(
+    own, leave, other = pl.pallas_call(
         lambda *refs: main_kernel(lat // 2, *refs),
-        out_shape=(tiles(12),) * 2,
+        out_shape=(tiles(12),) * 3,
         in_specs=[vmem] * 10,
-        out_specs=(vmem,) * 2,
+        out_specs=(vmem,) * 3,
         scratch_shapes=[
             pltpu.VMEM((3, 2, 34, 16, LANES), BF16),
             pltpu.VMEM((53, 16, LANES), BF16),
@@ -626,21 +634,25 @@
         compiler_params=pltpu.CompilerParams(vmem_limit_bytes=32 << 20),
         name="steps",
     )(near, phases, a1, b1, a2, b2, weights, forward, inverse, inner)
-    swapped = lax.ppermute(other, "lat", partner)
-    core = lax.rem(lax.axis_index("lat"), 2)
     if freqs == 2:
-        mine = core == lax.axis_index("freq")
-        stay = jnp.where(mine, own, swapped)
-        leave = jnp.where(mine, swapped, own)
-        come = lax.ppermute(leave, "freq", [(0, 1), (1, 0)])
+        ring, cross = [], []
+        for place in range(lat):
+            for freq in range(2):
+                here, across = 2 * place + freq, 2 * (place ^ 1)
+                ring.append((here, across + freq if freq == place % 2 else 2 * place + 1 - freq))
+                cross.append((here, across + 1 - freq))
+        come = lax.ppermute(leave, ("lat", "freq"), ring)
+        over = lax.ppermute(other, ("lat", "freq"), cross)
         return pl.pallas_call(
             final_kernel,
             out_shape=jax.ShapeDtypeStruct((STEPS, sources // 2, points), F32),
-            in_specs=[vmem] * 2,
+            in_specs=[vmem] * 3,
             out_specs=vmem,
             compiler_params=pltpu.CompilerParams(vmem_limit_bytes=4 << 20),
             name="total",
-        )(stay, come)
+        )(own, come, over)
+    swapped = lax.ppermute(other, "lat", partner)
+    core = lax.rem(lax.axis_index("lat"), 2)
     parts = [jnp.where(core == 0, own, swapped), jnp.where(core == 0, swapped, own)]
     rows = [
         [jnp.stack([image_rows(p, n, b) for b in range(2 * pairs)], axis=1) for p in parts]

time: 24.9 us -> 24.8 us (level)
  the two profiles are of different devices: /device:TPU:28 before, /device:TPU:11 now
where the time goes in v7:
time: 24.8 us; the launch traced here: 24.6 us
  Pallas kernels  11.1 us (45%)
  starting transfers between devices  6.95 us (28%)
  waiting for transfers between devices  5.87 us (24%)
  between operations  0.73 us (3%)
    pallas_call x1, Pallas kernels, on_device(): pl.pallas_call(lambda *refs: main_kernel(lat // 2, *refs), out_shape=(til...  6.33 us
    ppermute x1, waiting for transfers between devices, on_device(): a1 = lax.ppermute(near, 'lat', matching(lat, 2, 0))  2.82 us
    ppermute x1, starting transfers between devices, on_device(): b2 = lax.ppermute(far_b, 'lat', matching(lat, 4, 1))  2.5 us
    ppermute x1, waiting for transfers between devices, on_device(): over = lax.ppermute(other, ('lat', 'freq'), cross)  2.34 us
    pallas_call x1, Pallas kernels, on_device(): pl.pallas_call(lambda *refs: inner_kernel(lat // 2, *refs), out_shape=til...  1.85 us
    pallas_call x1, Pallas kernels, on_device(): pl.pallas_call(prep_kernel, out_shape=(tiles(pairs + 2), tiles(pairs + 2...  1.43 us
    ppermute x1, starting transfers between devices, on_device(): b1 = lax.ppermute(near, 'lat', matching(lat, 2, 1))  1.33 us
    ppermute x1, starting transfers between devices, on_device(): come = lax.ppermute(leave, ('lat', 'freq'), ring)  1.26 us
  transfers between devices with their start and end apart: 7, of which 5 were waited for; matrix products, arithmetic and copies ran while one was open for 0% of the time, Pallas kernels for 10%

profile of v7, /device:TPU:11, one launch (start us, length us, event | category | flops | bytes accessed | tf_op | source)
XLA Modules:
  0.0 24.6 jit_solution(1125674714001265909)
XLA Ops:
  0.0 0.0 copy-start
  0.0 1.4 %prep.1 = (bf16[10,16,128]{2,1,0:T(8,128)(2,1)S(1)}, bf16[18,16,128]{2,1,0:T(8,128)(2,1)S(1)}) custom-call(f32[4,1,8,2048]{3,2,1,0:T(8,128)} %wave_hbm.1, f32[3,2048]{1,0:T(4,128)} %slow_hbm.1, s32[3,16]{1,0:T(4,128)} %index_hbm.1, bf16[512,128]{1,0:T(8,128)(2,1)} %constant.6.clone.first_hbm), custom_call_target="tpu_custom_call" | custom-call | flops 1000000000 | bytes 10000000 | tf_op jit(solution)/shard_map/prep/pallas_call | solution.py:548
  1.4 0.7 %collective-permute-start = (bf16[18,16,128]{2,1,0:T(8,128)(2,1)S(1)}, bf16[18,16,128]{2,1,0:T(8,128)(2,1)S(1)}, u32[]{:S(2)}, u32[]{:S(2)}) collective-permute-start(bf16[18,16,128]{2,1,0:T(8,128)(2,1)S(1)} %get-tuple-element.15.sent_ref), channel_id=1, source_target_pairs={{0,2},{2,0},{4,6},{6,4},{8,10},{10,8},{12,14},{14,12},{16,18},{18,... | collective-permute-start | bytes 221192 | tf_op jit(solution)/shard_map/ppermute | solution.py:572
  2.8 0.3 %collective-permute-done.got_ref = bf16[18,16,128]{2,1,0:T(8,128)(2,1)S(1)} collective-permute-done((bf16[18,16,128]{2,1,0:T(8,128)(2,1)S(1)}, bf16[18,16,128]{2,1,0:T(8,128)(2,1)S(1)}, u32[]{:S(2)}, u32[]{:S(2)}) %collective-permute-start) | collective-permute-done | bytes 73760 | tf_op jit(solution)/shard_map/ppermute | solution.py:572
  3.1 0.1 unit.1
  3.2 1.3 %collective-permute-start.2 = (bf16[24,16,128]{2,1,0:T(8,128)(2,1)S(1)}, bf16[24,16,128]{2,1,0:T(8,128)(2,1)S(1)}, u32[]{:S(2)}, u32[]{:S(2)}) collective-permute-start(bf16[24,16,128]{2,1,0:T(8,128)(2,1)S(1)} %get-tuple-element.16.refs_0_), channel_id=1, source_target_pairs={{0,2},{2,0},{4,8},{6,10},{8,4},{10,6},{12,16},{14,18},{16,12},{18,... | collective-permute-start | bytes 294920 | tf_op jit(solution)/shard_map/ppermute | solution.py:589
  4.5 0.1 collective-permute-start.1
  4.6 0.0 copy-done
  4.6 0.7 %weights.1.refs_3_.refs_6_ = bf16[3,2,2112,128]{3,2,1,0:T(8,128)(2,1)S(1)} custom-call(bf16[4,2112,128]{2,1,0:T(8,128)(2,1)S(1)} %bitcast.3), custom_call_target="tpu_custom_call" | custom-call | flops 100000000 | bytes 10000000 | tf_op jit(solution)/shard_map/weights/pallas_call | solution.py:594
  5.3 0.2 collective-permute-start.3
  5.5 0.0 copy-start.1
  5.5 0.0 copy-start.2
  5.5 2.5 %collective-permute-start.4 = (bf16[12,16,128]{2,1,0:T(8,128)(2,1)S(1)}, bf16[12,16,128]{2,1,0:T(8,128)(2,1)S(1)}, u32[]{:S(2)}, u32[]{:S(2)}) collective-permute-start(bf16[12,16,128]{2,1,0:T(8,128)(2,1)S(1)} %get-tuple-element.19), channel_id=1, source_target_pairs={{0,2},{2,0},{4,6},{6,4},{8,16},{10,18},{12,20},{14,22},{16,8},{18,... | collective-permute-start | bytes 147464 | tf_op jit(solution)/shard_map/ppermute | solution.py:591
  8.0 0.1 collective-permute-done.2.refs_2_.refs_3_
  8.1 2.8 %collective-permute-done.1.refs_1_.refs_2_ = bf16[24,16,128]{2,1,0:T(8,128)(2,1)S(1)} collective-permute-done((bf16[24,16,128]{2,1,0:T(8,128)(2,1)S(1)}, bf16[24,16,128]{2,1,0:T(8,128)(2,1)S(1)}, u32[]{:S(2)}, u32[]{:S(2)}) %collective-permute-start.1) | collective-permute-done | bytes 98336 | tf_op jit(solution)/shard_map/ppermute | solution.py:588
  11.0 1.9 %inner.1.refs_9_ = bf16[28,16,128]{2,1,0:T(8,128)(2,1)S(1)} custom-call(bf16[24,16,128]{2,1,0:T(8,128)(2,1)S(1)} %get-tuple-element.16.refs_0_, bf16[24,16,128]{2,1,0:T(8,128)(2,1)S(1)} %collective-permute-done.1.refs_1_.refs_2_, bf16[24,16,128]{2,1,0:T(8,128)(2,1)S(1)} %collective-permute-done.2.refs_2_.refs_3_, ...), custom_call_target="tpu_custom_call" | custom-call | flops 2000000000 | bytes 10000000 | tf_op jit(solution)/shard_map/inner/pallas_call | solution.py:603
  12.8 0.0 collective-permute-done.3.refs_4_
  12.8 0.0 collective-permute-done.4.refs_5_
  12.8 0.0 copy-done.1
  12.9 0.0 copy-done.2
  12.9 6.3 %steps.1 = (bf16[12,16,128]{2,1,0:T(8,128)(2,1)S(1)}, bf16[12,16,128]{2,1,0:T(8,128)(2,1)S(1)}, bf16[12,16,128]{2,1,0:T(8,128)(2,1)S(1)}) custom-call(bf16[24,16,128]{2,1,0:T(8,128)(2,1)S(1)} %get-tuple-element.16.refs_0_, f32[3,32,128]{2,1,0:T(8,128)S(1)} %get-tuple-element.17.refs_1_, bf16[24,16,128]{2,1,0:T(8,128)(2,1)S(1)} %collective-permute-done.1.refs_1_.refs_2_, ...), custom_call_target="tpu_custom_call" | custom-call | tf_op jit(solution)/shard_map/steps/pallas_call | solution.py:617
  19.2 1.3 %collective-permute-start.5 = (bf16[12,16,128]{2,1,0:T(8,128)(2,1)S(1)}, bf16[12,16,128]{2,1,0:T(8,128)(2,1)S(1)}, u32[]{:S(2)}, u32[]{:S(2)}) collective-permute-start(bf16[12,16,128]{2,1,0:T(8,128)(2,1)S(1)} %get-tuple-element.21), channel_id=1, source_target_pairs={{0,2},{1,0},{2,3},{3,1},{4,6},{5,4},{6,7},{7,5},{8,10},{9,8},{10,1... | collective-permute-start | bytes 147464 | tf_op jit(solution)/shard_map/ppermute | solution.py:644
  20.5 0.9 %collective-permute-start.6 = (bf16[12,16,128]{2,1,0:T(8,128)(2,1)S(1)}, bf16[12,16,128]{2,1,0:T(8,128)(2,1)S(1)}, u32[]{:S(2)}, u32[]{:S(2)}) collective-permute-start(bf16[12,16,128]{2,1,0:T(8,128)(2,1)S(1)} %get-tuple-element.22), channel_id=1, source_target_pairs={{0,3},{1,2},{2,1},{3,0},{4,7},{5,6},{6,5},{7,4},{8,11},{9,10},{10,... | collective-permute-start | bytes 147464 | tf_op jit(solution)/shard_map/ppermute | solution.py:645
  21.3 0.3 %collective-permute-done.5.a_ref = bf16[12,16,128]{2,1,0:T(8,128)(2,1)S(1)} collective-permute-done((bf16[12,16,128]{2,1,0:T(8,128)(2,1)S(1)}, bf16[12,16,128]{2,1,0:T(8,128)(2,1)S(1)}, u32[]{:S(2)}, u32[]{:S(2)}) %collective-permute-start.5) | collective-permute-done | bytes 49184 | tf_op jit(solution)/shard_map/ppermute | solution.py:644
  21.6 2.3 %collective-permute-done.6.b_ref = bf16[12,16,128]{2,1,0:T(8,128)(2,1)S(1)} collective-permute-done((bf16[12,16,128]{2,1,0:T(8,128)(2,1)S(1)}, bf16[12,16,128]{2,1,0:T(8,128)(2,1)S(1)}, u32[]{:S(2)}, u32[]{:S(2)}) %collective-permute-start.6) | collective-permute-done | bytes 49184 | tf_op jit(solution)/shard_map/ppermute | solution.py:645
  24.0 0.7 %total.1 = f32[3,4,2048]{2,1,0:T(4,128)} custom-call(bf16[12,16,128]{2,1,0:T(8,128)(2,1)S(1)} %get-tuple-element.20.own_ref, bf16[12,16,128]{2,1,0:T(8,128)(2,1)S(1)} %collective-permute-done.5.a_ref, bf16[12,16,128]{2,1,0:T(8,128)(2,1)S(1)} %collective-permute-done.6.b_ref), custom_call_target="tpu_custom_call" | custom-call | tf_op jit(solution)/shard_map/total/pallas_call | solution.py:646
Async XLA Ops:
  0.0 4.6 %copy-start = (bf16[1,4,2112,128]{3,2,1,0:T(8,128)(2,1)S(1)}, bf16[1,4,2112,128]{3,2,1,0:T(8,128)(2,1)}, u32[]{:S(2)}) copy-start(bf16[1,4,2112,128]{3,2,1,0:T(8,128)(2,1)} %param.9) | copy-start | bytes 6488068
  1.4 1.6 %collective-permute-start = (bf16[18,16,128]{2,1,0:T(8,128)(2,1)S(1)}, bf16[18,16,128]{2,1,0:T(8,128)(2,1)S(1)}, u32[]{:S(2)}, u32[]{:S(2)}) collective-permute-start(bf16[18,16,128]{2,1,0:T(8,128)(2,1)S(1)} %get-tuple-element.15.sent_ref), channel_id=1, source_target_pairs={{0,2},{2,0},{4,6},{6,4},{8,10},{10,8},{12,14},{14,12},{16,18},{18,... | collective-permute-start | bytes 221192 | tf_op jit(solution)/shard_map/ppermute | solution.py:572
  3.2 5.0 %collective-permute-start.2 = (bf16[24,16,128]{2,1,0:T(8,128)(2,1)S(1)}, bf16[24,16,128]{2,1,0:T(8,128)(2,1)S(1)}, u32[]{:S(2)}, u32[]{:S(2)}) collective-permute-start(bf16[24,16,128]{2,1,0:T(8,128)(2,1)S(1)} %get-tuple-element.16.refs_0_), channel_id=1, source_target_pairs={{0,2},{2,0},{4,8},{6,10},{8,4},{10,6},{12,16},{14,18},{16,12},{18,... | collective-permute-start | bytes 294920 | tf_op jit(solution)/shard_map/ppermute | solution.py:589
  4.5 6.5 %collective-permute-start.1 = (bf16[24,16,128]{2,1,0:T(8,128)(2,1)S(1)}, bf16[24,16,128]{2,1,0:T(8,128)(2,1)S(1)}, u32[]{:S(2)}, u32[]{:S(2)}) collective-permute-start(bf16[24,16,128]{2,1,0:T(8,128)(2,1)S(1)} %get-tuple-element.16.refs_0_), channel_id=1, source_target_pairs={{0,4},{2,6},{4,0},{6,2},{8,12},{10,14},{12,8},{14,10},{16,20},{18,... | collective-permute-start | bytes 294920 | tf_op jit(solution)/shard_map/ppermute | solution.py:588
  5.3 7.5 %collective-permute-start.3 = (bf16[12,16,128]{2,1,0:T(8,128)(2,1)S(1)}, bf16[12,16,128]{2,1,0:T(8,128)(2,1)S(1)}, u32[]{:S(2)}, u32[]{:S(2)}) collective-permute-start(bf16[12,16,128]{2,1,0:T(8,128)(2,1)S(1)} %get-tuple-element.18), channel_id=1, source_target_pairs={{0,8},{2,10},{4,12},{6,14},{8,0},{10,2},{12,4},{14,6},{16,24},{18,... | collective-permute-start | bytes 147464 | tf_op jit(solution)/shard_map/ppermute | solution.py:590
  5.5 7.4 %copy-start.1 = (bf16[256,256]{1,0:T(8,128)(2,1)S(1)}, bf16[256,256]{1,0:T(8,128)(2,1)}, u32[]{:S(2)}) copy-start(bf16[256,256]{1,0:T(8,128)(2,1)} %constant.8.clone.refs_8_) | copy-start | bytes 393220
  5.5 7.4 %copy-start.2 = (bf16[384,128]{1,0:T(8,128)(2,1)S(1)}, bf16[384,128]{1,0:T(8,128)(2,1)}, u32[]{:S(2)}) copy-start(bf16[384,128]{1,0:T(8,128)(2,1)} %constant.7.clone.refs_7_) | copy-start | bytes 294916
  5.5 7.3 %collective-permute-start.4 = (bf16[12,16,128]{2,1,0:T(8,128)(2,1)S(1)}, bf16[12,16,128]{2,1,0:T(8,128)(2,1)S(1)}, u32[]{:S(2)}, u32[]{:S(2)}) collective-permute-start(bf16[12,16,128]{2,1,0:T(8,128)(2,1)S(1)} %get-tuple-element.19), channel_id=1, source_target_pairs={{0,2},{2,0},{4,6},{6,4},{8,16},{10,18},{12,20},{14,22},{16,8},{18,... | collective-permute-start | bytes 147464 | tf_op jit(solution)/shard_map/ppermute | solution.py:591
  19.2 2.4 %collective-permute-start.5 = (bf16[12,16,128]{2,1,0:T(8,128)(2,1)S(1)}, bf16[12,16,128]{2,1,0:T(8,128)(2,1)S(1)}, u32[]{:S(2)}, u32[]{:S(2)}) collective-permute-start(bf16[12,16,128]{2,1,0:T(8,128)(2,1)S(1)} %get-tuple-element.21), channel_id=1, source_target_pairs={{0,2},{1,0},{2,3},{3,1},{4,6},{5,4},{6,7},{7,5},{8,10},{9,8},{10,1... | collective-permute-start | bytes 147464 | tf_op jit(solution)/shard_map/ppermute | solution.py:644
  20.5 3.5 %collective-permute-start.6 = (bf16[12,16,128]{2,1,0:T(8,128)(2,1)S(1)}, bf16[12,16,128]{2,1,0:T(8,128)(2,1)S(1)}, u32[]{:S(2)}, u32[]{:S(2)}) collective-permute-start(bf16[12,16,128]{2,1,0:T(8,128)(2,1)S(1)} %get-tuple-element.22), channel_id=1, source_target_pairs={{0,3},{1,2},{2,1},{3,0},{4,7},{5,6},{6,5},{7,4},{8,11},{9,10},{10,... | collective-permute-start | bytes 147464 | tf_op jit(solution)/shard_map/ppermute | solution.py:645
